TPU v7x, 32 devices: a 4x4x1 block of a 4x4x8 slice. The times are simulated.
32 devices in a mesh: dp: 1 (over z), tp: 4 (over y), cp: 8 (over x, core).
Axes of the slice: x: 4, y: 4, z: 1, core: 2. Of those that a mesh axis runs over, the one named last changes fastest.
The devices are a block of a 4x4x8 slice.
Arguments:
- x_in: bfloat16 [1, 8192, 2048], P('dp', 'cp')
- w_q: bfloat16 [2048, 16, 128], P(None, 'tp')
- w_k: bfloat16 [2048, 16, 128], P(None, 'tp')
- w_v: bfloat16 [2048, 16, 128], P(None, 'tp')
- w_o: bfloat16 [16, 128, 2048], P('tp')
- q_norm_w: float32 [16, 128], P('tp')
- k_norm_w: float32 [16, 128], P('tp')
- post_norm_w: float32 [2048], replicated
- grad_y: bfloat16 [1, 8192, 2048], P('dp', 'cp')
Outputs:
- output 1: bfloat16 [1, 8192, 2048], P('dp', 'cp')
- output 2: bfloat16 [1, 8192, 2048], P('dp', 'cp')
- output 3: float32 [2048, 16, 128], P('dp', 'tp')
- output 4: float32 [2048, 16, 128], P('dp', 'tp')
- output 5: float32 [2048, 16, 128], P('dp', 'tp')
- output 6: float32 [16, 128, 2048], P(('dp', 'tp'))
- output 7: float32 [16, 128], P(('dp', 'tp'))
- output 8: float32 [16, 128], P(('dp', 'tp'))
- output 9: float32 [2048], P('dp')
All inputs are finite; a program needn't handle non-finite values.
Results may differ from a plain program's by a relative error of at most 0.01742.
Values are sent between devices in bfloat16 or wider.
A program may use at most 768 MiB of HBM per device.

v0:
```python
import jax
import jax.numpy as jnp
from jax import lax
from jax.sharding import PartitionSpec as P

ROPE_THETA = 500000.0
NORM_EPS = 1e-6
MASK_VALUE = -1e30


def rope_tables(start_pos, seq_rows, head_dim):
    half_dim = head_dim // 2
    inv_freq = ROPE_THETA ** (-2.0 * jnp.arange(half_dim, dtype=jnp.float32) / head_dim)
    positions = (start_pos + jnp.arange(seq_rows)).astype(jnp.float32)
    angles = positions[:, None] * inv_freq[None, :]
    return jnp.cos(angles), jnp.sin(angles)


def apply_rope(values, cos_tab, sin_tab):
    half_dim = values.shape[-1] // 2
    low_half = values[..., :half_dim]
    high_half = values[..., half_dim:]
    cos_rows = cos_tab[:, None, :]
    sin_rows = sin_tab[:, None, :]
    return jnp.concatenate([low_half * cos_rows - high_half * sin_rows, high_half * cos_rows + low_half * sin_rows], axis=-1)


def rope_back(grad_in, cos_tab, sin_tab):
    half_dim = grad_in.shape[-1] // 2
    low_half = grad_in[..., :half_dim]
    high_half = grad_in[..., half_dim:]
    cos_rows = cos_tab[:, None, :]
    sin_rows = sin_tab[:, None, :]
    return jnp.concatenate([low_half * cos_rows + high_half * sin_rows, high_half * cos_rows - low_half * sin_rows], axis=-1)


def whole_norm(lin_out, weight, width):
    sq_sum = lax.psum(jnp.sum(lin_out * lin_out, axis=(2, 3)), "tp")
    inv_rms = lax.rsqrt(sq_sum / width + NORM_EPS)[:, :, None, None]
    normed = lin_out * inv_rms
    return normed * weight, normed, inv_rms


def whole_norm_back(grad_out, normed, inv_rms, weight, width):
    grad_weight = jnp.sum(grad_out * normed, axis=(0, 1))
    grad_normed = grad_out * weight
    dot_sum = lax.psum(jnp.sum(grad_normed * normed, axis=(2, 3)), "tp")
    grad_lin = inv_rms * (grad_normed - normed * (dot_sum / width)[:, :, None, None])
    return grad_lin, grad_weight


def attend_block(q_rot, k_blk, v_blk, stats_in, score_scale, causal):
    row_max, row_sum, out_acc = stats_in
    scores = jnp.einsum("blkgd,bmkd->bklgm", q_rot, k_blk, preferred_element_type=jnp.float32) * score_scale
    if causal:
        block_len = q_rot.shape[1]
        lower_tri = jnp.arange(block_len)[:, None] >= jnp.arange(block_len)[None, :]
        scores = jnp.where(lower_tri[:, None, :], scores, MASK_VALUE)
    new_max = jnp.maximum(row_max, jnp.max(scores, axis=-1))
    prob_blk = jnp.exp(scores - new_max[..., None])
    rescale = jnp.exp(row_max - new_max)
    new_sum = row_sum * rescale + jnp.sum(prob_blk, axis=-1)
    new_acc = out_acc * rescale[..., None] + jnp.einsum("bklgm,bmkd->bklgd", prob_blk.astype(jnp.bfloat16), v_blk, preferred_element_type=jnp.float32)
    return new_max, new_sum, new_acc


def attend_block_back(q_rot, k_blk, v_blk, grad_o, log_sum, row_delta, score_scale, causal):
    scores = jnp.einsum("blkgd,bmkd->bklgm", q_rot, k_blk, preferred_element_type=jnp.float32) * score_scale
    if causal:
        block_len = q_rot.shape[1]
        lower_tri = jnp.arange(block_len)[:, None] >= jnp.arange(block_len)[None, :]
        scores = jnp.where(lower_tri[:, None, :], scores, MASK_VALUE)
    prob_blk = jnp.exp(scores - log_sum[..., None])
    grad_v = jnp.einsum("bklgm,blkgd->bkmd", prob_blk.astype(jnp.bfloat16), grad_o, preferred_element_type=jnp.float32)
    grad_p = jnp.einsum("blkgd,bmkd->bklgm", grad_o, v_blk, preferred_element_type=jnp.float32)
    grad_s = (prob_blk * (grad_p - row_delta[..., None]) * score_scale).astype(jnp.bfloat16)
    grad_q = jnp.einsum("bklgm,bmkd->bklgd", grad_s, k_blk, preferred_element_type=jnp.float32)
    grad_k = jnp.einsum("bklgm,blkgd->bkmd", grad_s, q_rot, preferred_element_type=jnp.float32)
    return grad_q, grad_k, grad_v


def solution(mesh):
    tp_size = mesh.shape["tp"]
    cp_size = mesh.shape["cp"]
    perm_next = [(src_dev, (src_dev + 1) % cp_size) for src_dev in range(cp_size)]
    act_spec = P("dp", "cp", None)
    col_spec = P(None, "tp", None)
    part_col = P("dp", "tp", None)
    in_specs = (act_spec, col_spec, col_spec, col_spec, P("tp", None, None), P("tp", None), P("tp", None), P(None), act_spec)
    out_specs = (act_spec, act_spec, part_col, part_col, part_col, P(("dp", "tp"), None, None), P(("dp", "tp"), None), P(("dp", "tp"), None), P("dp"))

    def local_run(x_in, w_q, w_k, w_v, w_o, q_norm_w, k_norm_w, post_norm_w, grad_y):
        n_batch = x_in.shape[0]
        block_len = x_in.shape[1]
        heads_loc = w_q.shape[1]
        kv_loc = w_k.shape[1]
        head_dim = w_q.shape[2]
        group_size = heads_loc // kv_loc
        q_width = heads_loc * head_dim * tp_size
        k_width = kv_loc * head_dim * tp_size
        score_scale = head_dim ** -0.5
        cp_index = lax.axis_index("cp")
        cos_tab, sin_tab = rope_tables(cp_index * block_len, block_len, head_dim)

        q_lin = jnp.einsum("bld,dhe->blhe", x_in, w_q, preferred_element_type=jnp.float32)
        k_lin = jnp.einsum("bld,dhe->blhe", x_in, w_k, preferred_element_type=jnp.float32)
        v_lin = jnp.einsum("bld,dhe->blhe", x_in, w_v, preferred_element_type=jnp.float32)
        q_scaled, q_hat, q_inv = whole_norm(q_lin, q_norm_w, q_width)
        k_scaled, k_hat, k_inv = whole_norm(k_lin, k_norm_w, k_width)
        q_rot = apply_rope(q_scaled, cos_tab, sin_tab).astype(jnp.bfloat16).reshape(n_batch, block_len, kv_loc, group_size, head_dim)
        k_rot = apply_rope(k_scaled, cos_tab, sin_tab).astype(jnp.bfloat16)
        v_val = v_lin.astype(jnp.bfloat16)

        stat_shape = (n_batch, kv_loc, block_len, group_size)
        first_state = (jnp.full(stat_shape, MASK_VALUE, jnp.float32), jnp.zeros(stat_shape, jnp.float32), jnp.zeros(stat_shape + (head_dim,), jnp.float32))
        soft_state = attend_block(q_rot, k_rot, v_val, first_state, score_scale, True)

        def fwd_step(step_idx, loop_state):
            k_cur, v_cur, stats_in = loop_state
            k_cur, v_cur = lax.ppermute((k_cur, v_cur), "cp", perm_next)

            def use_block(stats_now):
                return attend_block(q_rot, k_cur, v_cur, stats_now, score_scale, False)

            def keep_block(stats_now):
                return stats_now

            stats_out = lax.cond(step_idx <= cp_index, use_block, keep_block, stats_in)
            return k_cur, v_cur, stats_out

        row_max, row_sum, out_acc = lax.fori_loop(1, cp_size, fwd_step, (k_rot, v_val, soft_state))[2]
        attn_out = (out_acc / row_sum[..., None]).astype(jnp.bfloat16).transpose(0, 2, 1, 3, 4).reshape(n_batch, block_len, heads_loc, head_dim)
        log_sum = row_max + jnp.log(row_sum)

        proj = lax.psum(jnp.einsum("blhe,hed->bld", attn_out, w_o, preferred_element_type=jnp.float32), "tp")
        post_inv = lax.rsqrt(jnp.mean(proj * proj, axis=-1, keepdims=True) + NORM_EPS)
        post_hat = proj * post_inv
        y_out = (x_in + post_hat * post_norm_w).astype(jnp.bfloat16)

        grad_f = grad_y.astype(jnp.float32)
        grad_post = jnp.sum(grad_f * post_hat, axis=(0, 1))
        grad_hat = grad_f * post_norm_w
        grad_proj = (post_inv * (grad_hat - post_hat * jnp.mean(grad_hat * post_hat, axis=-1, keepdims=True))).astype(jnp.bfloat16)
        grad_w_o = jnp.einsum("blhe,bld->hed", attn_out, grad_proj, preferred_element_type=jnp.float32)
        grad_attn = jnp.einsum("bld,hed->blhe", grad_proj, w_o, preferred_element_type=jnp.float32)
        row_delta = jnp.sum(grad_attn * attn_out, axis=-1).reshape(n_batch, block_len, kv_loc, group_size).transpose(0, 2, 1, 3)
        grad_o = grad_attn.astype(jnp.bfloat16).reshape(n_batch, block_len, kv_loc, group_size, head_dim)

        diag_q, diag_k, diag_v = attend_block_back(q_rot, k_rot, v_val, grad_o, log_sum, row_delta, score_scale, True)

        def bwd_step(step_idx, loop_state):
            k_cur, v_cur, dk_cur, dv_cur, dq_cur = loop_state
            k_cur, v_cur, dk_cur, dv_cur = lax.ppermute((k_cur, v_cur, dk_cur, dv_cur), "cp", perm_next)

            def use_block(acc_in):
                part_q, part_k, part_v = attend_block_back(q_rot, k_cur, v_cur, grad_o, log_sum, row_delta, score_scale, False)
                return acc_in[0] + part_q, acc_in[1] + part_k, acc_in[2] + part_v

            def keep_block(acc_in):
                return acc_in

            dq_cur, dk_cur, dv_cur = lax.cond(step_idx <= cp_index, use_block, keep_block, (dq_cur, dk_cur, dv_cur))
            return k_cur, v_cur, dk_cur, dv_cur, dq_cur

        back_state = lax.fori_loop(1, cp_size, bwd_step, (k_rot, v_val, diag_k, diag_v, diag_q))
        dk_home, dv_home = lax.ppermute((back_state[2], back_state[3]), "cp", perm_next)
        grad_q_rot = back_state[4].transpose(0, 2, 1, 3, 4).reshape(n_batch, block_len, heads_loc, head_dim)
        grad_k_rot = dk_home.transpose(0, 2, 1, 3)
        grad_v16 = dv_home.transpose(0, 2, 1, 3).astype(jnp.bfloat16)

        grad_q_lin, grad_q_norm = whole_norm_back(rope_back(grad_q_rot, cos_tab, sin_tab), q_hat, q_inv, q_norm_w, q_width)
        grad_k_lin, grad_k_norm = whole_norm_back(rope_back(grad_k_rot, cos_tab, sin_tab), k_hat, k_inv, k_norm_w, k_width)
        grad_q16 = grad_q_lin.astype(jnp.bfloat16)
        grad_k16 = grad_k_lin.astype(jnp.bfloat16)
        grad_w_q = jnp.einsum("bld,blhe->dhe", x_in, grad_q16, preferred_element_type=jnp.float32)
        grad_w_k = jnp.einsum("bld,blhe->dhe", x_in, grad_k16, preferred_element_type=jnp.float32)
        grad_w_v = jnp.einsum("bld,blhe->dhe", x_in, grad_v16, preferred_element_type=jnp.float32)
        grad_x_part = (jnp.einsum("blhe,dhe->bld", grad_q16, w_q, preferred_element_type=jnp.float32)
                       + jnp.einsum("blhe,dhe->bld", grad_k16, w_k, preferred_element_type=jnp.float32)
                       + jnp.einsum("blhe,dhe->bld", grad_v16, w_v, preferred_element_type=jnp.float32))
        grad_x = (grad_f + lax.psum(grad_x_part, "tp")).astype(jnp.bfloat16)
        weight_grads = lax.psum((grad_w_q, grad_w_k, grad_w_v, grad_w_o, grad_q_norm, grad_k_norm, grad_post), "cp")
        return (y_out, grad_x) + tuple(weight_grads)

    return jax.shard_map(local_run, mesh=mesh, in_specs=in_specs, out_specs=out_specs, check_vma=False)
```

profile of v0, /device:TPU:97, one launch (start us, length us, event | category | flops | bytes accessed | tf_op | source)
XLA Modules:
  0.0 1899.3 jit_solution(8788151131780073398)
XLA Ops:
  89.1 324.9 %while.42 = (s32[]{:T(128)}, bf16[1,1024,4,128]{3,1,2,0:T(8,128)(2,1)}, bf16[1,1024,4,128]{3,1,2,0:T(8,128)(2,1)}, f32[1,4,1024,1]{2,1,3,0:T(4,128)S(1)}, f32[1,...) while((s32[]{:T(128)}, ...), condition=%wide.region_11.12_spmd, body=%wide.region_6.11_spmd.sunk | while | flops 2182098944 | bytes 70517024 | solution.py:131
  116.1 27.5 %conditional.4 = ((f32[1,4,1024,1]{2,1,3,0:T(4,128)S(1)}, f32[1,4,1024,1]{2,1,3,0:T(4,128)S(1)}, f32[1,4,1024,1,128]{4,2,1,3,0:T(8,128)})) conditional(s32[]{:T(128)} %convert_element_type.204, (f32[1,4,1024,1]{2,1,3,0:T(4,128)S(1)}, f32[1,4,1024,1]{2,1,3,0:T(4,128)S(1)}, f32[1,4,1024,1,128]{4,2,1,3,0:T(8,128)}) %tuple.97, ...), branch_computations={%region_7.7_spmd, %region_8.10_spmd} | conditional | flops 2182098944 | bytes 57933856 | solution.py:128
  178.2 30.0 %collective-permute-start.1 = (bf16[1,1024,4,128]{3,1,2,0:T(8,128)(2,1)}, bf16[1,1024,4,128]{3,1,2,0:T(8,128)(2,1)}, u32[]{:S(2)}, u32[]{:S(2)}) collective-permute-start(bf16[1,1024,4,128]{3,1,2,0:T(8,128)(2,1)} %get-tuple-element.684), channel_id=1, source_target_pairs={{0,1},{1,2},{2,3},{3,4},{4,5},{5,6},{6,7},{7,0},{8,9},{9,10},{10,1... | collective-permute-start | bytes 3145736 | tf_op jit(solution)/shard_map/while/body/eval_jaxpr/ppermute | solution.py:120
  238.2 26.8 %collective-permute-start = (bf16[1,1024,4,128]{3,1,2,0:T(8,128)(2,1)}, bf16[1,1024,4,128]{3,1,2,0:T(8,128)(2,1)}, u32[]{:S(2)}, u32[]{:S(2)}) collective-permute-start(bf16[1,1024,4,128]{3,1,2,0:T(8,128)(2,1)} %get-tuple-element.683), channel_id=1, source_target_pairs={{0,1},{1,2},{2,3},{3,4},{4,5},{5,6},{6,7},{7,0},{8,9},{9,10},{10,1... | collective-permute-start | bytes 3145736 | tf_op jit(solution)/shard_map/while/body/eval_jaxpr/ppermute | solution.py:120
  371.2 26.5 %collective-permute-start = (bf16[1,1024,4,128]{3,1,2,0:T(8,128)(2,1)}, bf16[1,1024,4,128]{3,1,2,0:T(8,128)(2,1)}, u32[]{:S(2)}, u32[]{:S(2)}) collective-permute-start(bf16[1,1024,4,128]{3,1,2,0:T(8,128)(2,1)} %get-tuple-element.683), channel_id=1, source_target_pairs={{0,1},{1,2},{2,3},{3,4},{4,5},{5,6},{6,7},{7,0},{8,9},{9,10},{10,1... | collective-permute-start | bytes 3145736 | tf_op jit(solution)/shard_map/while/body/eval_jaxpr/ppermute | solution.py:120
  424.2 216.3 %all-reduce.8.cloned.1.call-done = f32[1,1024,2048]{2,1,0:T(8,128)} async-done(((f32[1,1024,2048]{2,1,0:T(8,128)}), f32[1,1024,2048]{2,1,0:T(8,128)}) %all-reduce.8.cloned.1.call-update) | async-done | bytes 8388624 | tf_op jit(solution)/shard_map/psum | solution.py:135
  688.9 681.0 %while.43 = (s32[]{:T(128)}, bf16[1,1024,4,128]{3,1,2,0:T(8,128)(2,1)}, bf16[1,1024,4,128]{3,1,2,0:T(8,128)(2,1)}, f32[1,4,1024,128]{3,2,1,0:T(8,128)}, f32[1,4,...) while((s32[]{:T(128)}, ...), condition=%wide.region_19.0_spmd, body=%wide.region_16.19_spmd.sunk | while | flops 5408030720 | bytes 149996000 | solution.py:165
  692.8 55.0 %collective-permute-done.3 = bf16[1,1024,4,128]{3,1,2,0:T(8,128)(2,1)} collective-permute-done((bf16[1,1024,4,128]{3,1,2,0:T(8,128)(2,1)}, bf16[1,1024,4,128]{3,1,2,0:T(8,128)(2,1)}, u32[]{:S(2)}, u32[]{:S(2)}) %collective-permute-start.3) | collective-permute-done | bytes 1048608 | tf_op jit(solution)/shard_map/while/body/eval_jaxpr/ppermute | solution.py:153
  760.0 37.1 %conditional.5 = ((f32[1,4,1024,1,128]{4,2,1,3,0:T(8,128)}, f32[1,4,1024,128]{3,2,1,0:T(8,128)}, f32[1,4,1024,128]{3,2,1,0:T(8,128)})) conditional(s32[]{:T(128)} %convert_element_type.205, (f32[1,4,1024,1,128]{4,2,1,3,0:T(8,128)}, f32[1,4,1024,128]{3,2,1,0:T(8,128)}, f32[1,4,1024,128]{3,2,1,0:T(8,128)}) %tuple.100, ...), branch_computations={%region_17.17_spmd, %region_18.18_spmd} | conditional | flops 5408030720 | bytes 112246872 | solution.py:162
  807.3 55.1 %collective-permute-done.3 = bf16[1,1024,4,128]{3,1,2,0:T(8,128)(2,1)} collective-permute-done((bf16[1,1024,4,128]{3,1,2,0:T(8,128)(2,1)}, bf16[1,1024,4,128]{3,1,2,0:T(8,128)(2,1)}, u32[]{:S(2)}, u32[]{:S(2)}) %collective-permute-start.3) | collective-permute-done | bytes 1048608 | tf_op jit(solution)/shard_map/while/body/eval_jaxpr/ppermute | solution.py:153
  880.8 39.6 %collective-permute-start.5 = (f32[1,4,1024,128]{3,2,1,0:T(8,128)}, f32[1,4,1024,128]{3,2,1,0:T(8,128)}, u32[]{:S(2)}, u32[]{:S(2)}) collective-permute-start(f32[1,4,1024,128]{3,2,1,0:T(8,128)} %get-tuple-element.716), channel_id=1, source_target_pairs={{0,1},{1,2},{2,3},{3,4},{4,5},{5,6},{6,7},{7,0},{8,9},{9,10},{10,1... | collective-permute-start | bytes 6291464 | tf_op jit(solution)/shard_map/while/body/eval_jaxpr/ppermute | solution.py:153
  921.9 55.1 %collective-permute-done.3 = bf16[1,1024,4,128]{3,1,2,0:T(8,128)(2,1)} collective-permute-done((bf16[1,1024,4,128]{3,1,2,0:T(8,128)(2,1)}, bf16[1,1024,4,128]{3,1,2,0:T(8,128)(2,1)}, u32[]{:S(2)}, u32[]{:S(2)}) %collective-permute-start.3) | collective-permute-done | bytes 1048608 | tf_op jit(solution)/shard_map/while/body/eval_jaxpr/ppermute | solution.py:153
  997.9 36.2 %collective-permute-start.4 = (f32[1,4,1024,128]{3,2,1,0:T(8,128)}, f32[1,4,1024,128]{3,2,1,0:T(8,128)}, u32[]{:S(2)}, u32[]{:S(2)}) collective-permute-start(f32[1,4,1024,128]{3,2,1,0:T(8,128)} %get-tuple-element.715), channel_id=1, source_target_pairs={{0,1},{1,2},{2,3},{3,4},{4,5},{5,6},{6,7},{7,0},{8,9},{9,10},{10,1... | collective-permute-start | bytes 6291464 | tf_op jit(solution)/shard_map/while/body/eval_jaxpr/ppermute | solution.py:153
  1036.5 31.7 %collective-permute-done.3 = bf16[1,1024,4,128]{3,1,2,0:T(8,128)(2,1)} collective-permute-done((bf16[1,1024,4,128]{3,1,2,0:T(8,128)(2,1)}, bf16[1,1024,4,128]{3,1,2,0:T(8,128)(2,1)}, u32[]{:S(2)}, u32[]{:S(2)}) %collective-permute-start.3) | collective-permute-done | bytes 1048608 | tf_op jit(solution)/shard_map/while/body/eval_jaxpr/ppermute | solution.py:153
  1089.1 22.5 %collective-permute-start.4 = (f32[1,4,1024,128]{3,2,1,0:T(8,128)}, f32[1,4,1024,128]{3,2,1,0:T(8,128)}, u32[]{:S(2)}, u32[]{:S(2)}) collective-permute-start(f32[1,4,1024,128]{3,2,1,0:T(8,128)} %get-tuple-element.715), channel_id=1, source_target_pairs={{0,1},{1,2},{2,3},{3,4},{4,5},{5,6},{6,7},{7,0},{8,9},{9,10},{10,1... | collective-permute-start | bytes 6291464 | tf_op jit(solution)/shard_map/while/body/eval_jaxpr/ppermute | solution.py:153
  1111.6 39.6 %collective-permute-start.3 = (bf16[1,1024,4,128]{3,1,2,0:T(8,128)(2,1)}, bf16[1,1024,4,128]{3,1,2,0:T(8,128)(2,1)}, u32[]{:S(2)}, u32[]{:S(2)}) collective-permute-start(bf16[1,1024,4,128]{3,1,2,0:T(8,128)(2,1)} %get-tuple-element.714), channel_id=1, source_target_pairs={{0,1},{1,2},{2,3},{3,4},{4,5},{5,6},{6,7},{7,0},{8,9},{9,10},{10,1... | collective-permute-start | bytes 3145736 | tf_op jit(solution)/shard_map/while/body/eval_jaxpr/ppermute | solution.py:153
  1183.7 42.4 %collective-permute-start.4 = (f32[1,4,1024,128]{3,2,1,0:T(8,128)}, f32[1,4,1024,128]{3,2,1,0:T(8,128)}, u32[]{:S(2)}, u32[]{:S(2)}) collective-permute-start(f32[1,4,1024,128]{3,2,1,0:T(8,128)} %get-tuple-element.715), channel_id=1, source_target_pairs={{0,1},{1,2},{2,3},{3,4},{4,5},{5,6},{6,7},{7,0},{8,9},{9,10},{10,1... | collective-permute-start | bytes 6291464 | tf_op jit(solution)/shard_map/while/body/eval_jaxpr/ppermute | solution.py:153
  1228.7 35.9 %collective-permute-start.2 = (bf16[1,1024,4,128]{3,1,2,0:T(8,128)(2,1)}, bf16[1,1024,4,128]{3,1,2,0:T(8,128)(2,1)S(1)}, u32[]{:S(2)}, u32[]{:S(2)}) collective-permute-start(bf16[1,1024,4,128]{3,1,2,0:T(8,128)(2,1)} %get-tuple-element.713), channel_id=1, source_target_pairs={{0,1},{1,2},{2,3},{3,4},{4,5},{5,6},{6,7},{7,0},{8,9},{9,10},{10,1... | collective-permute-start | bytes 3145736 | tf_op jit(solution)/shard_map/while/body/eval_jaxpr/ppermute | solution.py:153
  1285.9 31.2 %collective-permute-start.4 = (f32[1,4,1024,128]{3,2,1,0:T(8,128)}, f32[1,4,1024,128]{3,2,1,0:T(8,128)}, u32[]{:S(2)}, u32[]{:S(2)}) collective-permute-start(f32[1,4,1024,128]{3,2,1,0:T(8,128)} %get-tuple-element.715), channel_id=1, source_target_pairs={{0,1},{1,2},{2,3},{3,4},{4,5},{5,6},{6,7},{7,0},{8,9},{9,10},{10,1... | collective-permute-start | bytes 6291464 | tf_op jit(solution)/shard_map/while/body/eval_jaxpr/ppermute | solution.py:153
  1319.6 22.5 %collective-permute-start.2 = (bf16[1,1024,4,128]{3,1,2,0:T(8,128)(2,1)}, bf16[1,1024,4,128]{3,1,2,0:T(8,128)(2,1)S(1)}, u32[]{:S(2)}, u32[]{:S(2)}) collective-permute-start(bf16[1,1024,4,128]{3,1,2,0:T(8,128)(2,1)} %get-tuple-element.713), channel_id=1, source_target_pairs={{0,1},{1,2},{2,3},{3,4},{4,5},{5,6},{6,7},{7,0},{8,9},{9,10},{10,1... | collective-permute-start | bytes 3145736 | tf_op jit(solution)/shard_map/while/body/eval_jaxpr/ppermute | solution.py:153
  1426.8 22.9 %collective-permute-done.7 = bf16[1,4,1024,128]{3,2,1,0:T(8,128)(2,1)S(1)} collective-permute-done((bf16[1,4,1024,128]{3,2,1,0:T(8,128)(2,1)}, bf16[1,4,1024,128]{3,2,1,0:T(8,128)(2,1)S(1)}, u32[]{:S(2)}, u32[]{:S(2)}) %collective-permute-start.7) | collective-permute-done | bytes 1048608 | tf_op jit(solution)/shard_map/ppermute | solution.py:166
  1494.1 88.5 %all-reduce = (f32[4,128]{1,0:T(4,128)}, f32[4,128]{1,0:T(4,128)}, f32[2048]{0:T(1024)}) all-reduce(f32[4,128]{1,0:T(4,128)S(1)} %get-tuple-element.449, f32[4,128]{1,0:T(4,128)S(1)} %get-tuple-element.447, f32[2048]{0:T(1024)S(1)} %copy-done.52), channel_id=1, replica_groups=mesh['dp'=1,'tp'=4,'cp'=8] {'cp'}, use_global_device_ids=true, to_apply=%region_30.31 | all-reduce | flops 3072 | bytes 24576 | tf_op jit(solution)/shard_map/psum | solution.py:182
  1582.6 140.5 %all-reduce.12.cloned.1.call-done = (f32[2048,4,128]{0,2,1:T(8,128)}, f32[2048,4,128]{0,2,1:T(8,128)}, f32[2048,4,128]{0,2,1:T(8,128)}, f32[4,128,2048]{2,1,0:T(8,128)}) async-done(((f32[2048,4,128]{0,2,1:T(8,128)}, f32[2048,4,128]{0,2,1:T(8,128)}, f32[2048,4,128]{0,2,1:T(8,128)}, f32[4,128,2048]{2,1,0:T(8,128)}), (f32[2048,4,128]{0,2,1:T(8,128)}, f32[2048,4,128]{0,2,1:T(8,128)}, f32[2048,4,128]{0,2,1:T(8,128)}, ...) | async-done | bytes 16777232 | tf_op jit(solution)/shard_map/psum | solution.py:182
  1738.7 142.1 %all-reduce.10.cloned.1.call-done = f32[1,1024,2048]{2,1,0:T(8,128)} async-done(((f32[1,1024,2048]{2,1,0:T(8,128)}), f32[1,1024,2048]{2,1,0:T(8,128)}) %all-reduce.10.cloned.1.call-update) | async-done | bytes 8388624 | tf_op jit(solution)/shard_map/psum | solution.py:181
  (320 shorter events, 723.7 us)
Async XLA Ops:
  7.2 633.3 %all-reduce.8.cloned.1.call-start = ((), (), s32[]{:S(2)}) async-start(), calls=%async_computation | async-start | bytes 16777216 | tf_op jit(solution)/shard_map/psum | solution.py:135
  424.1 1298.9 %all-reduce.12.cloned.1.call-start = ((), (), s32[]{:S(2)}) async-start(), calls=%async_computation.2 | async-start | bytes 33554432 | tf_op jit(solution)/shard_map/psum | solution.py:182
  689.1 70.9 %collective-permute-start.5 = (f32[1,4,1024,128]{3,2,1,0:T(8,128)}, f32[1,4,1024,128]{3,2,1,0:T(8,128)}, u32[]{:S(2)}, u32[]{:S(2)}) collective-permute-start(f32[1,4,1024,128]{3,2,1,0:T(8,128)} %get-tuple-element.716), channel_id=1, source_target_pairs={{0,1},{1,2},{2,3},{3,4},{4,5},{5,6},{6,7},{7,0},{8,9},{9,10},{10,1... | collective-permute-start | bytes 6291464 | tf_op jit(solution)/shard_map/while/body/eval_jaxpr/ppermute | solution.py:153
  691.1 68.9 %collective-permute-start.4 = (f32[1,4,1024,128]{3,2,1,0:T(8,128)}, f32[1,4,1024,128]{3,2,1,0:T(8,128)}, u32[]{:S(2)}, u32[]{:S(2)}) collective-permute-start(f32[1,4,1024,128]{3,2,1,0:T(8,128)} %get-tuple-element.715), channel_id=1, source_target_pairs={{0,1},{1,2},{2,3},{3,4},{4,5},{5,6},{6,7},{7,0},{8,9},{9,10},{10,1... | collective-permute-start | bytes 6291464 | tf_op jit(solution)/shard_map/while/body/eval_jaxpr/ppermute | solution.py:153
  691.2 56.6 %collective-permute-start.3 = (bf16[1,1024,4,128]{3,1,2,0:T(8,128)(2,1)}, bf16[1,1024,4,128]{3,1,2,0:T(8,128)(2,1)}, u32[]{:S(2)}, u32[]{:S(2)}) collective-permute-start(bf16[1,1024,4,128]{3,1,2,0:T(8,128)(2,1)} %get-tuple-element.714), channel_id=1, source_target_pairs={{0,1},{1,2},{2,3},{3,4},{4,5},{5,6},{6,7},{7,0},{8,9},{9,10},{10,1... | collective-permute-start | bytes 3145736 | tf_op jit(solution)/shard_map/while/body/eval_jaxpr/ppermute | solution.py:153
  692.7 66.3 %collective-permute-start.2 = (bf16[1,1024,4,128]{3,1,2,0:T(8,128)(2,1)}, bf16[1,1024,4,128]{3,1,2,0:T(8,128)(2,1)S(1)}, u32[]{:S(2)}, u32[]{:S(2)}) collective-permute-start(bf16[1,1024,4,128]{3,1,2,0:T(8,128)(2,1)} %get-tuple-element.713), channel_id=1, source_target_pairs={{0,1},{1,2},{2,3},{3,4},{4,5},{5,6},{6,7},{7,0},{8,9},{9,10},{10,1... | collective-permute-start | bytes 3145736 | tf_op jit(solution)/shard_map/while/body/eval_jaxpr/ppermute | solution.py:153
  803.2 71.4 %collective-permute-start.5 = (f32[1,4,1024,128]{3,2,1,0:T(8,128)}, f32[1,4,1024,128]{3,2,1,0:T(8,128)}, u32[]{:S(2)}, u32[]{:S(2)}) collective-permute-start(f32[1,4,1024,128]{3,2,1,0:T(8,128)} %get-tuple-element.716), channel_id=1, source_target_pairs={{0,1},{1,2},{2,3},{3,4},{4,5},{5,6},{6,7},{7,0},{8,9},{9,10},{10,1... | collective-permute-start | bytes 6291464 | tf_op jit(solution)/shard_map/while/body/eval_jaxpr/ppermute | solution.py:153
  805.7 68.9 %collective-permute-start.4 = (f32[1,4,1024,128]{3,2,1,0:T(8,128)}, f32[1,4,1024,128]{3,2,1,0:T(8,128)}, u32[]{:S(2)}, u32[]{:S(2)}) collective-permute-start(f32[1,4,1024,128]{3,2,1,0:T(8,128)} %get-tuple-element.715), channel_id=1, source_target_pairs={{0,1},{1,2},{2,3},{3,4},{4,5},{5,6},{6,7},{7,0},{8,9},{9,10},{10,1... | collective-permute-start | bytes 6291464 | tf_op jit(solution)/shard_map/while/body/eval_jaxpr/ppermute | solution.py:153
  805.7 56.6 %collective-permute-start.3 = (bf16[1,1024,4,128]{3,1,2,0:T(8,128)(2,1)}, bf16[1,1024,4,128]{3,1,2,0:T(8,128)(2,1)}, u32[]{:S(2)}, u32[]{:S(2)}) collective-permute-start(bf16[1,1024,4,128]{3,1,2,0:T(8,128)(2,1)} %get-tuple-element.714), channel_id=1, source_target_pairs={{0,1},{1,2},{2,3},{3,4},{4,5},{5,6},{6,7},{7,0},{8,9},{9,10},{10,1... | collective-permute-start | bytes 3145736 | tf_op jit(solution)/shard_map/while/body/eval_jaxpr/ppermute | solution.py:153
  807.3 66.3 %collective-permute-start.2 = (bf16[1,1024,4,128]{3,1,2,0:T(8,128)(2,1)}, bf16[1,1024,4,128]{3,1,2,0:T(8,128)(2,1)S(1)}, u32[]{:S(2)}, u32[]{:S(2)}) collective-permute-start(bf16[1,1024,4,128]{3,1,2,0:T(8,128)(2,1)} %get-tuple-element.713), channel_id=1, source_target_pairs={{0,1},{1,2},{2,3},{3,4},{4,5},{5,6},{6,7},{7,0},{8,9},{9,10},{10,1... | collective-permute-start | bytes 3145736 | tf_op jit(solution)/shard_map/while/body/eval_jaxpr/ppermute | solution.py:153
  880.8 108.5 %collective-permute-start.5 = (f32[1,4,1024,128]{3,2,1,0:T(8,128)}, f32[1,4,1024,128]{3,2,1,0:T(8,128)}, u32[]{:S(2)}, u32[]{:S(2)}) collective-permute-start(f32[1,4,1024,128]{3,2,1,0:T(8,128)} %get-tuple-element.716), channel_id=1, source_target_pairs={{0,1},{1,2},{2,3},{3,4},{4,5},{5,6},{6,7},{7,0},{8,9},{9,10},{10,1... | collective-permute-start | bytes 6291464 | tf_op jit(solution)/shard_map/while/body/eval_jaxpr/ppermute | solution.py:153
  920.3 68.9 %collective-permute-start.4 = (f32[1,4,1024,128]{3,2,1,0:T(8,128)}, f32[1,4,1024,128]{3,2,1,0:T(8,128)}, u32[]{:S(2)}, u32[]{:S(2)}) collective-permute-start(f32[1,4,1024,128]{3,2,1,0:T(8,128)} %get-tuple-element.715), channel_id=1, source_target_pairs={{0,1},{1,2},{2,3},{3,4},{4,5},{5,6},{6,7},{7,0},{8,9},{9,10},{10,1... | collective-permute-start | bytes 6291464 | tf_op jit(solution)/shard_map/while/body/eval_jaxpr/ppermute | solution.py:153
  920.4 56.6 %collective-permute-start.3 = (bf16[1,1024,4,128]{3,1,2,0:T(8,128)(2,1)}, bf16[1,1024,4,128]{3,1,2,0:T(8,128)(2,1)}, u32[]{:S(2)}, u32[]{:S(2)}) collective-permute-start(bf16[1,1024,4,128]{3,1,2,0:T(8,128)(2,1)} %get-tuple-element.714), channel_id=1, source_target_pairs={{0,1},{1,2},{2,3},{3,4},{4,5},{5,6},{6,7},{7,0},{8,9},{9,10},{10,1... | collective-permute-start | bytes 3145736 | tf_op jit(solution)/shard_map/while/body/eval_jaxpr/ppermute | solution.py:153
  921.9 66.3 %collective-permute-start.2 = (bf16[1,1024,4,128]{3,1,2,0:T(8,128)(2,1)}, bf16[1,1024,4,128]{3,1,2,0:T(8,128)(2,1)S(1)}, u32[]{:S(2)}, u32[]{:S(2)}) collective-permute-start(bf16[1,1024,4,128]{3,1,2,0:T(8,128)(2,1)} %get-tuple-element.713), channel_id=1, source_target_pairs={{0,1},{1,2},{2,3},{3,4},{4,5},{5,6},{6,7},{7,0},{8,9},{9,10},{10,1... | collective-permute-start | bytes 3145736 | tf_op jit(solution)/shard_map/while/body/eval_jaxpr/ppermute | solution.py:153
  995.4 85.1 %collective-permute-start.5 = (f32[1,4,1024,128]{3,2,1,0:T(8,128)}, f32[1,4,1024,128]{3,2,1,0:T(8,128)}, u32[]{:S(2)}, u32[]{:S(2)}) collective-permute-start(f32[1,4,1024,128]{3,2,1,0:T(8,128)} %get-tuple-element.716), channel_id=1, source_target_pairs={{0,1},{1,2},{2,3},{3,4},{4,5},{5,6},{6,7},{7,0},{8,9},{9,10},{10,1... | collective-permute-start | bytes 6291464 | tf_op jit(solution)/shard_map/while/body/eval_jaxpr/ppermute | solution.py:153
  997.9 82.6 %collective-permute-start.4 = (f32[1,4,1024,128]{3,2,1,0:T(8,128)}, f32[1,4,1024,128]{3,2,1,0:T(8,128)}, u32[]{:S(2)}, u32[]{:S(2)}) collective-permute-start(f32[1,4,1024,128]{3,2,1,0:T(8,128)} %get-tuple-element.715), channel_id=1, source_target_pairs={{0,1},{1,2},{2,3},{3,4},{4,5},{5,6},{6,7},{7,0},{8,9},{9,10},{10,1... | collective-permute-start | bytes 6291464 | tf_op jit(solution)/shard_map/while/body/eval_jaxpr/ppermute | solution.py:153
  1086.6 88.5 %collective-permute-start.5 = (f32[1,4,1024,128]{3,2,1,0:T(8,128)}, f32[1,4,1024,128]{3,2,1,0:T(8,128)}, u32[]{:S(2)}, u32[]{:S(2)}) collective-permute-start(f32[1,4,1024,128]{3,2,1,0:T(8,128)} %get-tuple-element.716), channel_id=1, source_target_pairs={{0,1},{1,2},{2,3},{3,4},{4,5},{5,6},{6,7},{7,0},{8,9},{9,10},{10,1... | collective-permute-start | bytes 6291464 | tf_op jit(solution)/shard_map/while/body/eval_jaxpr/ppermute | solution.py:153
  1089.1 86.0 %collective-permute-start.4 = (f32[1,4,1024,128]{3,2,1,0:T(8,128)}, f32[1,4,1024,128]{3,2,1,0:T(8,128)}, u32[]{:S(2)}, u32[]{:S(2)}) collective-permute-start(f32[1,4,1024,128]{3,2,1,0:T(8,128)} %get-tuple-element.715), channel_id=1, source_target_pairs={{0,1},{1,2},{2,3},{3,4},{4,5},{5,6},{6,7},{7,0},{8,9},{9,10},{10,1... | collective-permute-start | bytes 6291464 | tf_op jit(solution)/shard_map/while/body/eval_jaxpr/ppermute | solution.py:153
  1181.2 96.0 %collective-permute-start.5 = (f32[1,4,1024,128]{3,2,1,0:T(8,128)}, f32[1,4,1024,128]{3,2,1,0:T(8,128)}, u32[]{:S(2)}, u32[]{:S(2)}) collective-permute-start(f32[1,4,1024,128]{3,2,1,0:T(8,128)} %get-tuple-element.716), channel_id=1, source_target_pairs={{0,1},{1,2},{2,3},{3,4},{4,5},{5,6},{6,7},{7,0},{8,9},{9,10},{10,1... | collective-permute-start | bytes 6291464 | tf_op jit(solution)/shard_map/while/body/eval_jaxpr/ppermute | solution.py:153
  1183.7 93.5 %collective-permute-start.4 = (f32[1,4,1024,128]{3,2,1,0:T(8,128)}, f32[1,4,1024,128]{3,2,1,0:T(8,128)}, u32[]{:S(2)}, u32[]{:S(2)}) collective-permute-start(f32[1,4,1024,128]{3,2,1,0:T(8,128)} %get-tuple-element.715), channel_id=1, source_target_pairs={{0,1},{1,2},{2,3},{3,4},{4,5},{5,6},{6,7},{7,0},{8,9},{9,10},{10,1... | collective-permute-start | bytes 6291464 | tf_op jit(solution)/shard_map/while/body/eval_jaxpr/ppermute | solution.py:153
  1283.4 80.1 %collective-permute-start.5 = (f32[1,4,1024,128]{3,2,1,0:T(8,128)}, f32[1,4,1024,128]{3,2,1,0:T(8,128)}, u32[]{:S(2)}, u32[]{:S(2)}) collective-permute-start(f32[1,4,1024,128]{3,2,1,0:T(8,128)} %get-tuple-element.716), channel_id=1, source_target_pairs={{0,1},{1,2},{2,3},{3,4},{4,5},{5,6},{6,7},{7,0},{8,9},{9,10},{10,1... | collective-permute-start | bytes 6291464 | tf_op jit(solution)/shard_map/while/body/eval_jaxpr/ppermute | solution.py:153
  1285.9 77.6 %collective-permute-start.4 = (f32[1,4,1024,128]{3,2,1,0:T(8,128)}, f32[1,4,1024,128]{3,2,1,0:T(8,128)}, u32[]{:S(2)}, u32[]{:S(2)}) collective-permute-start(f32[1,4,1024,128]{3,2,1,0:T(8,128)} %get-tuple-element.715), channel_id=1, source_target_pairs={{0,1},{1,2},{2,3},{3,4},{4,5},{5,6},{6,7},{7,0},{8,9},{9,10},{10,1... | collective-permute-start | bytes 6291464 | tf_op jit(solution)/shard_map/while/body/eval_jaxpr/ppermute | solution.py:153
  1372.8 81.4 %collective-permute-start.6 = (f32[1,4,1024,128]{2,3,1,0:T(8,128)}, f32[1,4,1024,128]{2,3,1,0:T(8,128)}, u32[]{:S(2)}, u32[]{:S(2)}) collective-permute-start(f32[1,4,1024,128]{2,3,1,0:T(8,128)} %copy.43), channel_id=1, source_target_pairs={{0,1},{1,2},{2,3},{3,4},{4,5},{5,6},{6,7},{7,0},{8,9},{9,10},{10,1... | collective-permute-start | bytes 6291464 | tf_op jit(solution)/shard_map/ppermute | solution.py:166
  1480.9 399.9 %all-reduce.10.cloned.1.call-start = ((), (), s32[]{:S(2)}) async-start(), calls=%async_computation.1 | async-start | bytes 16777216 | tf_op jit(solution)/shard_map/psum | solution.py:181
  (80 other events, 1991.4 us)
Sparse Core Ops, SparseCore 0:
  424.2 216.2 all-reduce.7
  1481.1 241.9 all-reduce.11
  1725.5 155.2 all-reduce.9
where the time goes:
time: 1910 us; the launch traced here: 1900 us
  waiting for transfers between devices  919 us (48%)
  starting transfers between devices  489 us (26%)
  matrix products  158 us (8%)
  local copies, waits for them, and re-layouts  152 us (8%)
  blocking collectives  107 us (6%)
  other arithmetic  59.4 us (3%)
    ppermute x28, starting transfers between devices, bwd_step(): lax.ppermute((k_cur, v_cur, dk_cur, dv_cur), 'cp', perm_next)  297 us
    ppermute x28, waiting for transfers between devices, bwd_step(): lax.ppermute((k_cur, v_cur, dk_cur, dv_cur), 'cp', perm_next)  281 us
    psum x1, waiting for transfers between devices, local_run(): lax.psum(jnp.einsum('blhe,hed->bld', attn_out, w_o, preferred_element_typ...  216 us
    ppermute x14, starting transfers between devices, fwd_step(): k_cur, v_cur = lax.ppermute((k_cur, v_cur), 'cp', perm_next)  150 us
    psum x1, waiting for transfers between devices, local_run(): grad_x = (grad_f + lax.psum(grad_x_part, 'tp')).astype(jnp.bfloat16)  142 us
    psum x1, waiting for transfers between devices, local_run(): lax.psum((grad_w_q, grad_w_k, grad_w_v, grad_w_o, grad_q_norm, grad_k_nor...  140 us
    ppermute x14, waiting for transfers between devices, fwd_step(): k_cur, v_cur = lax.ppermute((k_cur, v_cur), 'cp', perm_next)  116 us
    while x42, local copies, waits for them, and re-layouts  97.4 us
  transfers between devices with their start and end apart: 47, of which 29 were waited for; matrix products, arithmetic and copies ran while one was open for 3% of the time, Pallas kernels for 0%

commit v1 on v0

v1 whole, which is shorter than its diff:
```python
import functools
import math

import jax
import jax.numpy as jnp
from jax import lax
from jax.experimental import pallas as pl
from jax.experimental.pallas import tpu as pltpu
from jax.sharding import PartitionSpec as P

ROPE_THETA = 500000.0
NORM_EPS = 1e-6
LOG2E = 1.4426950408889634
VMEM = pltpu.VMEM
MESH = pl.DeviceIdType.MESH
NT = (((1,), (1,)), ((), ()))


def rope_tables(start_pos, seq_rows, head_dim):
    half_dim = head_dim // 2
    inv_freq = ROPE_THETA ** (-2.0 * jnp.arange(half_dim, dtype=jnp.float32) / head_dim)
    positions = (start_pos + jnp.arange(seq_rows)).astype(jnp.float32)
    angles = positions[:, None] * inv_freq[None, :]
    return jnp.cos(angles), jnp.sin(angles)


def apply_rope(values, cos_tab, sin_tab):
    half_dim = values.shape[-1] // 2
    low_half = values[..., :half_dim]
    high_half = values[..., half_dim:]
    return jnp.concatenate([low_half * cos_tab - high_half * sin_tab, high_half * cos_tab + low_half * sin_tab], axis=-1)


def rope_back(grad_in, cos_tab, sin_tab):
    return apply_rope(grad_in, cos_tab, -sin_tab)


def vmem_call(kernel, out_shape, n_in, scratch, collective_id=None, limit=48 << 20, cost=None):
    params = dict(vmem_limit_bytes=limit)
    if collective_id is not None:
        params.update(collective_id=collective_id, has_side_effects=True)
    return pl.pallas_call(
        kernel,
        out_shape=out_shape,
        in_specs=[pl.BlockSpec(memory_space=VMEM)] * n_in,
        out_specs=[pl.BlockSpec(memory_space=VMEM)] * len(out_shape),
        scratch_shapes=scratch,
        compiler_params=pltpu.CompilerParams(**params),
        cost_estimate=cost,
    )


def remote(src, dst, send_sem, recv_sem, device_id):
    return pltpu.make_async_remote_copy(src_ref=src, dst_ref=dst, send_sem=send_sem, recv_sem=recv_sem, device_id=device_id, device_id_type=MESH)


def cp_barrier(me, cp_size):
    barrier = pltpu.get_barrier_semaphore()
    for step in range(1, cp_size):
        pl.semaphore_signal(barrier, inc=1, device_id={"cp": lax.rem(me + step, cp_size)}, device_id_type=MESH)
    pl.semaphore_wait(barrier, cp_size - 1)


def group_barrier(me_tp, me_cp, tp_size, cp_size):
    barrier = pltpu.get_barrier_semaphore()
    for st in range(tp_size):
        for sc in range(cp_size):
            if st or sc:
                pl.semaphore_signal(barrier, inc=1, device_id={"tp": lax.rem(me_tp + st, tp_size), "cp": lax.rem(me_cp + sc, cp_size)}, device_id_type=MESH)
    pl.semaphore_wait(barrier, tp_size * cp_size - 1)


def scatter_qkv(heads, cp_size, q_in, k_in, v_in, q_out, k_out, v_out, loc, qs, qr, ks, kr, vs, vr, fks, fkr, fvs, fvr):
    me = lax.axis_index("cp")
    core = lax.rem(me, 2)
    chip = me // 2
    cp_barrier(me, cp_size)
    sends = []
    for r in (1, heads - 1, 2):
        dst = lax.rem(chip + r, heads)
        sends.append(remote(k_in.at[dst], k_out.at[me], ks.at[r], kr.at[r], {"cp": dst * 2 + core}))
        sends.append(remote(v_in.at[dst], v_out.at[me], vs.at[r], vr.at[r], {"cp": dst * 2 + core}))
    for r in range(1, cp_size):
        dst = lax.rem(me + r, cp_size)
        sends.append(remote(q_in.at[dst], q_out.at[me], qs.at[r], qr.at[r], {"cp": dst}))
    for copy in sends:
        copy.start()
    local = [
        pltpu.make_async_copy(q_in.at[me], q_out.at[me], loc.at[0]),
        pltpu.make_async_copy(k_in.at[chip], k_out.at[me], loc.at[1]),
        pltpu.make_async_copy(v_in.at[chip], v_out.at[me], loc.at[2]),
    ]
    for copy in local:
        copy.start()
    partner = {"cp": me + 1 - 2 * core}
    forwards = []
    for r in (0, 1, heads - 1, 2):
        src = lax.rem(chip - r + heads, heads) * 2 + core
        if r == 0:
            local[1].wait()
            local[2].wait()
        else:
            remote(k_in.at[0], k_out.at[src], ks.at[r], kr.at[r], partner).wait_recv()
            remote(v_in.at[0], v_out.at[src], vs.at[r], vr.at[r], partner).wait_recv()
        for buf, ss, rs in ((k_out, fks, fkr), (v_out, fvs, fvr)):
            copy = remote(buf.at[src], buf.at[src], ss.at[r], rs.at[r], partner)
            copy.start()
            forwards.append(copy)
    local[0].wait()
    for copy in sends:
        copy.wait_send()
    for r in range(1, cp_size):
        remote(q_in.at[0], q_out.at[lax.rem(me - r + cp_size, cp_size)], qs.at[r], qr.at[r], partner).wait_recv()
    for copy in forwards:
        copy.wait()


def attend(sub, scale, q_ref, k_ref, v_ref, o_ref, lse_ref, vt_scr, m_scr, l_scr, acc_scr):
    blk = pl.program_id(0)
    core = lax.rem(lax.axis_index("cp"), 2)
    coef = scale * LOG2E
    block_len = k_ref.shape[1]
    vt_scr[blk] = v_ref[blk].T
    m_scr[...] = jnp.full_like(m_scr, -jnp.inf)
    l_scr[...] = jnp.zeros_like(l_scr)
    acc_scr[...] = jnp.zeros_like(acc_scr)

    def step(b, masked):
        k_blk = k_ref[b]
        vt_blk = vt_scr[b]
        for part in range(2):
            cols = slice(part * sub, (part + 1) * sub)
            s = lax.dot_general(k_blk, q_ref[0, cols, :], NT, preferred_element_type=jnp.float32)
            if masked:
                first = (core if part == 0 else 3 - core) * sub
                kv_pos = lax.broadcasted_iota(jnp.int32, (block_len, sub), 0)
                q_pos = first + lax.broadcasted_iota(jnp.int32, (block_len, sub), 1)
                s = jnp.where(kv_pos <= q_pos, s, -jnp.inf)
            m_old = m_scr[:, cols]
            m_new = jnp.maximum(m_old, jnp.max(s, axis=0, keepdims=True))
            p = jnp.exp2(s * coef - m_new * coef)
            alpha = jnp.exp2((m_old - m_new) * coef)
            l_scr[:, cols] = l_scr[:, cols] * alpha + jnp.sum(p, axis=0, keepdims=True)
            acc_scr[:, cols] = acc_scr[:, cols] * alpha + jnp.dot(vt_blk, p.astype(jnp.bfloat16), preferred_element_type=jnp.float32)
            m_scr[:, cols] = m_new

    def body(b, carry):
        step(b, False)
        return carry

    lax.fori_loop(0, blk, body, 0)
    step(blk, True)
    o_ref[0] = (acc_scr[...] / l_scr[...]).T.astype(o_ref.dtype)
    lse_ref[0] = m_scr[...] * coef + jnp.log2(l_scr[...])


def attend_back(sub, scale, q_ref, k_ref, v_ref, o_ref, do_ref, lse_ref, dq_ref, dk_ref, dv_ref, kt_scr, dqt_scr, dl_scr):
    blk = pl.program_id(0)
    core = lax.rem(lax.axis_index("cp"), 2)
    coef = scale * LOG2E
    rows = q_ref.shape[1]
    block_len = k_ref.shape[1]
    kt_scr[blk] = k_ref[blk].T
    prod = o_ref[0].astype(jnp.float32) * do_ref[0].astype(jnp.float32)
    dl_scr[...] = jnp.sum(prod.T, axis=0, keepdims=True)
    dqt_scr[...] = jnp.zeros_like(dqt_scr)

    def step(b, masked):
        q = q_ref[0]
        do = do_ref[0]
        lse = lse_ref[0]
        delta = dl_scr[...]
        for part in range(block_len // sub):
            kv = slice(part * sub, (part + 1) * sub)
            k_blk = k_ref[b, kv, :]
            s = lax.dot_general(k_blk, q, NT, preferred_element_type=jnp.float32)
            p = jnp.exp2(s * coef - lse)
            if masked:
                kv_pos = part * sub + lax.broadcasted_iota(jnp.int32, (sub, rows), 0)
                col = lax.broadcasted_iota(jnp.int32, (sub, rows), 1)
                q_pos = jnp.where(col < sub, core * sub + col, (2 - core) * sub + col)
                p = jnp.where(kv_pos <= q_pos, p, 0.0)
            dp = lax.dot_general(v_ref[b, kv, :], do, NT, preferred_element_type=jnp.float32)
            ds = (p * (dp - delta)).astype(jnp.bfloat16)
            new_v = jnp.dot(p.astype(jnp.bfloat16), do, preferred_element_type=jnp.float32)
            new_k = jnp.dot(ds, q, preferred_element_type=jnp.float32) * scale
            if masked:
                dv_ref[b, kv, :] = new_v
                dk_ref[b, kv, :] = new_k
            else:
                dv_ref[b, kv, :] += new_v
                dk_ref[b, kv, :] += new_k
            dqt_scr[...] += jnp.dot(kt_scr[b, :, kv], ds, preferred_element_type=jnp.float32)

    def body(b, carry):
        step(b, False)
        return carry

    step(blk, True)
    lax.fori_loop(0, blk, body, 0)
    dq_ref[0] = dqt_scr[...].T * scale


def heads_to_rows(heads, tp_size, cp_size, o_in, o_out, ss, rs, loc):
    me_tp = lax.axis_index("tp")
    me_cp = lax.axis_index("cp")
    core = lax.rem(me_cp, 2)
    head = me_tp * heads + me_cp // 2
    sub = o_out.shape[1]
    group_barrier(me_tp, me_cp, tp_size, cp_size)
    for s in range(2):
        dst_tp = core if s == 0 else 3 - core
        for r in range(cp_size):
            dst_cp = lax.rem(me_cp + r, cp_size)
            src = o_in.at[dst_cp, pl.ds(s * sub, sub), :]
            if r == 0:
                own = dst_tp == me_tp

                @pl.when(own)
                def _():
                    pltpu.make_async_copy(src, o_out.at[head], rs.at[head]).start()

                @pl.when(jnp.logical_not(own))
                def _():
                    remote(src, o_out.at[head], ss.at[s, 0], rs.at[head], {"tp": dst_tp, "cp": dst_cp}).start()
            else:
                remote(src, o_out.at[head], ss.at[s, r], rs.at[head], {"tp": dst_tp, "cp": dst_cp}).start()
    for h in range(heads * tp_size):
        pltpu.make_async_copy(o_out.at[h], o_out.at[h], rs.at[h]).wait()
    for s in range(2):
        dst_tp = core if s == 0 else 3 - core
        for r in range(cp_size):
            wait = remote(o_in.at[0, pl.ds(0, sub), :], o_out.at[head], ss.at[s, r], rs.at[head], {"cp": me_cp})
            if r == 0:
                @pl.when(dst_tp != me_tp)
                def _():
                    wait.wait_send()
            else:
                wait.wait_send()


def rows_to_heads(heads, tp_size, cp_size, g_in, g_out, ss, rs, loc):
    me_tp = lax.axis_index("tp")
    me_cp = lax.axis_index("cp")
    core = lax.rem(me_cp, 2)
    sub = g_in.shape[1]
    row_core = jnp.where(me_tp < 2, me_tp, 3 - me_tp)
    row_slot = me_tp // 2
    group_barrier(me_tp, me_cp, tp_size, cp_size)
    for rt in range(tp_size):
        dst_tp = lax.rem(me_tp + rt, tp_size)
        for r in range(heads):
            dst_chip = lax.rem(me_cp // 2 + r, heads)
            dst_cp = dst_chip * 2 + row_core
            src = g_in.at[dst_tp * heads + dst_chip]
            dst = g_out.at[me_cp, pl.ds(row_slot * sub, sub), :]
            if rt == 0 and r == 0:
                @pl.when(row_core == core)
                def _():
                    pltpu.make_async_copy(src, dst, rs.at[me_cp, row_slot]).start()

                @pl.when(row_core != core)
                def _():
                    remote(src, dst, ss.at[rt, r], rs.at[me_cp, row_slot], {"tp": dst_tp, "cp": dst_cp}).start()
            else:
                remote(src, dst, ss.at[rt, r], rs.at[me_cp, row_slot], {"tp": dst_tp, "cp": dst_cp}).start()
    for i in range(cp_size):
        for s in range(2):
            part = g_out.at[i, pl.ds(s * sub, sub), :]
            pltpu.make_async_copy(part, part, rs.at[i, s]).wait()
    for rt in range(tp_size):
        for r in range(heads):
            wait = remote(g_in.at[0], g_out.at[0, pl.ds(0, sub), :], ss.at[rt, r], rs.at[0, 0], {"cp": me_cp})
            if rt == 0 and r == 0:
                @pl.when(row_core != core)
                def _():
                    wait.wait_send()
            else:
                wait.wait_send()


def gather_grads(heads, cp_size, dq_in, dk_in, dv_in, dq_out, dk_out, dv_out, pk, pv, sk, sv, loc, qs, qr, pks, pkr, pvs, pvr, ks, kr, vs, vr):
    me = lax.axis_index("cp")
    core = lax.rem(me, 2)
    chip = me // 2
    cp_barrier(me, cp_size)
    partner = {"cp": me + 1 - 2 * core}
    pair = []
    for x in range(heads):
        for src, dst, ss, rs in ((dk_in, pk, pks, pkr), (dv_in, pv, pvs, pvr)):
            copy = remote(src.at[2 * x + 1 - core], dst.at[x], ss.at[x], rs.at[x], partner)
            copy.start()
            pair.append(copy)
    sends = []
    for r in range(1, cp_size):
        dst = lax.rem(me + r, cp_size)
        copy = remote(dq_in.at[dst], dq_out.at[chip, core], qs.at[r], qr.at[r], {"cp": dst})
        copy.start()
        sends.append(copy)
    own = pltpu.make_async_copy(dq_in.at[me], dq_out.at[chip, core], loc.at[0])
    own.start()
    for x in range(heads):
        pair[2 * x].wait()
        pair[2 * x + 1].wait()
        sk[x] = dk_in[2 * x + core] + pk[x]
        sv[x] = (dv_in[2 * x + core] + pv[x]).astype(sv.dtype)
    for r in (1, heads - 1, 2):
        dst = lax.rem(chip + r, heads)
        for src, out, ss, rs in ((sk, dk_out, ks, kr), (sv, dv_out, vs, vr)):
            copy = remote(src.at[dst], out.at[chip], ss.at[r], rs.at[r], {"cp": dst * 2 + core})
            copy.start()
            sends.append(copy)
    locals_ = [pltpu.make_async_copy(sk.at[chip], dk_out.at[chip], loc.at[1]), pltpu.make_async_copy(sv.at[chip], dv_out.at[chip], loc.at[2])]
    for copy in locals_:
        copy.start()
    own.wait()
    for copy in locals_:
        copy.wait()
    for copy in sends:
        copy.wait_send()
    for r in range(1, cp_size):
        src = lax.rem(me - r + cp_size, cp_size)
        remote(dq_in.at[0], dq_out.at[src // 2, lax.rem(src, 2)], qs.at[r], qr.at[r], partner).wait_recv()
    for r in (1, heads - 1, 2):
        src = lax.rem(chip - r + heads, heads)
        remote(sk.at[0], dk_out.at[src], ks.at[r], kr.at[r], partner).wait_recv()
        remote(sv.at[0], dv_out.at[src], vs.at[r], vr.at[r], partner).wait_recv()


def solution(mesh):
    tp_size = mesh.shape["tp"]
    cp_size = mesh.shape["cp"]
    act_spec = P("dp", "cp", None)
    col_spec = P(None, "tp", None)
    part_col = P("dp", "tp", None)
    in_specs = (act_spec, col_spec, col_spec, col_spec, P("tp", None, None), P("tp", None), P("tp", None), P(None), act_spec)
    out_specs = (act_spec, act_spec, part_col, part_col, part_col, P(("dp", "tp"), None, None), P(("dp", "tp"), None), P(("dp", "tp"), None), P("dp"))
    dma = pltpu.SemaphoreType.DMA

    def local_run(x_in, w_q, w_k, w_v, w_o, q_norm_w, k_norm_w, post_norm_w, grad_y):
        n_batch, block_len, d_model = x_in.shape
        heads, head_dim = w_q.shape[1:]
        assert n_batch == 1 and w_k.shape[1] == heads and cp_size == 2 * heads and tp_size == 4
        sub = block_len // tp_size
        rows = 2 * sub
        width = heads * head_dim * tp_size
        scale = head_dim ** -0.5
        f32 = jnp.float32
        b16 = jnp.bfloat16
        tp_index = lax.axis_index("tp")
        cp_index = lax.axis_index("cp")
        cos_tab, sin_tab = rope_tables(cp_index * block_len, block_len, head_dim)
        x_loc = x_in[0]
        dy_loc = grad_y[0]
        w_o_full = lax.all_gather(w_o, "tp", axis=0, tiled=True)

        q_lin = jnp.einsum("ld,dhe->hle", x_loc, w_q, preferred_element_type=f32)
        k_lin = jnp.einsum("ld,dhe->hle", x_loc, w_k, preferred_element_type=f32)
        v_lin = jnp.einsum("ld,dhe->hle", x_loc, w_v, preferred_element_type=f32)
        sq = lax.psum(jnp.stack([jnp.sum(q_lin * q_lin, axis=(0, 2)), jnp.sum(k_lin * k_lin, axis=(0, 2))]), "tp")
        inv = lax.rsqrt(sq / width + NORM_EPS)
        q_inv = inv[0][None, :, None]
        k_inv = inv[1][None, :, None]
        q_rot = apply_rope(q_lin * q_inv * q_norm_w[:, None, :], cos_tab, sin_tab).astype(b16)
        k_rot = apply_rope(k_lin * k_inv * k_norm_w[:, None, :], cos_tab, sin_tab).astype(b16)
        v_val = v_lin.astype(b16)

        q4 = q_rot.reshape(heads, 4, sub, head_dim)
        q_send = jnp.stack([q4[:, 0], q4[:, 3], q4[:, 1], q4[:, 2]], axis=1).reshape(cp_size, rows, head_dim)
        q_all, k_all, v_all = vmem_call(
            functools.partial(scatter_qkv, heads, cp_size),
            [jax.ShapeDtypeStruct((cp_size, rows, head_dim), b16)] + [jax.ShapeDtypeStruct((cp_size, block_len, head_dim), b16)] * 2,
            3,
            [dma((3,)), dma((cp_size,)), dma((cp_size,))] + [dma((heads,))] * 8,
            collective_id=0,
        )(q_send, k_rot, v_val)

        qspec = pl.BlockSpec((1, rows, head_dim), lambda i: (i, 0, 0))
        lspec = pl.BlockSpec((1, 1, rows), lambda i: (i, 0, 0))
        whole = pl.BlockSpec(memory_space=VMEM)
        pair_flops = cp_size * (cp_size + 1) // 2 * rows * block_len * head_dim * 2
        o_all, lse = pl.pallas_call(
            functools.partial(attend, sub, scale),
            grid=(cp_size,),
            in_specs=[qspec, whole, whole],
            out_specs=[qspec, lspec],
            out_shape=[jax.ShapeDtypeStruct((cp_size, rows, head_dim), b16), jax.ShapeDtypeStruct((cp_size, 1, rows), f32)],
            scratch_shapes=[VMEM((cp_size, head_dim, block_len), b16), VMEM((1, rows), f32), VMEM((1, rows), f32), VMEM((head_dim, rows), f32)],
            compiler_params=pltpu.CompilerParams(vmem_limit_bytes=48 << 20),
            cost_estimate=pl.CostEstimate(flops=2 * pair_flops, bytes_accessed=6 << 20, transcendentals=0),
        )(q_all, k_all, v_all)

        n_heads = heads * tp_size
        o_rows = vmem_call(
            functools.partial(heads_to_rows, heads, tp_size, cp_size),
            [jax.ShapeDtypeStruct((n_heads, sub, head_dim), b16)],
            1,
            [dma((2, cp_size)), dma((n_heads,)), dma((1,))],
            collective_id=1,
        )(o_all)[0]

        x_rows = lax.dynamic_slice_in_dim(x_loc, tp_index * sub, sub, 0)
        dy_rows = lax.dynamic_slice_in_dim(dy_loc, tp_index * sub, sub, 0).astype(f32)
        proj = jnp.einsum("hle,hed->ld", o_rows, w_o_full, preferred_element_type=f32)
        post_inv = lax.rsqrt(jnp.mean(proj * proj, axis=-1, keepdims=True) + NORM_EPS)
        post_hat = proj * post_inv
        y_rows = (x_rows + post_hat * post_norm_w).astype(b16)
        grad_post = jnp.sum(dy_rows * post_hat, axis=0)
        grad_hat = dy_rows * post_norm_w
        gp_rows = (post_inv * (grad_hat - post_hat * jnp.mean(grad_hat * post_hat, axis=-1, keepdims=True))).astype(b16)
        do_rows = jnp.einsum("ld,hed->hle", gp_rows, w_o_full, preferred_element_type=f32).astype(b16)

        do_all = vmem_call(
            functools.partial(rows_to_heads, heads, tp_size, cp_size),
            [jax.ShapeDtypeStruct((cp_size, rows, head_dim), b16)],
            1,
            [dma((tp_size, heads)), dma((cp_size, 2)), dma((1,))],
            collective_id=2,
        )(do_rows)[0]

        y_out = lax.all_gather(y_rows, "tp", axis=0, tiled=True)
        grad_proj = lax.all_gather(gp_rows, "tp", axis=0, tiled=True)
        o_gath = lax.all_gather(o_rows, "tp", axis=0)
        o_own = lax.dynamic_slice_in_dim(o_gath, tp_index * heads, heads, 1)

        dq_all, dk_all, dv_all = pl.pallas_call(
            functools.partial(attend_back, sub, scale),
            grid=(cp_size,),
            in_specs=[qspec, whole, whole, qspec, qspec, lspec],
            out_specs=[qspec, whole, whole],
            out_shape=[jax.ShapeDtypeStruct((cp_size, rows, head_dim), f32)] + [jax.ShapeDtypeStruct((cp_size, block_len, head_dim), f32)] * 2,
            scratch_shapes=[VMEM((cp_size, head_dim, block_len), b16), VMEM((head_dim, rows), f32), VMEM((1, rows), f32)],
            compiler_params=pltpu.CompilerParams(vmem_limit_bytes=48 << 20),
            cost_estimate=pl.CostEstimate(flops=5 * pair_flops, bytes_accessed=16 << 20, transcendentals=0),
        )(q_all, k_all, v_all, o_all, do_all, lse)

        grad_w_o = jnp.einsum("thle,tld->hed", o_own, grad_proj.reshape(tp_size, sub, d_model), preferred_element_type=f32)

        dq_home, dk_home, dv_home = vmem_call(
            functools.partial(gather_grads, heads, cp_size),
            [jax.ShapeDtypeStruct((heads, 2, rows, head_dim), f32), jax.ShapeDtypeStruct((heads, block_len, head_dim), f32), jax.ShapeDtypeStruct((heads, block_len, head_dim), b16)],
            3,
            [VMEM((heads, block_len, head_dim), f32)] * 3 + [VMEM((heads, block_len, head_dim), b16)]
            + [dma((3,)), dma((cp_size,)), dma((cp_size,))] + [dma((heads,))] * 8,
            collective_id=3,
        )(dq_all, dk_all, dv_all)
        dq5 = dq_home.reshape(heads, 4, sub, head_dim)
        dq_rot = jnp.stack([dq5[:, 0], dq5[:, 2], dq5[:, 3], dq5[:, 1]], axis=1).reshape(heads, block_len, head_dim)

        dq_s = rope_back(dq_rot, cos_tab, sin_tab)
        dk_s = rope_back(dk_home, cos_tab, sin_tab)
        q_hat = q_lin * q_inv
        k_hat = k_lin * k_inv
        grad_qn = jnp.sum(dq_s * q_hat, axis=1)
        grad_kn = jnp.sum(dk_s * k_hat, axis=1)
        dq_n = dq_s * q_norm_w[:, None, :]
        dk_n = dk_s * k_norm_w[:, None, :]
        dots = lax.psum(jnp.stack([jnp.sum(dq_n * q_hat, axis=(0, 2)), jnp.sum(dk_n * k_hat, axis=(0, 2))]), "tp") / width
        dq16 = (q_inv * (dq_n - q_hat * dots[0][None, :, None])).astype(b16)
        dk16 = (k_inv * (dk_n - k_hat * dots[1][None, :, None])).astype(b16)
        grad_w_q = jnp.einsum("ld,hle->dhe", x_loc, dq16, preferred_element_type=f32)
        grad_w_k = jnp.einsum("ld,hle->dhe", x_loc, dk16, preferred_element_type=f32)
        grad_w_v = jnp.einsum("ld,hle->dhe", x_loc, dv_home, preferred_element_type=f32)
        dx_part = (jnp.einsum("hle,dhe->ld", dq16, w_q, preferred_element_type=f32)
                   + jnp.einsum("hle,dhe->ld", dk16, w_k, preferred_element_type=f32)
                   + jnp.einsum("hle,dhe->ld", dv_home, w_v, preferred_element_type=f32))
        dx_rows = lax.psum_scatter(dx_part, "tp", scatter_dimension=0, tiled=True)
        grad_x = lax.all_gather((dy_rows + dx_rows).astype(b16), "tp", axis=0, tiled=True)
        grad_post = lax.psum(grad_post, ("tp", "cp"))
        weight_grads = lax.psum((grad_w_q, grad_w_k, grad_w_v, grad_w_o, grad_qn, grad_kn), "cp")
        return (y_out[None], grad_x[None]) + tuple(weight_grads) + (grad_post,)

    return jax.shard_map(local_run, mesh=mesh, in_specs=in_specs, out_specs=out_specs, check_vma=False)
```

time: 1910 us -> 757 us (0.40)
  waiting for transfers between devices: 919 us -> 254 us
  starting transfers between devices: 489 us -> 1.12 us
  Pallas kernels: 0 us -> 270 us
  local copies, waits for them, and re-layouts: 152 us -> 45.2 us
  matrix products: 158 us -> 60.2 us
  other arithmetic: 59.4 us -> 24.5 us
  blocking collectives: 107 us -> 82.4 us
    ppermute x44 -> x0, starting transfers between devices: 489 us -> none  [the longest x28 297 us: bwd_step(): lax.ppermute((k_cur, v_cur, dk_cur, dv_cur), 'cp', perm_next)]
    ppermute x44 -> x0, waiting for transfers between devices: 420 us -> none  [the longest x28 281 us: bwd_step(): lax.ppermute((k_cur, v_cur, dk_cur, dv_cur), 'cp', perm_next)]
    psum x3 -> x1, waiting for transfers between devices: 499 us -> 166 us  [local_run(): lax.psum((grad_w_q, grad_w_k, grad_w_v, grad_w_o, grad_qn, grad_kn), 'cp')]
    pallas_call x0 -> x6, Pallas kernels: none -> 270 us  [the longest x1 64.4 us: local_run(): vmem_call(functools.partial(gather_grads, heads, cp_size), [jax.ShapeDtyp...]
    while x48 -> x0, local copies, waits for them, and re-layouts: 110 us -> none
    dot_general x23 -> x12, matrix products: 147 us -> 60.2 us  [the longest x1 7.05 us: local_run(): jnp.einsum('ld,hle->dhe', x_loc, dq16, preferred_element_type=f32)]
    reduce_scatter x0 -> x1, waiting for transfers between devices: none -> 53.7 us  [local_run(): dx_rows = lax.psum_scatter(dx_part, 'tp', scatter_dimension=0, tiled=True)]
    all_gather x0 -> x5, waiting for transfers between devices: none -> 32.4 us  [the longest x1 32.4 us: local_run(): lax.all_gather((dy_rows + dx_rows).astype(b16), 'tp', axis=0, tiled=True)]
  transfers between devices with their start and end apart: 47 -> 7, of which waited for: 29 -> 3; matrix products, arithmetic and copies ran while one was open for 3% -> 14% of each run, Pallas kernels for 0% -> 36%
where the time goes in v1:
time: 757 us; the launch traced here: 752 us
  Pallas kernels  270 us (36%)
  waiting for transfers between devices  254 us (34%)
  blocking collectives  82.4 us (11%)
  matrix products  60.2 us (8%)
  local copies, waits for them, and re-layouts  45.2 us (6%)
  other arithmetic  24.5 us (3%)
  between operations  15.2 us (2%)
    psum x1, waiting for transfers between devices, local_run(): lax.psum((grad_w_q, grad_w_k, grad_w_v, grad_w_o, grad_qn, grad_kn), 'cp')  166 us
    pallas_call x1, Pallas kernels, local_run(): vmem_call(functools.partial(gather_grads, heads, cp_size), [jax.ShapeDtyp...  64.4 us
    pallas_call x1, Pallas kernels, local_run(): pl.pallas_call(functools.partial(attend, sub, scale), grid=(cp_size,), in...  60.9 us
    pallas_call x1, Pallas kernels, local_run(): pl.pallas_call(functools.partial(attend_back, sub, scale), grid=(cp_size,...  58.5 us
    reduce_scatter x1, waiting for transfers between devices, local_run(): dx_rows = lax.psum_scatter(dx_part, 'tp', scatter_dimension=0, tiled=True)  53.7 us
    psum x1, blocking collectives, local_run(): grad_post = lax.psum(grad_post, ('tp', 'cp'))  46.1 us
    pallas_call x1, Pallas kernels, local_run(): vmem_call(functools.partial(scatter_qkv, heads, cp_size), [jax.ShapeDtype...  43.3 us
    unnamed x70, local copies, waits for them, and re-layouts  39.2 us
  transfers between devices with their start and end apart: 7, of which 3 were waited for; matrix products, arithmetic and copies ran while one was open for 14% of the time, Pallas kernels for 36%

profile of v1, /device:TPU:97, one launch (start us, length us, event | category | flops | bytes accessed | tf_op | source)
XLA Modules:
  0.0 751.5 jit_solution(11347952068270494823)
XLA Ops:
  8.1 6.5 multiply_reduce_fusion.2
  17.5 6.5 multiply_reduce_fusion.1
  26.9 13.0 %psum.63 = f32[2,1024]{1,0:T(2,128)S(1)} all-reduce(f32[2,1024]{1,0:T(2,128)S(1)} %pad_maximum_fusion.4), channel_id=1, replica_groups=mesh['dp'=1,'tp'=4,'cp'=8] {'tp'}, use_global_device_ids=true, to_apply=%region_2.0 | all-reduce | flops 2048 | bytes 16384 | tf_op jit(solution)/shard_map/psum | solution.py:360
  51.9 43.3 %shard_map.160 = (bf16[8,512,128]{2,1,0:T(8,128)(2,1)S(1)}, bf16[8,1024,128]{2,1,0:T(8,128)(2,1)}, bf16[8,1024,128]{2,1,0:T(8,128)(2,1)}) custom-call(bf16[8,512,128]{2,1,0:T(8,128)(2,1)S(1)} %bitcast.126, bf16[4,1024,128]{2,1,0:T(8,128)(2,1)S(1)} %pad_maximum_fusion.3.k_in, bf16[4,1024,128]{2,1,0:T(8,128)(2,1)S(1)} %fusion.60.v_in), custom_call_target="tpu_custom_call" | custom-call | tf_op jit(solution)/shard_map/pallas_call | solution.py:370
  97.2 60.9 %shard_map.161 = (bf16[8,512,128]{2,1,0:T(8,128)(2,1)S(1)}, f32[8,1,512]{2,1,0:T(1,128)S(1)}) custom-call(bf16[8,512,128]{2,1,0:T(8,128)(2,1)S(1)} %get-tuple-element.20.q_ref, bf16[8,1024,128]{2,1,0:T(8,128)(2,1)S(1)} %copy-done.4, bf16[8,1024,128]{2,1,0:T(8,128)(2,1)} %get-tuple-element.22.v_ref), custom_call_target="tpu_custom_call" | custom-call | flops 9663676416 | bytes 6291456 | tf_op jit(solution)/shard_map/pallas_call | solution.py:382
  158.1 19.1 %shard_map.162 = bf16[16,256,128]{2,1,0:T(8,128)(2,1)} custom-call(bf16[8,512,128]{2,1,0:T(8,128)(2,1)S(1)} %get-tuple-element.23.o_in.o_ref), custom_call_target="tpu_custom_call" | custom-call | tf_op jit(solution)/shard_map/pallas_call | solution.py:394
  177.6 5.3 multiply_reduce_fusion
  187.2 6.1 fusion.59.g_in
  193.3 23.2 %shard_map.163.do_ref = bf16[8,512,128]{2,1,0:T(8,128)(2,1)S(1)} custom-call(bf16[16,256,128]{2,1,0:T(8,128)(2,1)S(1)} %fusion.59.g_in), custom_call_target="tpu_custom_call" | custom-call | tf_op jit(solution)/shard_map/pallas_call | solution.py:413
  220.3 58.5 %shard_map.164 = (f32[8,512,128]{2,1,0:T(8,128)S(1)}, f32[8,1024,128]{2,1,0:T(8,128)}, f32[8,1024,128]{2,1,0:T(8,128)}) custom-call(bf16[8,512,128]{2,1,0:T(8,128)(2,1)S(1)} %copy-done.6, bf16[8,1024,128]{2,1,0:T(8,128)(2,1)} %get-tuple-element.21.k_ref, bf16[8,1024,128]{2,1,0:T(8,128)(2,1)} %get-tuple-element.22.v_ref, ...), custom_call_target="tpu_custom_call" | custom-call | flops 24159191040 | bytes 16777216 | tf_op jit(solution)/shard_map/pallas_call | solution.py:426
  280.1 64.4 %shard_map.165 = (f32[4,2,512,128]{3,2,1,0:T(8,128)S(1)}, f32[4,1024,128]{2,1,0:T(8,128)S(1)}, bf16[4,1024,128]{2,1,0:T(8,128)(2,1)S(1)}) custom-call(f32[8,512,128]{2,1,0:T(8,128)} %copy-done.1, f32[8,1024,128]{2,1,0:T(8,128)} %get-tuple-element.26.dk_in, f32[8,1024,128]{2,1,0:T(8,128)} %get-tuple-element.27.dv_in), custom_call_target="tpu_custom_call" | custom-call | tf_op jit(solution)/shard_map/pallas_call | solution.py:439
  352.0 10.0 %psum.64 = f32[2,1024]{1,0:T(2,128)S(1)} all-reduce(f32[2,1024]{1,0:T(2,128)S(1)} %pad_maximum_fusion.5), channel_id=1, replica_groups=mesh['dp'=1,'tp'=4,'cp'=8] {'tp'}, use_global_device_ids=true, to_apply=%region_7.0 | all-reduce | flops 2048 | bytes 16384 | tf_op jit(solution)/shard_map/psum | solution.py:458
  373.5 5.8 bitcast_add_fusion
  380.4 7.0 fusion.12
  396.3 6.9 convolution_bitcast_fusion
  403.4 53.7 %reduce-scatter.2.cloned.1.call-done = f32[256,2048]{1,0:T(8,128)} async-done(((f32[1024,2048]{1,0:T(8,128)}), f32[256,2048]{1,0:T(8,128)}) %reduce-scatter.2.cloned.1.call-update) | async-done | bytes 2097168 | tf_op jit(solution)/shard_map/reduce_scatter | solution.py:467
  460.3 13.3 %all-reduce = (f32[4,128]{1,0:T(4,128)}, f32[4,128]{1,0:T(4,128)}) all-reduce(f32[4,128]{1,0:T(4,128)S(1)} %get-tuple-element.60, f32[4,128]{1,0:T(4,128)S(1)} %get-tuple-element.58), channel_id=1, replica_groups=mesh['dp'=1,'tp'=4,'cp'=8] {'cp'}, use_global_device_ids=true, to_apply=%region_14.0 | all-reduce | flops 1024 | bytes 8192 | tf_op jit(solution)/shard_map/psum | solution.py:470
  473.6 46.1 %psum.71 = f32[2048]{0:T(1024)} all-reduce(f32[2048]{0:T(1024)S(1)} %get-tuple-element.62), channel_id=1, replica_groups=mesh['dp'=1,'tp'=4,'cp'=8] {'tp','cp'}, use_global_device_ids=true, to_apply=%region_18.0 | all-reduce | flops 2048 | bytes 16384 | tf_op jit(solution)/shard_map/psum | solution.py:469
  519.6 165.8 %all-reduce.4.cloned.1.call-done = (f32[2048,4,128]{0,2,1:T(8,128)}, f32[2048,4,128]{0,2,1:T(8,128)}, f32[2048,4,128]{0,2,1:T(8,128)}, f32[4,128,2048]{2,1,0:T(8,128)}) async-done(((f32[2048,4,128]{0,2,1:T(8,128)}, f32[2048,4,128]{0,2,1:T(8,128)}, f32[2048,4,128]{0,2,1:T(8,128)}, f32[4,128,2048]{2,1,0:T(8,128)}), (f32[2048,4,128]{0,2,1:T(8,128)}, f32[2048,4,128]{0,2,1:T(8,128)}, f32[2048,4,128]{0,2,1:T(8,128)}, ...) | async-done | bytes 16777232 | tf_op jit(solution)/shard_map/psum | solution.py:470
  685.4 5.2 copy.62
  690.7 5.2 copy.63
  695.9 5.2 copy.64
  701.1 32.4 %all-gather.11.cloned.1.call-done = bf16[1024,2048]{1,0:T(8,128)(2,1)} async-done(((bf16[256,2048]{1,0:T(8,128)(2,1)}), bf16[1024,2048]{1,0:T(8,128)(2,1)}) %all-gather.11.cloned.1.call-update) | async-done | bytes 4194320 | tf_op jit(solution)/shard_map/all_gather | solution.py:468
  733.5 4.9 copy.97
  (117 shorter events, 67.7 us)
Async XLA Ops:
  7.2 41.3 %copy-start = (bf16[2048,4,128]{2,1,0:T(4,128)(2,1)S(1)}, bf16[2048,4,128]{2,1,0:T(4,128)(2,1)}, u32[]{:S(2)}) copy-start(bf16[2048,4,128]{2,1,0:T(4,128)(2,1)} %param.12) | copy-start | bytes 6291460
  7.2 170.4 %all-gather.7.cloned.1.call-start = ((), (), s32[]{:S(2)}) async-start(), calls=%async_computation.1 | async-start | bytes 10485760 | tf_op jit(solution)/shard_map/all_gather | solution.py:355
  8.0 388.3 %all-gather.15.cloned.1.call-start = ((), (), s32[]{:S(2)}) async-start(), calls=%async_computation.6 | async-start | bytes 5242880 | tf_op jit(solution)/shard_map/all_gather | solution.py:423
  24.0 19.0 %copy-start.28 = (f32[4,128]{1,0:T(4,128)S(1)}, f32[4,128]{1,0:T(4,128)}, u32[]{:S(2)}) copy-start(f32[4,128]{1,0:T(4,128)} %param.14) | copy-start | bytes 6148
  24.0 19.0 %copy-start.29 = (f32[4,128]{1,0:T(4,128)S(1)}, f32[4,128]{1,0:T(4,128)}, u32[]{:S(2)}) copy-start(f32[4,128]{1,0:T(4,128)} %param.15) | copy-start | bytes 6148
  43.0 2.9 copy-start.21
  95.2 62.9 %copy-start.5 = (bf16[8,512,128]{2,1,0:T(8,128)(2,1)}, bf16[8,512,128]{2,1,0:T(8,128)(2,1)S(1)}, u32[]{:S(2)}) copy-start(bf16[8,512,128]{2,1,0:T(8,128)(2,1)S(1)} %get-tuple-element.20.q_ref) | copy-start | bytes 3145732
  177.3 219.0 %all-gather.13.cloned.1.call-start = ((), (), s32[]{:S(2)}) async-start(), calls=%async_computation.5 | async-start | bytes 5242880 | tf_op jit(solution)/shard_map/all_gather | solution.py:422
  177.6 5.4 copy-start.27
  177.6 5.4 copy-start.25
  217.6 239.5 %reduce-scatter.2.cloned.1.call-start = ((), (), s32[]{:S(2)}) async-start(), calls=%async_computation.3 | async-start | bytes 10485760 | tf_op jit(solution)/shard_map/reduce_scatter | solution.py:467
  347.8 2.8 copy-start.14
  347.8 4.1 copy-start.17
  347.9 3.2 copy-start.9
  362.0 3.6 copy-start.10
  362.0 4.1 copy-start.13
  362.1 5.1 copy-start.15
  379.3 140.3 %all-gather.9.cloned.1.call-start = ((), (), s32[]{:S(2)}) async-start(), calls=%async_computation.2 | async-start | bytes 5242880 | tf_op jit(solution)/shard_map/all_gather | solution.py:421
  380.0 305.5 %all-reduce.4.cloned.1.call-start = ((), (), s32[]{:S(2)}) async-start(), calls=%async_computation.7 | async-start | bytes 33554432 | tf_op jit(solution)/shard_map/psum | solution.py:470
  380.3 7.1 copy-start.8
  380.3 7.1 copy-start.20
  403.3 330.2 %all-gather.11.cloned.1.call-start = ((), (), s32[]{:S(2)}) async-start(), calls=%async_computation.4 | async-start | bytes 5242880 | tf_op jit(solution)/shard_map/all_gather | solution.py:468
  733.5 4.9 copy-start.24
  738.4 3.7 copy-start.23
  (15 other events, 25.5 us)
Sparse Core Ops, SparseCore 0:
  9.6 84.8 all-gather.6
  177.4 57.7 all-gather.14
  236.8 46.0 all-gather.12
  379.4 77.5 reduce-scatter.1
  458.5 46.1 all-gather.8
  507.8 177.6 all-reduce.3
  687.6 45.8 all-gather.10

commit v2 on v1

--- a/solution.py
+++ b/solution.py
@@ -115,41 +115,71 @@
         copy.wait()
 
 
-def attend(sub, scale, q_ref, k_ref, v_ref, o_ref, lse_ref, vt_scr, m_scr, l_scr, acc_scr):
+def attend(sub, scale, q_ref, k_ref, v_ref, o_ref, lse_ref, vt_scr, m_scr, l_scr, acc_scr, s_a, s_b, mx_a):
     blk = pl.program_id(0)
     core = lax.rem(lax.axis_index("cp"), 2)
     coef = scale * LOG2E
-    block_len = k_ref.shape[1]
+    half = k_ref.shape[1] // 2
+    cols = q_ref.shape[1]
+    chunk = half // 2
     vt_scr[blk] = v_ref[blk].T
     m_scr[...] = jnp.full_like(m_scr, -jnp.inf)
     l_scr[...] = jnp.zeros_like(l_scr)
     acc_scr[...] = jnp.zeros_like(acc_scr)
 
-    def step(b, masked):
-        k_blk = k_ref[b]
-        vt_blk = vt_scr[b]
-        for part in range(2):
-            cols = slice(part * sub, (part + 1) * sub)
-            s = lax.dot_general(k_blk, q_ref[0, cols, :], NT, preferred_element_type=jnp.float32)
-            if masked:
-                first = (core if part == 0 else 3 - core) * sub
-                kv_pos = lax.broadcasted_iota(jnp.int32, (block_len, sub), 0)
-                q_pos = first + lax.broadcasted_iota(jnp.int32, (block_len, sub), 1)
-                s = jnp.where(kv_pos <= q_pos, s, -jnp.inf)
-            m_old = m_scr[:, cols]
-            m_new = jnp.maximum(m_old, jnp.max(s, axis=0, keepdims=True))
-            p = jnp.exp2(s * coef - m_new * coef)
-            alpha = jnp.exp2((m_old - m_new) * coef)
-            l_scr[:, cols] = l_scr[:, cols] * alpha + jnp.sum(p, axis=0, keepdims=True)
-            acc_scr[:, cols] = acc_scr[:, cols] * alpha + jnp.dot(vt_blk, p.astype(jnp.bfloat16), preferred_element_type=jnp.float32)
-            m_scr[:, cols] = m_new
+    def fold(op, values):
+        return op(values.reshape(values.shape[0] // 8, 8, cols), axis=0)
+
+    def scores(b, h, c):
+        kv = slice(h * half + c * chunk, h * half + (c + 1) * chunk)
+        return lax.dot_general(k_ref[b, kv, :], q_ref[0], NT, preferred_element_type=jnp.float32)
+
+    def mask(s, h, c):
+        kv_pos = h * half + c * chunk + lax.broadcasted_iota(jnp.int32, s.shape, 0)
+        col = lax.broadcasted_iota(jnp.int32, s.shape, 1)
+        q_pos = jnp.where(col < sub, core * sub + col, (2 - core) * sub + col)
+        return jnp.where(kv_pos <= q_pos, s, -jnp.inf)
+
+    def step(buf, mx, b, h, nxt):
+        m_old = m_scr[...]
+        m_new = jnp.maximum(m_old, mx)
+        mc = m_new * coef
+        alpha = jnp.exp2((m_old - m_new) * coef)
+        lsum = jnp.zeros((8, cols), jnp.float32)
+        new_mx = None
+        for c in range(2):
+            rows = slice(c * chunk, (c + 1) * chunk)
+            if nxt is not None:
+                nbuf, nb, nh, masked = nxt
+                s = scores(nb, nh, c)
+                if masked:
+                    s = mask(s, nh, c)
+                nbuf[rows, :] = s
+                part = fold(jnp.max, s)
+                new_mx = part if new_mx is None else jnp.maximum(new_mx, part)
+            p = jnp.exp2(buf[rows, :] * coef - mc)
+            lsum = lsum + fold(jnp.sum, p)
+            pv = jnp.dot(vt_scr[b, :, h * half + c * chunk : h * half + (c + 1) * chunk], p.astype(jnp.bfloat16), preferred_element_type=jnp.float32)
+            acc_scr[...] = acc_scr[...] * alpha + pv if c == 0 else acc_scr[...] + pv
+        l_scr[...] = l_scr[...] * alpha + jnp.sum(lsum, axis=0, keepdims=True)
+        m_scr[...] = m_new
+        return None if nxt is None else jnp.max(new_mx, axis=0, keepdims=True)
+
+    for c in range(2):
+        s_a[c * chunk : (c + 1) * chunk, :] = scores(0, 0, c)
+    mx_a[...] = jnp.max(s_a[...], axis=0, keepdims=True)
 
     def body(b, carry):
-        step(b, False)
+        mx_b = step(s_a, mx_a[...], b, 0, (s_b, b, 1, False))
+        mx_a[...] = step(s_b, mx_b, b, 1, (s_a, b + 1, 0, False))
         return carry
 
     lax.fori_loop(0, blk, body, 0)
-    step(blk, True)
+    for c in range(2):
+        rows = slice(c * chunk, (c + 1) * chunk)
+        s_a[rows, :] = mask(s_a[rows, :], 0, c)
+    mx_b = step(s_a, jnp.max(s_a[...], axis=0, keepdims=True), blk, 0, (s_b, blk, 1, True))
+    step(s_b, mx_b, blk, 1, None)
     o_ref[0] = (acc_scr[...] / l_scr[...]).T.astype(o_ref.dtype)
     lse_ref[0] = m_scr[...] * coef + jnp.log2(l_scr[...])
 
@@ -327,6 +357,204 @@
         remote(sv.at[0], dv_out.at[src], vs.at[r], vr.at[r], partner).wait_recv()
 
 
+def sum_tp(tp_size, vec, out, got, ss, rs):
+    me = lax.axis_index("tp")
+    barrier = pltpu.get_barrier_semaphore()
+    for r in range(1, tp_size):
+        pl.semaphore_signal(barrier, inc=1, device_id={"tp": lax.rem(me + r, tp_size)}, device_id_type=MESH)
+    pl.semaphore_wait(barrier, tp_size - 1)
+    copies = []
+    for r in range(1, tp_size):
+        copy = remote(vec, got.at[r], ss.at[r], rs.at[r], {"tp": lax.rem(me + r, tp_size)})
+        copy.start()
+        copies.append(copy)
+    for copy in copies:
+        copy.wait()
+    out[...] = (vec[...] + got[2]) + (got[1] + got[3])
+
+
+def reduce_tail(tp_size, cp_size, n_heads, *refs):
+    n_w = 4
+    w_in, (dx_in, dy_in, small) = refs[:n_w], refs[n_w : n_w + 3]
+    refs = refs[n_w + 3 :]
+    w_out, (dx_out, small_out) = refs[:n_w], refs[n_w : n_w + 2]
+    refs = refs[n_w + 2 :]
+    acc, pair, far_a, far_b, fin_l, fin_r = (refs[i * n_w : (i + 1) * n_w] for i in range(6))
+    refs = refs[6 * n_w :]
+    dxa, dxb, dx_own, dx_fa, dx_fb, dx_fl, dx_fr, dx16, got_small, got_post, ss, rs, ps, pr, fs, fr, loc, sms, smr, gps, gpr = refs
+    me_tp = lax.axis_index("tp")
+    me_cp = lax.axis_index("cp")
+    core = lax.rem(me_cp, 2)
+    chip = me_cp // 2
+    ring = cp_size // 2
+    left, right, far = (lax.rem(chip + d, ring) for d in (ring - 1, 1, 2))
+    t_left, t_right, t_far = (lax.rem(me_tp + d, tp_size) for d in (tp_size - 1, 1, 2))
+    partner = {"cp": me_cp + 1 - 2 * core}
+    to_l, to_r = {"cp": left * 2 + core}, {"cp": right * 2 + core}
+    tp_l, tp_r = {"tp": t_left}, {"tp": t_right}
+    dx_i = n_w
+
+    barrier = pltpu.get_barrier_semaphore()
+    for r in range(1, cp_size):
+        pl.semaphore_signal(barrier, inc=1, device_id={"cp": lax.rem(me_cp + r, cp_size)}, device_id_type=MESH)
+    for r in range(1, tp_size):
+        pl.semaphore_signal(barrier, inc=1, device_id={"tp": lax.rem(me_tp + r, tp_size)}, device_id_type=MESH)
+    pl.semaphore_wait(barrier, cp_size + tp_size - 2)
+
+    sent = []
+
+    def go(src, dst, s_sem, r_sem, device):
+        copy = remote(src, dst, s_sem, r_sem, device)
+        copy.start()
+        sent.append(copy)
+
+    def landed(dst, s_sem, r_sem):
+        remote(dst, dst, s_sem, r_sem, partner).wait_recv()
+
+    def piece(ref, t, x, c, part=None):
+        size = w_in[t].shape[0] // cp_size
+        first = (2 * x + c) * size
+        if part is None:
+            return ref.at[pl.ds(pl.multiple_of(first, size), size), :]
+        return ref.at[pl.ds(pl.multiple_of(first + part * (size // 2), size // 2), size // 2), :]
+
+    def rows_of(ref, y, part=None):
+        size = dx_in.shape[0] // tp_size
+        if part is None:
+            return ref.at[pl.ds(pl.multiple_of(y * size, size), size), :]
+        return ref.at[pl.ds(pl.multiple_of(y * size + part * (size // 2), size // 2), size // 2), :]
+
+    def half_of(ref, part):
+        size = ref.shape[0] // 2
+        return ref.at[pl.ds(part * size, size), :]
+
+    for r in range(1, cp_size):
+        go(small, got_small.at[me_cp], sms.at[r], smr.at[r], {"cp": lax.rem(me_cp + r, cp_size)})
+    go(rows_of(dx_in, t_far, 0), dx_fa, ss.at[dx_i, 0], rs.at[dx_i, 0], tp_l)
+    go(rows_of(dx_in, t_far, 1), dx_fb, ss.at[dx_i, 1], rs.at[dx_i, 1], tp_r)
+    go(rows_of(dx_in, t_left, 1), half_of(dx_fr, 1), ss.at[dx_i, 2], rs.at[dx_i, 2], tp_l)
+    go(rows_of(dx_in, t_right, 0), half_of(dx_fl, 0), ss.at[dx_i, 3], rs.at[dx_i, 3], tp_r)
+    order = (far, left, right, chip)
+    loads = []
+    for t in range(n_w):
+        for i, x in enumerate(order):
+            go(piece(w_in[t], t, x, 1 - core), pair[t].at[x], ps.at[t, i], pr.at[t, i], partner)
+            copy = pltpu.make_async_copy(piece(w_in[t], t, x, core), acc[t].at[x], loc.at[t, i])
+            copy.start()
+            loads.append(copy)
+    dx_loads = [
+        pltpu.make_async_copy(rows_of(dx_in, t_left, 0), dxa, loc.at[n_w, 0]),
+        pltpu.make_async_copy(rows_of(dx_in, t_right, 1), dxb, loc.at[n_w, 1]),
+        pltpu.make_async_copy(rows_of(dx_in, me_tp), dx_own, loc.at[n_w, 2]),
+    ]
+    for copy in dx_loads:
+        copy.start()
+
+    for t in range(n_w):
+        for i, x in enumerate(order):
+            loads[t * 4 + i].wait()
+            landed(pair[t].at[x], ps.at[t, i], pr.at[t, i])
+            acc[t][x] += pair[t][x]
+        go(half_of(acc[t].at[far], 0), far_a[t], ss.at[t, 0], rs.at[t, 0], to_l)
+        go(half_of(acc[t].at[far], 1), far_b[t], ss.at[t, 1], rs.at[t, 1], to_r)
+        go(half_of(acc[t].at[left], 1), half_of(fin_r[t], 1), ss.at[t, 2], rs.at[t, 2], to_l)
+        go(half_of(acc[t].at[right], 0), half_of(fin_l[t], 0), ss.at[t, 3], rs.at[t, 3], to_r)
+
+    got_small[me_cp] = small[...]
+    for r in range(1, cp_size):
+        landed(got_small.at[lax.rem(me_cp - r + cp_size, cp_size)], sms.at[r], smr.at[r])
+    total = got_small[0]
+    for i in range(1, cp_size):
+        total = total + got_small[i]
+    small_out[...] = total
+    n_gain = small.shape[0] - got_post.shape[1]
+
+    def second_half(t, acc_l, acc_r, fa, fb, fl, fr, dev_l, dev_r):
+        half = fa.shape[0]
+        landed(fa, ss.at[t, 0], rs.at[t, 0])
+        acc_l[...] += fa[...]
+        landed(fb, ss.at[t, 1], rs.at[t, 1])
+        acc_r[...] += fb[...]
+        go(acc_l, half_of(fr, 0), ss.at[t, 4], rs.at[t, 4], dev_l)
+        go(acc_r, half_of(fl, 1), ss.at[t, 5], rs.at[t, 5], dev_r)
+
+    def all_landed(t, fl, fr):
+        landed(half_of(fr, 1), ss.at[t, 2], rs.at[t, 2])
+        landed(half_of(fl, 0), ss.at[t, 3], rs.at[t, 3])
+        landed(half_of(fr, 0), ss.at[t, 4], rs.at[t, 4])
+        landed(half_of(fl, 1), ss.at[t, 5], rs.at[t, 5])
+
+    for t in range(n_w):
+        second_half(t, half_of(acc[t].at[left], 0), half_of(acc[t].at[right], 1), far_a[t], far_b[t], fin_l[t], fin_r[t], to_l, to_r)
+    for copy in dx_loads:
+        copy.wait()
+    second_half(dx_i, dxa, dxb, dx_fa, dx_fb, dx_fl, dx_fr, tp_l, tp_r)
+    post = small_out.at[pl.ds(n_gain, got_post.shape[1]), :]
+    for r in range(1, tp_size):
+        go(post, got_post.at[r], gps.at[r], gpr.at[r], {"tp": lax.rem(me_tp + r, tp_size)})
+
+    outs = []
+    for t in range(n_w):
+        all_landed(t, fin_l[t], fin_r[t])
+        acc[t][chip] = acc[t][chip] + (fin_l[t][...] + fin_r[t][...])
+        src = acc[t].at[chip]
+        dst = piece(w_out[t], t, chip, core)
+        copy = pltpu.make_async_copy(src, dst, loc.at[t, 4])
+        copy.start()
+        outs.append(copy)
+        go(src, dst, ss.at[t, 6], rs.at[t, 6], to_l)
+        go(src, dst, ss.at[t, 7], rs.at[t, 7], to_r)
+        go(src, dst, fs.at[t, 0], fr.at[t, 0], partner)
+    all_landed(dx_i, dx_fl, dx_fr)
+    dx16[...] = (dx_own[...] + (dx_fl[...] + dx_fr[...]) + dy_in[...].astype(jnp.float32)).astype(dx16.dtype)
+    copy = pltpu.make_async_copy(dx16, rows_of(dx_out, me_tp), loc.at[n_w, 4])
+    copy.start()
+    outs.append(copy)
+    go(dx16, rows_of(dx_out, me_tp), ss.at[dx_i, 6], rs.at[dx_i, 6], tp_l)
+    go(dx16, rows_of(dx_out, me_tp), ss.at[dx_i, 7], rs.at[dx_i, 7], tp_r)
+
+    for t in range(n_w):
+        landed(piece(w_out[t], t, right, core), ss.at[t, 6], rs.at[t, 6])
+        half = piece(w_out[t], t, right, core, 0)
+        go(half, half, ss.at[t, 8], rs.at[t, 8], to_l)
+        whole = piece(w_out[t], t, right, core)
+        go(whole, whole, fs.at[t, 1], fr.at[t, 1], partner)
+        landed(piece(w_out[t], t, left, core), ss.at[t, 7], rs.at[t, 7])
+        half = piece(w_out[t], t, left, core, 1)
+        go(half, half, ss.at[t, 9], rs.at[t, 9], to_r)
+        whole = piece(w_out[t], t, left, core)
+        go(whole, whole, fs.at[t, 2], fr.at[t, 2], partner)
+    landed(rows_of(dx_out, t_right), ss.at[dx_i, 6], rs.at[dx_i, 6])
+    half = rows_of(dx_out, t_right, 0)
+    go(half, half, ss.at[dx_i, 8], rs.at[dx_i, 8], tp_l)
+    landed(rows_of(dx_out, t_left), ss.at[dx_i, 7], rs.at[dx_i, 7])
+    half = rows_of(dx_out, t_left, 1)
+    go(half, half, ss.at[dx_i, 9], rs.at[dx_i, 9], tp_r)
+
+    sums = small_out[n_gain:, :]
+    for r in range(1, tp_size):
+        landed(got_post.at[r], gps.at[r], gpr.at[r])
+    sums = (sums + got_post[2]) + (got_post[1] + got_post[3])
+
+    for t in range(n_w):
+        for kind, part in ((8, 0), (9, 1)):
+            half = piece(w_out[t], t, far, core, part)
+            landed(half, ss.at[t, kind], rs.at[t, kind])
+            go(half, half, fs.at[t, 3 + part], fr.at[t, 3 + part], partner)
+    for kind, part in ((8, 0), (9, 1)):
+        landed(rows_of(dx_out, t_far, part), ss.at[dx_i, kind], rs.at[dx_i, kind])
+    for t in range(n_w):
+        for i, x in enumerate((chip, right, left)):
+            landed(piece(w_out[t], t, x, 1 - core), fs.at[t, i], fr.at[t, i])
+        for part in range(2):
+            landed(piece(w_out[t], t, far, 1 - core, part), fs.at[t, 3 + part], fr.at[t, 3 + part])
+    for copy in outs:
+        copy.wait()
+    for copy in sent:
+        copy.wait_send()
+    small_out[n_gain:, :] = sums
+
+
 def solution(mesh):
     tp_size = mesh.shape["tp"]
     cp_size = mesh.shape["cp"]
@@ -357,7 +585,18 @@
         q_lin = jnp.einsum("ld,dhe->hle", x_loc, w_q, preferred_element_type=f32)
         k_lin = jnp.einsum("ld,dhe->hle", x_loc, w_k, preferred_element_type=f32)
         v_lin = jnp.einsum("ld,dhe->hle", x_loc, w_v, preferred_element_type=f32)
-        sq = lax.psum(jnp.stack([jnp.sum(q_lin * q_lin, axis=(0, 2)), jnp.sum(k_lin * k_lin, axis=(0, 2))]), "tp")
+        def tp_sum(q_part, k_part, cid):
+            vec = jnp.stack([q_part, k_part]).reshape(-1, 128)
+            out = vmem_call(
+                functools.partial(sum_tp, tp_size),
+                [jax.ShapeDtypeStruct(vec.shape, f32)],
+                1,
+                [VMEM((tp_size,) + vec.shape, f32), dma((tp_size,)), dma((tp_size,))],
+                collective_id=cid,
+            )(vec)[0]
+            return out.reshape(2, -1)
+
+        sq = tp_sum(jnp.sum(q_lin * q_lin, axis=(0, 2)), jnp.sum(k_lin * k_lin, axis=(0, 2)), 4)
         inv = lax.rsqrt(sq / width + NORM_EPS)
         q_inv = inv[0][None, :, None]
         k_inv = inv[1][None, :, None]
@@ -385,7 +624,8 @@
             in_specs=[qspec, whole, whole],
             out_specs=[qspec, lspec],
             out_shape=[jax.ShapeDtypeStruct((cp_size, rows, head_dim), b16), jax.ShapeDtypeStruct((cp_size, 1, rows), f32)],
-            scratch_shapes=[VMEM((cp_size, head_dim, block_len), b16), VMEM((1, rows), f32), VMEM((1, rows), f32), VMEM((head_dim, rows), f32)],
+            scratch_shapes=[VMEM((cp_size, head_dim, block_len), b16), VMEM((1, rows), f32), VMEM((1, rows), f32), VMEM((head_dim, rows), f32)]
+            + [VMEM((block_len // 2, rows), f32)] * 2 + [VMEM((1, rows), f32)],
             compiler_params=pltpu.CompilerParams(vmem_limit_bytes=48 << 20),
             cost_estimate=pl.CostEstimate(flops=2 * pair_flops, bytes_accessed=6 << 20, transcendentals=0),
         )(q_all, k_all, v_all)
@@ -455,7 +695,7 @@
         grad_kn = jnp.sum(dk_s * k_hat, axis=1)
         dq_n = dq_s * q_norm_w[:, None, :]
         dk_n = dk_s * k_norm_w[:, None, :]
-        dots = lax.psum(jnp.stack([jnp.sum(dq_n * q_hat, axis=(0, 2)), jnp.sum(dk_n * k_hat, axis=(0, 2))]), "tp") / width
+        dots = tp_sum(jnp.sum(dq_n * q_hat, axis=(0, 2)), jnp.sum(dk_n * k_hat, axis=(0, 2)), 5) / width
         dq16 = (q_inv * (dq_n - q_hat * dots[0][None, :, None])).astype(b16)
         dk16 = (k_inv * (dk_n - k_hat * dots[1][None, :, None])).astype(b16)
         grad_w_q = jnp.einsum("ld,hle->dhe", x_loc, dq16, preferred_element_type=f32)
@@ -464,10 +704,30 @@
         dx_part = (jnp.einsum("hle,dhe->ld", dq16, w_q, preferred_element_type=f32)
                    + jnp.einsum("hle,dhe->ld", dk16, w_k, preferred_element_type=f32)
                    + jnp.einsum("hle,dhe->ld", dv_home, w_v, preferred_element_type=f32))
-        dx_rows = lax.psum_scatter(dx_part, "tp", scatter_dimension=0, tiled=True)
-        grad_x = lax.all_gather((dy_rows + dx_rows).astype(b16), "tp", axis=0, tiled=True)
-        grad_post = lax.psum(grad_post, ("tp", "cp"))
-        weight_grads = lax.psum((grad_w_q, grad_w_k, grad_w_v, grad_w_o, grad_qn, grad_kn), "cp")
-        return (y_out[None], grad_x[None]) + tuple(weight_grads) + (grad_post,)
+        w_parts = [grad_w_o.reshape(-1, d_model)] + [g.reshape(d_model, -1) for g in (grad_w_v, grad_w_q, grad_w_k)]
+        small = jnp.concatenate([grad_qn, grad_kn, grad_post.reshape(-1, head_dim)], axis=0)
+        any_spec = pl.BlockSpec(memory_space=pl.ANY)
+        vmem_spec = pl.BlockSpec(memory_space=VMEM)
+
+        def bufs(lead, div):
+            return [VMEM(lead + (w.shape[0] // div, w.shape[1]), f32) for w in w_parts]
+
+        ring = cp_size // 2
+        rows_dx, half_dx = VMEM((sub, d_model), f32), VMEM((sub // 2, d_model), f32)
+        res = pl.pallas_call(
+            functools.partial(reduce_tail, tp_size, cp_size, heads),
+            out_shape=[jax.ShapeDtypeStruct(w.shape, f32) for w in w_parts] + [jax.ShapeDtypeStruct((block_len, d_model), b16), jax.ShapeDtypeStruct(small.shape, f32)],
+            in_specs=[any_spec] * 5 + [vmem_spec] * 2,
+            out_specs=[any_spec] * 5 + [vmem_spec],
+            scratch_shapes=bufs((ring,), cp_size) * 2 + bufs((), 2 * cp_size) * 2 + bufs((), cp_size) * 2
+            + [half_dx, half_dx, rows_dx, half_dx, half_dx, rows_dx, rows_dx, VMEM((sub, d_model), b16)]
+            + [VMEM((cp_size,) + small.shape, f32), VMEM((tp_size, d_model // head_dim, head_dim), f32)]
+            + [dma((5, 10))] * 2 + [dma((4, 4))] * 2 + [dma((4, 5))] * 2 + [dma((5, 5))] + [dma((cp_size,))] * 2 + [dma((tp_size,))] * 2,
+            compiler_params=pltpu.CompilerParams(vmem_limit_bytes=56 << 20, collective_id=6, has_side_effects=True),
+        )(*w_parts, dx_part, dy_rows.astype(b16), small)
+        grad_w_o, grad_w_v, grad_w_q, grad_w_k = (g.reshape(t.shape) for g, t in zip(res[:4], (grad_w_o, grad_w_v, grad_w_q, grad_w_k)))
+        grad_x, small_sum = res[4:]
+        grad_qn, grad_kn = small_sum[:heads], small_sum[heads : 2 * heads]
+        return (y_out[None], grad_x[None], grad_w_q, grad_w_k, grad_w_v, grad_w_o, grad_qn, grad_kn, small_sum[2 * heads :].reshape(-1))
 
     return jax.shard_map(local_run, mesh=mesh, in_specs=in_specs, out_specs=out_specs, check_vma=False)

time: 757 us -> 616 us (0.81)
  waiting for transfers between devices: 254 us -> 36.9 us
  Pallas kernels: 270 us -> 407 us
  blocking collectives: 82.4 us -> 0 us
  local copies, waits for them, and re-layouts: 45.2 us -> 64.4 us
    psum x1 -> x0, waiting for transfers between devices: 166 us -> none  [local_run(): lax.psum((grad_w_q, grad_w_k, grad_w_v, grad_w_o, grad_qn, grad_kn), 'cp')]
    pallas_call x0 -> x3, Pallas kernels: none -> 164 us  [the longest x1 151 us: local_run(): pl.pallas_call(functools.partial(reduce_tail, tp_size, cp_size, heads), o...]
    psum x4 -> x0, blocking collectives: 82.4 us -> none  [the longest x1 46.1 us: local_run(): grad_post = lax.psum(grad_post, ('tp', 'cp'))]
    reduce_scatter x1 -> x0, waiting for transfers between devices: 53.7 us -> none  [local_run(): dx_rows = lax.psum_scatter(dx_part, 'tp', scatter_dimension=0, tiled=True)]
    all_gather x1, waiting for transfers between devices: 0.01 us -> 36 us  [local_run(): o_gath = lax.all_gather(o_rows, 'tp', axis=0)]
    all_gather x1 -> x0, waiting for transfers between devices: 32.4 us -> none  [local_run(): lax.all_gather((dy_rows + dx_rows).astype(b16), 'tp', axis=0, tiled=True)]
    reshape x0 -> x9, local copies, waits for them, and re-layouts: none -> 32.3 us  [the longest x3 16 us: local_run(): g.reshape(d_model, -1)]
    pallas_call x1, Pallas kernels: 60.9 us -> 34.5 us  [local_run(): pl.pallas_call(functools.partial(attend, sub, scale), grid=(cp_size,), in...]
  transfers between devices with their start and end apart: 7 -> 4, of which waited for: 3 -> 1; matrix products, arithmetic and copies ran while one was open for 14% -> 22% of each run, Pallas kernels for 36% -> 67%
where the time goes in v2:
time: 616 us; the launch traced here: 610 us
  Pallas kernels  407 us (66%)
  local copies, waits for them, and re-layouts  64.4 us (10%)
  matrix products  59.1 us (10%)
  waiting for transfers between devices  36.9 us (6%)
  other arithmetic  28.2 us (5%)
  between operations  14.5 us (2%)
    pallas_call x1, Pallas kernels, local_run(): pl.pallas_call(functools.partial(reduce_tail, tp_size, cp_size, heads), o...  151 us
    pallas_call x1, Pallas kernels, local_run(): vmem_call(functools.partial(gather_grads, heads, cp_size), [jax.ShapeDtyp...  64.4 us
    pallas_call x1, Pallas kernels, local_run(): pl.pallas_call(functools.partial(attend_back, sub, scale), grid=(cp_size,...  58.7 us
    pallas_call x1, Pallas kernels, local_run(): vmem_call(functools.partial(scatter_qkv, heads, cp_size), [jax.ShapeDtype...  43.6 us
    all_gather x1, waiting for transfers between devices, local_run(): o_gath = lax.all_gather(o_rows, 'tp', axis=0)  36 us
    pallas_call x1, Pallas kernels, local_run(): pl.pallas_call(functools.partial(attend, sub, scale), grid=(cp_size,), in...  34.5 us
    pallas_call x1, Pallas kernels, local_run(): vmem_call(functools.partial(rows_to_heads, heads, tp_size, cp_size), [jax...  21.5 us
    unnamed x68, local copies, waits for them, and re-layouts  20.7 us
  transfers between devices with their start and end apart: 4, of which 1 were waited for; matrix products, arithmetic and copies ran while one was open for 22% of the time, Pallas kernels for 67%

profile of v2, /device:TPU:97, one launch (start us, length us, event | category | flops | bytes accessed | tf_op | source)
XLA Modules:
  0.0 610.5 jit_solution(17238658606304877990)
XLA Ops:
  8.1 6.7 %multiply_reduce_fusion.2 = (f32[1024]{0:T(1024)S(1)}, f32[4,128,1024]{2,1,0:T(8,128)}) fusion(bf16[1,1024,2048]{2,1,0:T(8,128)(2,1)} %param.9, bf16[2048,4,128]{2,1,0:T(4,128)(2,1)} %param.10), kind=kOutput, calls=%fused_computation.65 | convolution fusion | flops 2148531200 | bytes 8392704 | tf_op jit(solution)/shard_map/ld,dhe->hle/dot_general | solution.py:585
  18.6 7.6 %shard_map.160 = f32[16,128]{1,0:T(8,128)S(1)} custom-call(f32[16,128]{1,0:T(8,128)S(1)} %reshape.202.vec), custom_call_target="tpu_custom_call" | custom-call | tf_op jit(solution)/shard_map/pallas_call | solution.py:590
  44.4 43.6 %shard_map.161 = (bf16[8,512,128]{2,1,0:T(8,128)(2,1)S(1)}, bf16[8,1024,128]{2,1,0:T(8,128)(2,1)}, bf16[8,1024,128]{2,1,0:T(8,128)(2,1)}) custom-call(bf16[8,512,128]{2,1,0:T(8,128)(2,1)S(1)} %bitcast.125, bf16[4,1024,128]{2,1,0:T(8,128)(2,1)S(1)} %pad_maximum_fusion.3.k_in, bf16[4,1024,128]{2,1,0:T(8,128)(2,1)S(1)} %fusion.50.v_in), custom_call_target="tpu_custom_call" | custom-call | tf_op jit(solution)/shard_map/pallas_call | solution.py:609
  89.9 34.5 %shard_map.162 = (bf16[8,512,128]{2,1,0:T(8,128)(2,1)S(1)}, f32[8,1,512]{2,1,0:T(1,128)S(1)}) custom-call(bf16[8,512,128]{2,1,0:T(8,128)(2,1)S(1)} %get-tuple-element.26.q_ref, bf16[8,1024,128]{2,1,0:T(8,128)(2,1)S(1)} %copy-done.4, bf16[8,1024,128]{2,1,0:T(8,128)(2,1)} %get-tuple-element.28.v_ref), custom_call_target="tpu_custom_call" | custom-call | flops 9663676416 | bytes 6291456 | tf_op jit(solution)/shard_map/pallas_call | solution.py:621
  124.5 20.2 %shard_map.163 = bf16[16,256,128]{2,1,0:T(8,128)(2,1)} custom-call(bf16[8,512,128]{2,1,0:T(8,128)(2,1)S(1)} %get-tuple-element.29.o_in.o_ref), custom_call_target="tpu_custom_call" | custom-call | tf_op jit(solution)/shard_map/pallas_call | solution.py:634
  144.9 5.4 multiply_reduce_fusion
  156.3 36.0 %all-gather.12.cloned.1.call-done = bf16[64,256,128]{2,1,0:T(8,128)(2,1)} async-done(((bf16[16,256,128]{2,1,0:T(8,128)(2,1)}), bf16[64,256,128]{2,1,0:T(8,128)(2,1)}) %all-gather.12.cloned.1.call-update) | async-done | bytes 4194320 | tf_op jit(solution)/shard_map/all_gather | solution.py:663
  196.8 6.1 fusion.49.g_in
  202.9 21.5 %shard_map.164.do_ref = bf16[8,512,128]{2,1,0:T(8,128)(2,1)S(1)} custom-call(bf16[16,256,128]{2,1,0:T(8,128)(2,1)S(1)} %fusion.49.g_in), custom_call_target="tpu_custom_call" | custom-call | tf_op jit(solution)/shard_map/pallas_call | solution.py:653
  224.4 58.7 %shard_map.165 = (f32[8,512,128]{2,1,0:T(8,128)S(1)}, f32[8,1024,128]{2,1,0:T(8,128)}, f32[8,1024,128]{2,1,0:T(8,128)}) custom-call(bf16[8,512,128]{2,1,0:T(8,128)(2,1)S(1)} %copy-done.6, bf16[8,1024,128]{2,1,0:T(8,128)(2,1)} %get-tuple-element.27.k_ref, bf16[8,1024,128]{2,1,0:T(8,128)(2,1)} %get-tuple-element.28.v_ref, ...), custom_call_target="tpu_custom_call" | custom-call | flops 24159191040 | bytes 16777216 | tf_op jit(solution)/shard_map/pallas_call | solution.py:666
  284.5 64.4 %shard_map.166 = (f32[4,2,512,128]{3,2,1,0:T(8,128)S(1)}, f32[4,1024,128]{2,1,0:T(8,128)S(1)}, bf16[4,1024,128]{2,1,0:T(8,128)(2,1)S(1)}) custom-call(f32[8,512,128]{2,1,0:T(8,128)} %copy-done.3, f32[8,1024,128]{2,1,0:T(8,128)} %get-tuple-element.32.dk_in, f32[8,1024,128]{2,1,0:T(8,128)} %get-tuple-element.33.dv_in), custom_call_target="tpu_custom_call" | custom-call | tf_op jit(solution)/shard_map/pallas_call | solution.py:679
  359.9 6.0 shard_map.167
  374.4 5.3 copy.56.refs_3_
  383.8 4.5 fusion.2
  388.3 5.3 copy.55.refs_2_
  393.6 6.6 %fusion.4 = f32[4,128,2048]{2,1,0:T(8,128)} fusion(bf16[4,1024,128]{2,1,0:T(8,128)(2,1)S(1)} %get-tuple-element.34, bf16[1,1024,2048]{2,1,0:T(8,128)(2,1)} %param.9), kind=kOutput, calls=%fused_computation.6 | convolution fusion | flops 2147483648 | bytes 9437184 | tf_op jit(solution)/shard_map/ld,hle->dhe/dot_general | solution.py:703
  400.2 5.3 copy.54.refs_1_
  413.0 5.8 bitcast_add_fusion.refs_4_
  418.7 6.9 %convolution_bitcast_fusion.refs_0_ = f32[512,2048]{1,0:T(8,128)} fusion(bf16[512,256,4]{1,0,2:T(8,128)(2,1)} %bitcast.137, bf16[4,256,2048]{2,1,0:T(8,128)(2,1)} %bitcast.144), kind=kOutput, calls=%fused_computation.14 | convolution fusion | flops 2147483648 | bytes 9437184 | tf_op jit(solution)/shard_map/thle,tld->hed/dot_general | solution.py:677
  425.6 150.7 %shard_map.168 = (f32[512,2048]{1,0:T(8,128)}, f32[2048,512]{1,0:T(8,128)}, f32[2048,512]{1,0:T(8,128)}, f32[2048,512]{1,0:T(8,128)}, bf16[1024,2048]{1,0:T(8,128)(2,1)}, /*index=5*/f32[24,128]{1,0:T(8,128)}) custom-call(f32[512,2048]{1,0:T(8,128)} %convolution_bitcast_fusion.refs_0_, f32[2048,512]{1,0:T(8,128)} %copy.54.refs_1_, f32[2048,512]{1,0:T(8,128)} %copy.55.refs_2_, ...), custom_call_target="tpu_custom_call" | custom-call | tf_op jit(solution)/shard_map/pallas_call | solution.py:717
  576.3 5.2 reshape.212
  581.5 5.2 reshape.213
  586.7 5.2 reshape.214
  593.1 4.9 copy.81
  (116 shorter events, 74.5 us)
Async XLA Ops:
  7.2 33.8 %copy-start = (bf16[2048,4,128]{2,1,0:T(4,128)(2,1)S(1)}, bf16[2048,4,128]{2,1,0:T(4,128)(2,1)}, u32[]{:S(2)}) copy-start(bf16[2048,4,128]{2,1,0:T(4,128)(2,1)} %param.12) | copy-start | bytes 6291460
  7.2 137.6 %all-gather.6.cloned.1.call-start = ((), (), s32[]{:S(2)}) async-start(), calls=%async_computation | async-start | bytes 10485760 | tf_op jit(solution)/shard_map/all_gather | solution.py:583
  8.0 184.3 %all-gather.12.cloned.1.call-start = ((), (), s32[]{:S(2)}) async-start(), calls=%async_computation.3 | async-start | bytes 5242880 | tf_op jit(solution)/shard_map/all_gather | solution.py:663
  8.1 6.7 %copy-start.7 = (bf16[1,1024,2048]{2,1,0:T(8,128)(2,1)S(1)}, bf16[1,1024,2048]{2,1,0:T(8,128)(2,1)}, u32[]{:S(2)}) copy-start(bf16[1,1024,2048]{2,1,0:T(8,128)(2,1)} %param.9) | copy-start | bytes 12582916
  8.1 6.7 %copy-start.30 = (bf16[2048,4,128]{2,1,0:T(4,128)(2,1)S(1)}, bf16[2048,4,128]{2,1,0:T(4,128)(2,1)}, u32[]{:S(2)}) copy-start(bf16[2048,4,128]{2,1,0:T(4,128)(2,1)} %param.11) | copy-start | bytes 6291460
  29.5 5.9 copy-start.27
  29.5 5.9 copy-start.28
  88.0 36.5 %copy-start.5 = (bf16[8,512,128]{2,1,0:T(8,128)(2,1)}, bf16[8,512,128]{2,1,0:T(8,128)(2,1)S(1)}, u32[]{:S(2)}) copy-start(bf16[8,512,128]{2,1,0:T(8,128)(2,1)S(1)} %get-tuple-element.26.q_ref) | copy-start | bytes 3145732
  144.7 274.0 %all-gather.10.cloned.1.call-start = ((), (), s32[]{:S(2)}) async-start(), calls=%async_computation.2 | async-start | bytes 5242880 | tf_op jit(solution)/shard_map/all_gather | solution.py:662
  144.8 5.4 copy-start.26
  152.3 3.8 copy-start.17
  156.2 437.0 %all-gather.8.cloned.1.call-start = ((), (), s32[]{:S(2)}) async-start(), calls=%async_computation.1 | async-start | bytes 5242880 | tf_op jit(solution)/shard_map/all_gather | solution.py:661
  202.9 21.5 %copy-start.6 = (bf16[8,512,128]{2,1,0:T(8,128)(2,1)S(1)}, bf16[8,512,128]{2,1,0:T(8,128)(2,1)}, u32[]{:S(2)}) copy-start(bf16[8,512,128]{2,1,0:T(8,128)(2,1)} %copy-done.5) | copy-start | bytes 3145732
  355.8 4.1 copy-start.16
  355.8 3.2 copy-start.12
  365.9 4.1 copy-start.9
  369.9 4.5 copy-start.18
  379.7 4.1 copy-start.10
  383.8 4.5 copy-start.19
  406.1 4.4 copy-start.20
  406.1 4.4 copy-start.31
  586.7 5.2 copy-start.29
  593.1 4.9 copy-start.24
  598.1 3.7 copy-start.23
  (12 other events, 25.9 us)
Sparse Core Ops, SparseCore 0:
  9.6 84.6 all-gather.5
  144.9 47.3 all-gather.11
  193.9 55.9 all-gather.9
  351.3 47.1 all-gather.7

commit v3 on v2

v3 whole, which is shorter than its diff:
```python
import functools
import math

import jax
import jax.numpy as jnp
from jax import lax
from jax.experimental import pallas as pl
from jax.experimental.pallas import tpu as pltpu
from jax.sharding import PartitionSpec as P

ROPE_THETA = 500000.0
NORM_EPS = 1e-6
LOG2E = 1.4426950408889634
LIMIT = 56 << 20
LANES = 128
VMEM = pltpu.VMEM
MESH = pl.DeviceIdType.MESH
NT = (((1,), (1,)), ((), ()))


def rope_tables(start_pos, seq_rows, head_dim):
    half_dim = head_dim // 2
    lane = jnp.arange(head_dim)
    inv_freq = ROPE_THETA ** (-2.0 * (lane % half_dim).astype(jnp.float32) / head_dim)
    positions = (start_pos + jnp.arange(seq_rows)).astype(jnp.float32)
    angles = positions[:, None] * inv_freq[None, :]
    return jnp.cos(angles), jnp.where(lane < half_dim, -1.0, 1.0) * jnp.sin(angles)


def vmem_call(kernel, out_shape, n_in, scratch, collective_id=None, limit=LIMIT, cost=None):
    params = dict(vmem_limit_bytes=limit)
    if collective_id is not None:
        params.update(collective_id=collective_id, has_side_effects=True)
    return pl.pallas_call(
        kernel,
        out_shape=out_shape,
        in_specs=[pl.BlockSpec(memory_space=VMEM)] * n_in,
        out_specs=[pl.BlockSpec(memory_space=VMEM)] * len(out_shape),
        scratch_shapes=scratch,
        compiler_params=pltpu.CompilerParams(**params),
        cost_estimate=cost,
    )


def remote(src, dst, send_sem, recv_sem, device_id):
    return pltpu.make_async_remote_copy(src_ref=src, dst_ref=dst, send_sem=send_sem, recv_sem=recv_sem, device_id=device_id, device_id_type=MESH)


def cross_barrier(me_tp, me_cp, tp_size, cp_size):
    barrier = pltpu.get_barrier_semaphore()
    for axis, me, size in (("cp", me_cp, cp_size), ("tp", me_tp, tp_size)):
        for step in range(1, size):
            pl.semaphore_signal(barrier, inc=1, device_id={axis: lax.rem(me + step, size)}, device_id_type=MESH)
    pl.semaphore_wait(barrier, cp_size + tp_size - 2)


def cols(ref, head, rows=None):
    lanes = pl.ds(pl.multiple_of(head * LANES, LANES), LANES)
    return ref.at[:, lanes] if rows is None else ref.at[rows, lanes]


def sub_rows(core, slot, sub):
    first = core if slot == 0 else 3 - core
    return pl.ds(pl.multiple_of(first * sub, sub), sub)


def share_over_tp(tp_size, me, vec, got, ss, rs):
    copies = []
    for r in range(1, tp_size):
        copy = remote(vec, got.at[r], ss.at[r], rs.at[r], {"tp": lax.rem(me + r, tp_size)})
        copy.start()
        copies.append(copy)

    def finish():
        for copy in copies:
            copy.wait()
        return (vec[...] + got[2]) + (got[1] + got[3])

    return finish


def rolled(t, c, s):
    return t * c + pltpu.roll(t, LANES // 2, 1) * s


def group_barrier(me_tp, me_cp, tp_size, cp_size):
    barrier = pltpu.get_barrier_semaphore()
    for st in range(tp_size):
        for sc in range(cp_size):
            if st or sc:
                pl.semaphore_signal(barrier, inc=1, device_id={"tp": lax.rem(me_tp + st, tp_size), "cp": lax.rem(me_cp + sc, cp_size)}, device_id_type=MESH)
    pl.semaphore_wait(barrier, tp_size * cp_size - 1)


def scatter_qkv(heads, tp_size, cp_size, width, q_lin, k_lin, v_in, vec, q_gain, k_gain, cos_t, sin_t, q_out, k_out, v_out, inv_out, q16, k16, got, loc, qs, qr, ks, kr, vs, vr, fks, fkr, fvs, fvr, ts, tr):
    me_tp = lax.axis_index("tp")
    me = lax.axis_index("cp")
    core = lax.rem(me, 2)
    chip = me // 2
    sub = q_out.shape[1] // 2
    cross_barrier(me_tp, me, tp_size, cp_size)
    finish = share_over_tp(tp_size, me_tp, vec, got, ts, tr)
    far_chips = (1, heads - 1, 2)
    sends = []

    def spread(src, out, ss, rs):
        for r in far_chips:
            dst = lax.rem(chip + r, heads)
            copy = remote(cols(src, dst), out.at[me], ss.at[r], rs.at[r], {"cp": dst * 2 + core})
            copy.start()
            sends.append(copy)

    spread(v_in, v_out, vs, vr)
    inv_out[...] = lax.rsqrt(finish() / width + NORM_EPS)
    n_chunk = inv_out.shape[0] // 2
    inv_cols = inv_out[...].T

    def rotate(lin, gain, out16, first):
        for r in range(n_chunk):
            rows = slice(r * LANES, (r + 1) * LANES)
            scale = inv_cols[:, first + r : first + r + 1]
            for h in range(heads):
                lanes = slice(h * LANES, (h + 1) * LANES)
                out16[rows, lanes] = rolled(lin[rows, lanes] * scale * gain[:, lanes], cos_t[rows, :], sin_t[rows, :]).astype(out16.dtype)

    rotate(k_lin, k_gain, k16, n_chunk)
    spread(k16, k_out, ks, kr)
    rotate(q_lin, q_gain, q16, 0)
    own = [pltpu.make_async_copy(cols(k16, chip), k_out.at[me], loc.at[0]), pltpu.make_async_copy(cols(v_in, chip), v_out.at[me], loc.at[1])]
    for r in range(cp_size):
        dst = lax.rem(me + r, cp_size)
        for s in range(2):
            src = cols(q16, dst // 2, sub_rows(lax.rem(dst, 2), s, sub))
            place = q_out.at[me, s * sub : (s + 1) * sub, :]
            if r == 0:
                own.append(pltpu.make_async_copy(src, place, loc.at[2 + s]))
            else:
                copy = remote(src, place, qs.at[r, s], qr.at[r, s], {"cp": dst})
                copy.start()
                sends.append(copy)
    for copy in own:
        copy.start()
    partner = {"cp": me + 1 - 2 * core}
    forwards = []
    for r in (0,) + far_chips:
        src = lax.rem(chip - r + heads, heads) * 2 + core
        for i, (buf, ss, rs, fs, fr) in enumerate(((v_out, vs, vr, fvs, fvr), (k_out, ks, kr, fks, fkr))):
            if r == 0:
                own[1 - i].wait()
            else:
                remote(buf.at[src], buf.at[src], ss.at[r], rs.at[r], partner).wait_recv()
            copy = remote(buf.at[src], buf.at[src], fs.at[r], fr.at[r], partner)
            copy.start()
            forwards.append(copy)
    for copy in own[2:]:
        copy.wait()
    for copy in sends:
        copy.wait_send()
    for r in range(1, cp_size):
        for s in range(2):
            place = q_out.at[lax.rem(me - r + cp_size, cp_size), s * sub : (s + 1) * sub, :]
            remote(place, place, qs.at[r, s], qr.at[r, s], partner).wait_recv()
    for copy in forwards:
        copy.wait()


def attend(sub, scale, q_ref, k_ref, v_ref, o_ref, lse_ref, vt_scr, m_scr, l_scr, acc_scr, s_a, s_b, mx_a):
    blk = pl.program_id(0)
    core = lax.rem(lax.axis_index("cp"), 2)
    coef = scale * LOG2E
    half = k_ref.shape[1] // 2
    cols = q_ref.shape[1]
    chunk = half // 2
    vt_scr[blk] = v_ref[blk].T
    m_scr[...] = jnp.full_like(m_scr, -jnp.inf)
    l_scr[...] = jnp.zeros_like(l_scr)
    acc_scr[...] = jnp.zeros_like(acc_scr)

    def fold(op, values):
        return op(values.reshape(values.shape[0] // 8, 8, cols), axis=0)

    def scores(b, h, c):
        kv = slice(h * half + c * chunk, h * half + (c + 1) * chunk)
        return lax.dot_general(k_ref[b, kv, :], q_ref[0], NT, preferred_element_type=jnp.float32)

    def mask(s, h, c):
        kv_pos = h * half + c * chunk + lax.broadcasted_iota(jnp.int32, s.shape, 0)
        col = lax.broadcasted_iota(jnp.int32, s.shape, 1)
        q_pos = jnp.where(col < sub, core * sub + col, (2 - core) * sub + col)
        return jnp.where(kv_pos <= q_pos, s, -jnp.inf)

    def step(buf, mx, b, h, nxt):
        m_old = m_scr[...]
        m_new = jnp.maximum(m_old, mx)
        mc = m_new * coef
        alpha = jnp.exp2((m_old - m_new) * coef)
        lsum = jnp.zeros((8, cols), jnp.float32)
        new_mx = None
        for c in range(2):
            rows = slice(c * chunk, (c + 1) * chunk)
            if nxt is not None:
                nbuf, nb, nh, masked = nxt
                s = scores(nb, nh, c)
                if masked:
                    s = mask(s, nh, c)
                nbuf[rows, :] = s
                part = fold(jnp.max, s)
                new_mx = part if new_mx is None else jnp.maximum(new_mx, part)
            p = jnp.exp2(buf[rows, :] * coef - mc)
            lsum = lsum + fold(jnp.sum, p)
            pv = jnp.dot(vt_scr[b, :, h * half + c * chunk : h * half + (c + 1) * chunk], p.astype(jnp.bfloat16), preferred_element_type=jnp.float32)
            acc_scr[...] = acc_scr[...] * alpha + pv if c == 0 else acc_scr[...] + pv
        l_scr[...] = l_scr[...] * alpha + jnp.sum(lsum, axis=0, keepdims=True)
        m_scr[...] = m_new
        return None if nxt is None else jnp.max(new_mx, axis=0, keepdims=True)

    for c in range(2):
        s_a[c * chunk : (c + 1) * chunk, :] = scores(0, 0, c)
    mx_a[...] = jnp.max(s_a[...], axis=0, keepdims=True)

    def body(b, carry):
        mx_b = step(s_a, mx_a[...], b, 0, (s_b, b, 1, False))
        mx_a[...] = step(s_b, mx_b, b, 1, (s_a, b + 1, 0, False))
        return carry

    lax.fori_loop(0, blk, body, 0)
    for c in range(2):
        rows = slice(c * chunk, (c + 1) * chunk)
        s_a[rows, :] = mask(s_a[rows, :], 0, c)
    mx_b = step(s_a, jnp.max(s_a[...], axis=0, keepdims=True), blk, 0, (s_b, blk, 1, True))
    step(s_b, mx_b, blk, 1, None)
    o_ref[0] = (acc_scr[...] / l_scr[...]).T.astype(o_ref.dtype)
    lse_ref[0] = m_scr[...] * coef + jnp.log2(l_scr[...])


def attend_back(sub, scale, q_ref, k_ref, v_ref, o_ref, do_ref, lse_ref, dq_ref, dk_ref, dv_ref, kt_scr, dqt_scr, dl_scr):
    blk = pl.program_id(0)
    core = lax.rem(lax.axis_index("cp"), 2)
    coef = scale * LOG2E
    rows = q_ref.shape[1]
    block_len = k_ref.shape[1]
    kt_scr[blk] = k_ref[blk].T
    prod = o_ref[0].astype(jnp.float32) * do_ref[0].astype(jnp.float32)
    dl_scr[...] = jnp.sum(prod.T, axis=0, keepdims=True)
    dqt_scr[...] = jnp.zeros_like(dqt_scr)

    def step(b, masked):
        q = q_ref[0]
        do = do_ref[0]
        lse = lse_ref[0]
        delta = dl_scr[...]
        for part in range(block_len // sub):
            kv = slice(part * sub, (part + 1) * sub)
            k_blk = k_ref[b, kv, :]
            s = lax.dot_general(k_blk, q, NT, preferred_element_type=jnp.float32)
            p = jnp.exp2(s * coef - lse)
            if masked:
                kv_pos = part * sub + lax.broadcasted_iota(jnp.int32, (sub, rows), 0)
                col = lax.broadcasted_iota(jnp.int32, (sub, rows), 1)
                q_pos = jnp.where(col < sub, core * sub + col, (2 - core) * sub + col)
                p = jnp.where(kv_pos <= q_pos, p, 0.0)
            dp = lax.dot_general(v_ref[b, kv, :], do, NT, preferred_element_type=jnp.float32)
            ds = (p * (dp - delta)).astype(jnp.bfloat16)
            new_v = jnp.dot(p.astype(jnp.bfloat16), do, preferred_element_type=jnp.float32)
            new_k = jnp.dot(ds, q, preferred_element_type=jnp.float32) * scale
            if masked:
                dv_ref[b, kv, :] = new_v
                dk_ref[b, kv, :] = new_k
            else:
                dv_ref[b, kv, :] += new_v
                dk_ref[b, kv, :] += new_k
            dqt_scr[...] += jnp.dot(kt_scr[b, :, kv], ds, preferred_element_type=jnp.float32)

    def body(b, carry):
        step(b, False)
        return carry

    step(blk, True)
    lax.fori_loop(0, blk, body, 0)
    dq_ref[0] = dqt_scr[...].T * scale


def heads_to_rows(heads, tp_size, cp_size, o_in, o_out, ss, rs):
    me_tp = lax.axis_index("tp")
    me_cp = lax.axis_index("cp")
    core = lax.rem(me_cp, 2)
    head = me_tp * heads + me_cp // 2
    sub = o_out.shape[0]
    place = cols(o_out, head)
    group_barrier(me_tp, me_cp, tp_size, cp_size)
    for finish in range(2):
        if finish:
            for h in range(heads * tp_size):
                part = o_out.at[:, h * LANES : (h + 1) * LANES]
                pltpu.make_async_copy(part, part, rs.at[h]).wait()
        for s in range(2):
            dst_tp = core if s == 0 else 3 - core
            for r in range(cp_size):
                dst_cp = lax.rem(me_cp + r, cp_size)
                src = o_in.at[dst_cp, s * sub : (s + 1) * sub, :]
                copy = remote(src, place, ss.at[s, r], rs.at[head], {"tp": dst_tp, "cp": dst_cp})
                act = copy.wait_send if finish else copy.start
                if r:
                    act()
                    continue
                pl.when(dst_tp != me_tp)(act)
                if not finish:
                    pl.when(dst_tp == me_tp)(pltpu.make_async_copy(src, place, rs.at[head]).start)


def rows_to_heads(heads, tp_size, cp_size, g_in, g_out, ss, rs):
    me_tp = lax.axis_index("tp")
    me_cp = lax.axis_index("cp")
    core = lax.rem(me_cp, 2)
    sub = g_in.shape[0]
    row_core = jnp.where(me_tp < 2, me_tp, 3 - me_tp)
    slot = me_tp // 2
    place = g_out.at[me_cp, pl.ds(pl.multiple_of(slot * sub, sub), sub), :]
    group_barrier(me_tp, me_cp, tp_size, cp_size)
    for finish in range(2):
        if finish:
            for i in range(cp_size):
                for s in range(2):
                    part = g_out.at[i, s * sub : (s + 1) * sub, :]
                    pltpu.make_async_copy(part, part, rs.at[i, s]).wait()
        for rt in range(tp_size):
            dst_tp = lax.rem(me_tp + rt, tp_size)
            for r in range(heads):
                chip = lax.rem(me_cp // 2 + r, heads)
                src = cols(g_in, dst_tp * heads + chip)
                copy = remote(src, place, ss.at[rt, r], rs.at[me_cp, slot], {"tp": dst_tp, "cp": chip * 2 + row_core})
                act = copy.wait_send if finish else copy.start
                if rt or r:
                    act()
                    continue
                pl.when(row_core != core)(act)
                if not finish:
                    pl.when(row_core == core)(pltpu.make_async_copy(src, place, rs.at[me_cp, slot]).start)


def gather_grads(heads, tp_size, cp_size, width, dq_in, dk_in, dv_in, q_lin, k_lin, inv, q_gain, k_gain, cos_t, sin_t, dq_out, dk_out, dv_out, gain_out, dq, dk, pk, pv, sk, sv, part, got, loc, qs, qr, pks, pkr, pvs, pvr, ks, kr, vs, vr, ts, tr):
    me_tp = lax.axis_index("tp")
    me = lax.axis_index("cp")
    core = lax.rem(me, 2)
    chip = me // 2
    sub = dq_in.shape[1] // 2
    cross_barrier(me_tp, me, tp_size, cp_size)
    partner = {"cp": me + 1 - 2 * core}
    order = (1, heads - 1, 2, 0)
    pair, sends, own = [], [], []
    for i, r in enumerate(order):
        x = lax.rem(chip + r, heads)
        for src, dst, ss, rs in ((dk_in, pk, pks, pkr), (dv_in, pv, pvs, pvr)):
            copy = remote(src.at[2 * x + 1 - core], dst.at[x], ss.at[i], rs.at[i], partner)
            copy.start()
            pair.append(copy)
    for r in range(cp_size):
        dst = lax.rem(me + r, cp_size)
        for s in range(2):
            src = dq_in.at[dst, s * sub : (s + 1) * sub, :]
            place = cols(dq, chip, sub_rows(core, s, sub))
            if r == 0:
                own.append(pltpu.make_async_copy(src, place, loc.at[s]))
                own[s].start()
            else:
                copy = remote(src, place, qs.at[r, s], qr.at[r, s], {"cp": dst})
                copy.start()
                sends.append(copy)
    for i, r in enumerate(order):
        x = lax.rem(chip + r, heads)
        pair[2 * i].wait()
        pair[2 * i + 1].wait()
        sk[x] = dk_in[2 * x + core] + pk[x]
        sv[x] = (dv_in[2 * x + core] + pv[x]).astype(sv.dtype)
        for j, (src, out, ss, rs) in enumerate(((sk, dk, ks, kr), (sv, dv_out, vs, vr))):
            if r == 0:
                copy = pltpu.make_async_copy(src.at[x], cols(out, chip), loc.at[2 + j])
                own.append(copy)
            else:
                copy = remote(src.at[x], cols(out, chip), ss.at[r], rs.at[r], {"cp": x * 2 + core})
                sends.append(copy)
            copy.start()
    for copy in own:
        copy.wait()
    for r in range(1, cp_size):
        src = lax.rem(me - r + cp_size, cp_size)
        for s in range(2):
            place = cols(dq, src // 2, sub_rows(lax.rem(src, 2), s, sub))
            remote(place, place, qs.at[r, s], qr.at[r, s], partner).wait_recv()
    inv_cols = inv[...].T
    n_chunk = inv.shape[0] // 2
    dots = []

    def first_pass(i, grad, lin, gain):
        gains = [jnp.zeros((1, LANES), jnp.float32)] * heads
        for r in range(n_chunk):
            rows = slice(r * LANES, (r + 1) * LANES)
            scale = inv_cols[:, i * n_chunk + r : i * n_chunk + r + 1]
            total = jnp.zeros((LANES, LANES), jnp.float32)
            for h in range(heads):
                lanes = slice(h * LANES, (h + 1) * LANES)
                hat = lin[rows, lanes] * scale
                back = rolled(grad[rows, lanes], cos_t[rows, :], -sin_t[rows, :])
                both = back * hat
                gains[h] = gains[h] + jnp.sum(both, axis=0, keepdims=True)
                total = total + both * gain[:, lanes]
                grad[rows, lanes] = back * gain[:, lanes]
            dots.append(jnp.sum(total, axis=1, keepdims=True))
        for h in range(heads):
            gain_out[i * heads + h : i * heads + h + 1, :] = gains[h]

    first_pass(0, dq, q_lin, q_gain)
    for r in order[:-1]:
        place = cols(dk, lax.rem(chip - r + heads, heads))
        remote(place, place, ks.at[r], kr.at[r], partner).wait_recv()
    first_pass(1, dk, k_lin, k_gain)
    part[...] = jnp.concatenate(dots, axis=1).T
    total_dots = share_over_tp(tp_size, me_tp, part, got, ts, tr)() / width
    dot_cols = total_dots.T
    for i, (grad, lin, out) in enumerate(((dq, q_lin, dq_out), (dk, k_lin, dk_out))):
        for r in range(n_chunk):
            rows = slice(r * LANES, (r + 1) * LANES)
            c = i * n_chunk + r
            scale = inv_cols[:, c : c + 1]
            out[rows, :] = (scale * (grad[rows, :] - lin[rows, :] * scale * dot_cols[:, c : c + 1])).astype(out.dtype)
    for copy in sends:
        copy.wait_send()
    for r in order[:-1]:
        place = cols(dv_out, lax.rem(chip - r + heads, heads))
        remote(place, place, vs.at[r], vr.at[r], partner).wait_recv()


def reduce_tail(tp_size, cp_size, n_heads, *refs):
    n_w = 4
    w_in, (dx_in, dy_in, small) = refs[:n_w], refs[n_w : n_w + 3]
    refs = refs[n_w + 3 :]
    w_out, (dx_out, small_out) = refs[:n_w], refs[n_w : n_w + 2]
    refs = refs[n_w + 2 :]
    acc, pair, far_a, far_b, fin_l, fin_r = (refs[i * n_w : (i + 1) * n_w] for i in range(6))
    refs = refs[6 * n_w :]
    dxa, dxb, dx_own, dx_fa, dx_fb, dx_fl, dx_fr, dx16, got_small, got_post, ss, rs, ps, pr, fs, fr, loc, sms, smr, gps, gpr = refs
    me_tp = lax.axis_index("tp")
    me_cp = lax.axis_index("cp")
    core = lax.rem(me_cp, 2)
    chip = me_cp // 2
    ring = cp_size // 2
    left, right, far = (lax.rem(chip + d, ring) for d in (ring - 1, 1, 2))
    t_left, t_right, t_far = (lax.rem(me_tp + d, tp_size) for d in (tp_size - 1, 1, 2))
    partner = {"cp": me_cp + 1 - 2 * core}
    to_l, to_r = {"cp": left * 2 + core}, {"cp": right * 2 + core}
    tp_l, tp_r = {"tp": t_left}, {"tp": t_right}
    dx_i = n_w

    def ring_sems(t, kind):
        return ss.at[t, kind], rs.at[t, kind]

    def pair_sems(t, kind):
        return fs.at[t, kind], fr.at[t, kind]

    cross_barrier(me_tp, me_cp, tp_size, cp_size)
    sent = []

    def go(src, dst, s_sem, r_sem, device):
        copy = remote(src, dst, s_sem, r_sem, device)
        copy.start()
        sent.append(copy)

    def landed(dst, s_sem, r_sem):
        remote(dst, dst, s_sem, r_sem, partner).wait_recv()

    def piece(ref, t, x, c, part=None):
        size = w_in[t].shape[0] // cp_size
        first = (2 * x + c) * size
        if part is None:
            return ref.at[pl.ds(pl.multiple_of(first, size), size), :]
        return ref.at[pl.ds(pl.multiple_of(first + part * (size // 2), size // 2), size // 2), :]

    def rows_of(ref, y, part=None):
        size = dx_in.shape[0] // tp_size
        if part is None:
            return ref.at[pl.ds(pl.multiple_of(y * size, size), size), :]
        return ref.at[pl.ds(pl.multiple_of(y * size + part * (size // 2), size // 2), size // 2), :]

    def half_of(ref, part):
        size = ref.shape[0] // 2
        return ref.at[pl.ds(part * size, size), :]

    for r in range(1, cp_size):
        go(small, got_small.at[me_cp], sms.at[r], smr.at[r], {"cp": lax.rem(me_cp + r, cp_size)})
    go(rows_of(dx_in, t_far, 0), dx_fa, *ring_sems(dx_i, 0), tp_l)
    go(rows_of(dx_in, t_far, 1), dx_fb, *ring_sems(dx_i, 1), tp_r)
    go(rows_of(dx_in, t_left, 1), half_of(dx_fr, 1), *ring_sems(dx_i, 2), tp_l)
    go(rows_of(dx_in, t_right, 0), half_of(dx_fl, 0), *ring_sems(dx_i, 3), tp_r)
    order = (far, left, right, chip)
    loads = []
    for t in range(n_w):
        for i, x in enumerate(order):
            go(piece(w_in[t], t, x, 1 - core), pair[t].at[x], ps.at[t, i], pr.at[t, i], partner)
            copy = pltpu.make_async_copy(piece(w_in[t], t, x, core), acc[t].at[x], loc.at[t, i])
            copy.start()
            loads.append(copy)
    dx_loads = [
        pltpu.make_async_copy(rows_of(dx_in, t_left, 0), dxa, loc.at[n_w, 0]),
        pltpu.make_async_copy(rows_of(dx_in, t_right, 1), dxb, loc.at[n_w, 1]),
        pltpu.make_async_copy(rows_of(dx_in, me_tp), dx_own, loc.at[n_w, 2]),
    ]
    for copy in dx_loads:
        copy.start()

    for t in range(n_w):
        for i, x in enumerate(order):
            loads[t * 4 + i].wait()
            landed(pair[t].at[x], ps.at[t, i], pr.at[t, i])
            acc[t][x] += pair[t][x]
        go(half_of(acc[t].at[far], 0), far_a[t], *ring_sems(t, 0), to_l)
        go(half_of(acc[t].at[far], 1), far_b[t], *ring_sems(t, 1), to_r)
        go(half_of(acc[t].at[left], 1), half_of(fin_r[t], 1), *ring_sems(t, 2), to_l)
        go(half_of(acc[t].at[right], 0), half_of(fin_l[t], 0), *ring_sems(t, 3), to_r)

    got_small[me_cp] = small[...]
    for r in range(1, cp_size):
        landed(got_small.at[lax.rem(me_cp - r + cp_size, cp_size)], sms.at[r], smr.at[r])
    total = got_small[0]
    for i in range(1, cp_size):
        total = total + got_small[i]
    small_out[...] = total
    n_gain = small.shape[0] - got_post.shape[1]

    def second_half(t, acc_l, acc_r, fa, fb, fl, fr, dev_l, dev_r):
        half = fa.shape[0]
        landed(fa, *ring_sems(t, 0))
        acc_l[...] += fa[...]
        landed(fb, *ring_sems(t, 1))
        acc_r[...] += fb[...]
        go(acc_l, half_of(fr, 0), *ring_sems(t, 4), dev_l)
        go(acc_r, half_of(fl, 1), *ring_sems(t, 5), dev_r)

    def all_landed(t, fl, fr):
        landed(half_of(fr, 1), *ring_sems(t, 2))
        landed(half_of(fl, 0), *ring_sems(t, 3))
        landed(half_of(fr, 0), *ring_sems(t, 4))
        landed(half_of(fl, 1), *ring_sems(t, 5))

    for t in range(n_w):
        second_half(t, half_of(acc[t].at[left], 0), half_of(acc[t].at[right], 1), far_a[t], far_b[t], fin_l[t], fin_r[t], to_l, to_r)
    for copy in dx_loads:
        copy.wait()
    second_half(dx_i, dxa, dxb, dx_fa, dx_fb, dx_fl, dx_fr, tp_l, tp_r)
    post = small_out.at[pl.ds(n_gain, got_post.shape[1]), :]
    for r in range(1, tp_size):
        go(post, got_post.at[r], gps.at[r], gpr.at[r], {"tp": lax.rem(me_tp + r, tp_size)})

    outs = []
    for t in range(n_w):
        all_landed(t, fin_l[t], fin_r[t])
        acc[t][chip] = acc[t][chip] + (fin_l[t][...] + fin_r[t][...])
        src = acc[t].at[chip]
        dst = piece(w_out[t], t, chip, core)
        copy = pltpu.make_async_copy(src, dst, loc.at[t, 4])
        copy.start()
        outs.append(copy)
        go(src, dst, *ring_sems(t, 6), to_l)
        go(src, dst, *ring_sems(t, 7), to_r)
        go(src, dst, *pair_sems(t, 0), partner)
    all_landed(dx_i, dx_fl, dx_fr)
    dx16[...] = (dx_own[...] + (dx_fl[...] + dx_fr[...]) + dy_in[...].astype(jnp.float32)).astype(dx16.dtype)
    copy = pltpu.make_async_copy(dx16, rows_of(dx_out, me_tp), loc.at[n_w, 4])
    copy.start()
    outs.append(copy)
    go(dx16, rows_of(dx_out, me_tp), *ring_sems(dx_i, 6), tp_l)
    go(dx16, rows_of(dx_out, me_tp), *ring_sems(dx_i, 7), tp_r)

    for t in range(n_w):
        landed(piece(w_out[t], t, right, core), *ring_sems(t, 6))
        half = piece(w_out[t], t, right, core, 0)
        go(half, half, *ring_sems(t, 8), to_l)
        whole = piece(w_out[t], t, right, core)
        go(whole, whole, *pair_sems(t, 1), partner)
        landed(piece(w_out[t], t, left, core), *ring_sems(t, 7))
        half = piece(w_out[t], t, left, core, 1)
        go(half, half, *ring_sems(t, 9), to_r)
        whole = piece(w_out[t], t, left, core)
        go(whole, whole, *pair_sems(t, 2), partner)
    landed(rows_of(dx_out, t_right), *ring_sems(dx_i, 6))
    half = rows_of(dx_out, t_right, 0)
    go(half, half, *ring_sems(dx_i, 8), tp_l)
    landed(rows_of(dx_out, t_left), *ring_sems(dx_i, 7))
    half = rows_of(dx_out, t_left, 1)
    go(half, half, *ring_sems(dx_i, 9), tp_r)

    sums = small_out[n_gain:, :]
    for r in range(1, tp_size):
        landed(got_post.at[r], gps.at[r], gpr.at[r])
    sums = (sums + got_post[2]) + (got_post[1] + got_post[3])

    for t in range(n_w):
        for kind, part in ((8, 0), (9, 1)):
            half = piece(w_out[t], t, far, core, part)
            landed(half, *ring_sems(t, kind))
            go(half, half, *pair_sems(t, 3 + part), partner)
    for kind, part in ((8, 0), (9, 1)):
        landed(rows_of(dx_out, t_far, part), *ring_sems(dx_i, kind))
    for t in range(n_w):
        for i, x in enumerate((chip, right, left)):
            landed(piece(w_out[t], t, x, 1 - core), *pair_sems(t, i))
        for part in range(2):
            landed(piece(w_out[t], t, far, 1 - core, part), *pair_sems(t, 3 + part))
    for copy in outs:
        copy.wait()
    for copy in sent:
        copy.wait_send()
    small_out[n_gain:, :] = sums


def solution(mesh):
    tp_size = mesh.shape["tp"]
    cp_size = mesh.shape["cp"]
    act_spec = P("dp", "cp", None)
    col_spec = P(None, "tp", None)
    part_col = P("dp", "tp", None)
    in_specs = (act_spec, col_spec, col_spec, col_spec, P("tp", None, None), P("tp", None), P("tp", None), P(None), act_spec)
    out_specs = (act_spec, act_spec, part_col, part_col, part_col, P(("dp", "tp"), None, None), P(("dp", "tp"), None), P(("dp", "tp"), None), P("dp"))
    dma = pltpu.SemaphoreType.DMA

    def local_run(x_in, w_q, w_k, w_v, w_o, q_norm_w, k_norm_w, post_norm_w, grad_y):
        n_batch, block_len, d_model = x_in.shape
        heads, head_dim = w_q.shape[1:]
        assert n_batch == 1 and w_k.shape[1] == heads and cp_size == 2 * heads and tp_size == 4
        sub = block_len // tp_size
        rows = 2 * sub
        width = heads * head_dim * tp_size
        scale = head_dim ** -0.5
        f32 = jnp.float32
        b16 = jnp.bfloat16
        tp_index = lax.axis_index("tp")
        cp_index = lax.axis_index("cp")
        cos_tab, sin_tab = rope_tables(cp_index * block_len, block_len, head_dim)
        x_loc = x_in[0]
        dy_loc = grad_y[0]
        w_o_full = lax.all_gather(w_o.reshape(-1, d_model), "tp", axis=0, tiled=True)
        w_q2, w_k2, w_v2 = (w.reshape(d_model, -1) for w in (w_q, w_k, w_v))
        gains = [g.reshape(1, -1) for g in (q_norm_w, k_norm_w)]
        loc_width = heads * head_dim

        q_lin = jnp.dot(x_loc, w_q2, preferred_element_type=f32)
        k_lin = jnp.dot(x_loc, w_k2, preferred_element_type=f32)
        v_val = jnp.dot(x_loc, w_v2, preferred_element_type=f32).astype(b16)
        vec = jnp.stack([jnp.sum(t * t, axis=1) for t in (q_lin, k_lin)]).reshape(-1, LANES)
        vec_shape = jax.ShapeDtypeStruct(vec.shape, f32)
        kv_shape = jax.ShapeDtypeStruct((cp_size, block_len, head_dim), b16)
        lin16 = VMEM((block_len, loc_width), b16)
        tp_scratch = VMEM((tp_size,) + vec.shape, f32)
        q_all, k_all, v_all, inv = vmem_call(
            functools.partial(scatter_qkv, heads, tp_size, cp_size, width),
            [jax.ShapeDtypeStruct((cp_size, rows, head_dim), b16), kv_shape, kv_shape, vec_shape],
            8,
            [lin16, lin16, tp_scratch, dma((4,))] + [dma((cp_size, 2))] * 2 + [dma((heads,))] * 8 + [dma((tp_size,))] * 2,
            collective_id=0,
        )(q_lin, k_lin, v_val, vec, *gains, cos_tab, sin_tab)

        qspec = pl.BlockSpec((1, rows, head_dim), lambda i: (i, 0, 0))
        lspec = pl.BlockSpec((1, 1, rows), lambda i: (i, 0, 0))
        whole = pl.BlockSpec(memory_space=VMEM)
        pair_flops = cp_size * (cp_size + 1) // 2 * rows * block_len * head_dim * 2
        o_all, lse = pl.pallas_call(
            functools.partial(attend, sub, scale),
            grid=(cp_size,),
            in_specs=[qspec, whole, whole],
            out_specs=[qspec, lspec],
            out_shape=[jax.ShapeDtypeStruct((cp_size, rows, head_dim), b16), jax.ShapeDtypeStruct((cp_size, 1, rows), f32)],
            scratch_shapes=[VMEM((cp_size, head_dim, block_len), b16), VMEM((1, rows), f32), VMEM((1, rows), f32), VMEM((head_dim, rows), f32)]
            + [VMEM((block_len // 2, rows), f32)] * 2 + [VMEM((1, rows), f32)],
            compiler_params=pltpu.CompilerParams(vmem_limit_bytes=LIMIT),
            cost_estimate=pl.CostEstimate(flops=2 * pair_flops, bytes_accessed=6 << 20, transcendentals=0),
        )(q_all, k_all, v_all)

        n_heads = heads * tp_size
        o_rows = vmem_call(
            functools.partial(heads_to_rows, heads, tp_size, cp_size),
            [jax.ShapeDtypeStruct((sub, width), b16)],
            1,
            [dma((2, cp_size)), dma((n_heads,))],
            collective_id=1,
        )(o_all)[0]

        x_rows = lax.dynamic_slice_in_dim(x_loc, tp_index * sub, sub, 0)
        dy_rows = lax.dynamic_slice_in_dim(dy_loc, tp_index * sub, sub, 0)
        dy_f = dy_rows.astype(f32)
        proj = jnp.dot(o_rows, w_o_full, preferred_element_type=f32)
        post_inv = lax.rsqrt(jnp.mean(proj * proj, axis=-1, keepdims=True) + NORM_EPS)
        post_hat = proj * post_inv
        y_rows = (x_rows + post_hat * post_norm_w).astype(b16)
        grad_post = jnp.sum(dy_f * post_hat, axis=0)
        grad_hat = dy_f * post_norm_w
        gp_rows = (post_inv * (grad_hat - post_hat * jnp.mean(grad_hat * post_hat, axis=-1, keepdims=True))).astype(b16)
        do_rows = lax.dot_general(gp_rows, w_o_full, NT, preferred_element_type=f32).astype(b16)

        do_all = vmem_call(
            functools.partial(rows_to_heads, heads, tp_size, cp_size),
            [jax.ShapeDtypeStruct((cp_size, rows, head_dim), b16)],
            1,
            [dma((tp_size, heads)), dma((cp_size, 2))],
            collective_id=2,
        )(do_rows)[0]

        grad_proj = lax.all_gather(gp_rows, "tp", axis=0, tiled=True)
        o_gath = lax.all_gather(o_rows, "tp", axis=0, tiled=True)
        y_out = lax.all_gather(y_rows, "tp", axis=0, tiled=True)

        dq_all, dk_all, dv_all = pl.pallas_call(
            functools.partial(attend_back, sub, scale),
            grid=(cp_size,),
            in_specs=[qspec, whole, whole, qspec, qspec, lspec],
            out_specs=[qspec, whole, whole],
            out_shape=[jax.ShapeDtypeStruct((cp_size, rows, head_dim), f32)] + [jax.ShapeDtypeStruct((cp_size, block_len, head_dim), f32)] * 2,
            scratch_shapes=[VMEM((cp_size, head_dim, block_len), b16), VMEM((head_dim, rows), f32), VMEM((1, rows), f32)],
            compiler_params=pltpu.CompilerParams(vmem_limit_bytes=LIMIT),
            cost_estimate=pl.CostEstimate(flops=5 * pair_flops, bytes_accessed=16 << 20, transcendentals=0),
        )(q_all, k_all, v_all, o_all, do_all, lse)

        dq_all, grad_proj, o_gath = lax.optimization_barrier((dq_all, grad_proj, o_gath))
        lin_f, lin_h = VMEM((block_len, loc_width), f32), jax.ShapeDtypeStruct((block_len, loc_width), b16)
        head_f = VMEM((heads, block_len, head_dim), f32)
        dq16, dk16, dv16, gain_grads = vmem_call(
            functools.partial(gather_grads, heads, tp_size, cp_size, width),
            [lin_h, lin_h, lin_h, jax.ShapeDtypeStruct((2 * heads, head_dim), f32)],
            10,
            [lin_f, lin_f, head_f, head_f, head_f, VMEM((heads, block_len, head_dim), b16), VMEM(vec.shape, f32), tp_scratch, dma((4,))]
            + [dma((cp_size, 2))] * 2 + [dma((heads,))] * 8 + [dma((tp_size,))] * 2,
            collective_id=3,
        )(dq_all, dk_all, dv_all, q_lin, k_lin, inv, *gains, cos_tab, sin_tab)
        o_own = lax.dynamic_slice_in_dim(o_gath, tp_index * loc_width, loc_width, 1)

        def wgrad(left, right):
            return lax.dot_general(left, right, (((0,), (0,)), ((), ())), preferred_element_type=f32)

        grad_w_o, grad_w_v, grad_w_q, grad_w_k = wgrad(o_own, grad_proj), wgrad(x_loc, dv16), wgrad(x_loc, dq16), wgrad(x_loc, dk16)
        dx_part = sum(lax.dot_general(g, w, NT, preferred_element_type=f32) for g, w in ((dq16, w_q2), (dk16, w_k2), (dv16, w_v2)))
        w_parts = [grad_w_o, grad_w_v, grad_w_q, grad_w_k]
        small = jnp.concatenate([gain_grads, grad_post.reshape(-1, head_dim)], axis=0)
        any_spec = pl.BlockSpec(memory_space=pl.ANY)
        vmem_spec = pl.BlockSpec(memory_space=VMEM)

        def bufs(lead, div):
            return [VMEM(lead + (w.shape[0] // div, w.shape[1]), f32) for w in w_parts]

        ring = cp_size // 2
        rows_dx, half_dx = VMEM((sub, d_model), f32), VMEM((sub // 2, d_model), f32)
        res = pl.pallas_call(
            functools.partial(reduce_tail, tp_size, cp_size, heads),
            out_shape=[jax.ShapeDtypeStruct(w.shape, f32) for w in w_parts] + [jax.ShapeDtypeStruct((block_len, d_model), b16), jax.ShapeDtypeStruct(small.shape, f32)],
            in_specs=[any_spec] * 5 + [vmem_spec] * 2,
            out_specs=[any_spec] * 5 + [vmem_spec],
            scratch_shapes=bufs((ring,), cp_size) * 2 + bufs((), 2 * cp_size) * 2 + bufs((), cp_size) * 2
            + [half_dx, half_dx, rows_dx, half_dx, half_dx, rows_dx, rows_dx, VMEM((sub, d_model), b16)]
            + [VMEM((cp_size,) + small.shape, f32), VMEM((tp_size, d_model // head_dim, head_dim), f32)]
            + [dma((5, 10))] * 2 + [dma((4, 4))] * 2 + [dma((4, 5))] * 2 + [dma((5, 5))] + [dma((cp_size,))] * 2 + [dma((tp_size,))] * 2,
            compiler_params=pltpu.CompilerParams(vmem_limit_bytes=LIMIT, collective_id=6, has_side_effects=True),
        )(*w_parts, dx_part, dy_rows, small)
        grad_w_v, grad_w_q, grad_w_k = (g.reshape(w_q.shape) for g in res[1:4])
        grad_x, small_sum = res[4:]
        return (y_out[None], grad_x[None], grad_w_q, grad_w_k, grad_w_v, res[0].reshape(w_o.shape), small_sum[:heads], small_sum[heads : 2 * heads], small_sum[2 * heads :].reshape(-1))

    return jax.shard_map(local_run, mesh=mesh, in_specs=in_specs, out_specs=out_specs, check_vma=False)
```

time: 616 us -> 538 us (0.87)
  waiting for transfers between devices: 36.9 us -> 3.24 us
  local copies, waits for them, and re-layouts: 64.4 us -> 34.6 us
  other arithmetic: 28.2 us -> 10.2 us
    all_gather x2, waiting for transfers between devices: 36 us -> 0.03 us  [the longest x1 0.02 us: local_run(): lax.all_gather(w_o.reshape(-1, d_model), 'tp', axis=0, tiled=True)]
    reshape x8 -> x4, local copies, waits for them, and re-layouts: 31.7 us -> 16.3 us  [the longest x3 15.7 us: local_run(): grad_w_v, grad_w_q, grad_w_k = (g.reshape(w_q.shape) for g in res[1:4])]
    unnamed x68 -> x33, local copies, waits for them, and re-layouts: 20.7 us -> 10.7 us
    convert_element_type x2 -> x0, other arithmetic: 7.51 us -> none  [the longest x1 3.96 us: local_run(): dq16 = (q_inv * (dq_n - q_hat * dots[0][None, :, None])).astype(b16)]
    pallas_call x4 -> x2, Pallas kernels: 122 us -> 118 us  [the longest x1 69 us: local_run(): vmem_call(functools.partial(gather_grads, heads, tp_size, cp_size, width)...]
  transfers between devices with their start and end apart: 4 -> 4, of which waited for: 1 -> 1; matrix products, arithmetic and copies ran while one was open for 22% -> 18% of each run, Pallas kernels for 67% -> 77%
where the time goes in v3:
time: 538 us; the launch traced here: 533 us
  Pallas kernels  410 us (76%)
  matrix products  60.3 us (11%)
  local copies, waits for them, and re-layouts  34.6 us (6%)
  between operations  14.4 us (3%)
  other arithmetic  10.2 us (2%)
    pallas_call x1, Pallas kernels, local_run(): pl.pallas_call(functools.partial(reduce_tail, tp_size, cp_size, heads), o...  151 us
    pallas_call x1, Pallas kernels, local_run(): vmem_call(functools.partial(gather_grads, heads, tp_size, cp_size, width)...  69 us
    pallas_call x1, Pallas kernels, local_run(): pl.pallas_call(functools.partial(attend_back, sub, scale), grid=(cp_size,...  59 us
    pallas_call x1, Pallas kernels, local_run(): vmem_call(functools.partial(scatter_qkv, heads, tp_size, cp_size, width),...  49 us
    pallas_call x1, Pallas kernels, local_run(): pl.pallas_call(functools.partial(attend, sub, scale), grid=(cp_size,), in...  36.2 us
    pallas_call x1, Pallas kernels, local_run(): vmem_call(functools.partial(rows_to_heads, heads, tp_size, cp_size), [jax...  24.6 us
    pallas_call x1, Pallas kernels, local_run(): vmem_call(functools.partial(heads_to_rows, heads, tp_size, cp_size), [jax...  21.3 us
    dot_general x4, matrix products, wgrad(): lax.dot_general(left, right, (((0,), (0,)), ((), ())), preferred_element_...  19.4 us
  transfers between devices with their start and end apart: 4, of which 1 were waited for; matrix products, arithmetic and copies ran while one was open for 18% of the time, Pallas kernels for 77%

profile of v3, /device:TPU:97, one launch (start us, length us, event | category | flops | bytes accessed | tf_op | source)
XLA Modules:
  0.0 533.2 jit_solution(7876494774936179349)
XLA Ops:
  8.1 6.7 %multiply_reduce_fusion.2 = (f32[1024]{0:T(1024)S(1)}, f32[1024,512]{0,1:T(8,128)}) fusion(bf16[256,8,4,128]{3,2,1,0:T(4,128)(2,1)} %bitcast.98, bf16[1,1024,2048]{2,1,0:T(8,128)(2,1)} %param.9), kind=kOutput, calls=%fused_computation.37 | convolution fusion | flops 2148531200 | bytes 8392704 | tf_op jit(solution)/shard_map/dot_general | solution.py:645
  14.8 3.8 multiply_reduce_fusion.1
  19.2 3.5 copy.18.q_lin
  28.7 5.5 %fusion.42.v_in = bf16[1024,512]{1,0:T(8,128)(2,1)} fusion(bf16[256,8,4,128]{3,2,1,0:T(4,128)(2,1)S(1)} %bitcast.86, bf16[1,1024,2048]{2,1,0:T(8,128)(2,1)} %param.9), kind=kOutput, calls=%fused_computation.44 | convolution fusion | flops 2148007936 | bytes 7340032 | tf_op jit(solution)/shard_map/dot_general | solution.py:647
  34.2 49.0 %shard_map.160 = (bf16[8,512,128]{2,1,0:T(8,128)(2,1)}, bf16[8,1024,128]{2,1,0:T(8,128)(2,1)}, bf16[8,1024,128]{2,1,0:T(8,128)(2,1)}, f32[16,128]{1,0:T(8,128)}) custom-call(f32[1024,512]{1,0:T(8,128)} %copy.18.q_lin, f32[1024,512]{1,0:T(8,128)} %copy.19.k_lin, bf16[1024,512]{1,0:T(8,128)(2,1)} %fusion.42.v_in, f32[16,128]{1,0:T(8,128)} %reshape.99.vec, ...), custom_call_target="tpu_custom_call" | custom-call | tf_op jit(solution)/shard_map/pallas_call | solution.py:653
  83.2 36.2 %shard_map.161 = (bf16[8,512,128]{2,1,0:T(8,128)(2,1)}, f32[8,1,512]{2,1,0:T(1,128)}) custom-call(bf16[8,512,128]{2,1,0:T(8,128)(2,1)} %get-tuple-element.31.q_ref, bf16[8,1024,128]{2,1,0:T(8,128)(2,1)} %get-tuple-element.32.k_ref, bf16[8,1024,128]{2,1,0:T(8,128)(2,1)} %get-tuple-element.33.v_ref), custom_call_target="tpu_custom_call" | custom-call | flops 9663676416 | bytes 6291456 | tf_op jit(solution)/shard_map/pallas_call | solution.py:665
  119.4 21.3 %shard_map.162 = bf16[256,2048]{1,0:T(8,128)(2,1)} custom-call(bf16[8,512,128]{2,1,0:T(8,128)(2,1)} %get-tuple-element.34.o_in.o_ref), custom_call_target="tpu_custom_call" | custom-call | tf_op jit(solution)/shard_map/pallas_call | solution.py:678
  141.0 6.1 %multiply_reduce_fusion = (f32[256]{0:T(256)S(1)}, f32[256,2048]{1,0:T(8,128)S(1)}) fusion(bf16[256,2048]{1,0:T(8,128)(2,1)} %shard_map.162, bf16[2048,2048]{1,0:T(8,128)(2,1)} %all-gather.5.cloned.1.call-done), kind=kOutput, calls=%fused_computation.35 | convolution fusion | flops 2148531968 | bytes 11535360 | tf_op jit(solution)/shard_map/dot_general | solution.py:689
  149.3 3.7 fusion.25
  153.1 7.1 %convolution_convert_fusion.g_in = bf16[256,2048]{1,0:T(8,128)(2,1)} fusion(bf16[256,2048]{1,0:T(8,128)(2,1)} %get-tuple-element.56, bf16[2048,2048]{1,0:T(8,128)(2,1)} %all-gather.5.cloned.1.call-done), kind=kOutput, calls=%fused_computation.18 | convolution fusion | flops 2148007936 | bytes 10485760 | tf_op jit(solution)/shard_map/dot_general | solution.py:696
  160.2 24.6 %shard_map.163.do_ref = bf16[8,512,128]{2,1,0:T(8,128)(2,1)} custom-call(bf16[256,2048]{1,0:T(8,128)(2,1)} %convolution_convert_fusion.g_in), custom_call_target="tpu_custom_call" | custom-call | tf_op jit(solution)/shard_map/pallas_call | solution.py:698
  184.9 59.0 %shard_map.164 = (f32[8,512,128]{2,1,0:T(8,128)}, f32[8,1024,128]{2,1,0:T(8,128)}, f32[8,1024,128]{2,1,0:T(8,128)}) custom-call(bf16[8,512,128]{2,1,0:T(8,128)(2,1)} %get-tuple-element.31.q_ref, bf16[8,1024,128]{2,1,0:T(8,128)(2,1)} %get-tuple-element.32.k_ref, bf16[8,1024,128]{2,1,0:T(8,128)(2,1)} %get-tuple-element.33.v_ref, ...), custom_call_target="tpu_custom_call" | custom-call | flops 24159191040 | bytes 16777216 | tf_op jit(solution)/shard_map/pallas_call | solution.py:710
  246.2 69.0 %shard_map.165 = (bf16[1024,512]{1,0:T(8,128)(2,1)}, bf16[1024,512]{1,0:T(8,128)(2,1)}, bf16[1024,512]{1,0:T(8,128)(2,1)}, f32[8,128]{1,0:T(8,128)}) custom-call(f32[8,512,128]{2,1,0:T(8,128)} %get-tuple-element.39.dq_in, f32[8,1024,128]{2,1,0:T(8,128)} %get-tuple-element.40.dk_in, f32[8,1024,128]{2,1,0:T(8,128)} %get-tuple-element.41.dv_in, ...), custom_call_target="tpu_custom_call" | custom-call | tf_op jit(solution)/shard_map/pallas_call | solution.py:724
  316.5 3.7 fusion.29
  322.7 5.9 %fusion.47.refs_0_ = f32[512,2048]{1,0:T(8,128)} fusion(bf16[1024,2048]{1,0:T(8,128)(2,1)S(1)} %copy-done.9, bf16[1024,2048]{1,0:T(8,128)(2,1)} %all-gather.11.cloned.1.call-done, s32[]{:T(128)S(6)} %select_n.29), kind=kOutput, calls=%fused_computation.45 | convolution fusion | flops 2147483648 | bytes 9437188 | tf_op jit(solution)/shard_map/dot_general | solution.py:735
  328.6 4.4 fusion.15.refs_2_
  333.0 4.7 fusion.18.refs_3_
  337.7 4.4 fusion.12.refs_1_
  342.1 5.6 %add_add_fusion.refs_4_ = f32[1024,2048]{1,0:T(8,128)} fusion(f32[1024,2048]{1,0:T(8,128)S(1)} %fusion.32, f32[1024,2048]{1,0:T(8,128)S(1)} %fusion.29, bf16[1024,512]{1,0:T(8,128)(2,1)S(1)} %copy-done.4, bf16[256,8,4,128]{3,2,1,0:T(4,128)(2,1)S(1)} %bitcast.87), kind=kOutput, calls=%fused_computation | convolution fusion | flops 2151677952 | bytes 28311552 | tf_op jit(solution)/shard_map/dot_general | solution.py:738
  347.8 150.9 %shard_map.166 = (f32[512,2048]{1,0:T(8,128)}, f32[2048,512]{1,0:T(8,128)}, f32[2048,512]{1,0:T(8,128)}, f32[2048,512]{1,0:T(8,128)}, bf16[1024,2048]{1,0:T(8,128)(2,1)}, /*index=5*/f32[24,128]{1,0:T(8,128)}) custom-call(f32[512,2048]{1,0:T(8,128)} %fusion.47.refs_0_, f32[2048,512]{1,0:T(8,128)} %fusion.12.refs_1_, f32[2048,512]{1,0:T(8,128)} %fusion.15.refs_2_, ...), custom_call_target="tpu_custom_call" | custom-call | tf_op jit(solution)/shard_map/pallas_call | solution.py:749
  498.6 5.2 reshape.104
  503.9 5.2 reshape.105
  509.1 5.2 reshape.106
  515.5 4.9 copy.64
  (57 shorter events, 23.0 us)
Async XLA Ops:
  7.2 133.8 %all-gather.5.cloned.1.call-start = ((), (), s32[]{:S(2)}) async-start(), calls=%async_computation | async-start | bytes 10485760 | tf_op jit(solution)/shard_map/all_gather | solution.py:640
  8.0 235.9 %all-gather.11.cloned.1.call-start = ((), (), s32[]{:S(2)}) async-start(), calls=%async_computation.3 | async-start | bytes 5242880 | tf_op jit(solution)/shard_map/all_gather | solution.py:707
  8.1 6.7 %copy-start.5 = (bf16[1,1024,2048]{2,1,0:T(8,128)(2,1)S(1)}, bf16[1,1024,2048]{2,1,0:T(8,128)(2,1)}, u32[]{:S(2)}) copy-start(bf16[1,1024,2048]{2,1,0:T(8,128)(2,1)} %param.9) | copy-start | bytes 12582916
  8.1 6.7 %copy-start.10 = (bf16[2048,4,128]{2,1,0:T(4,128)(2,1)S(1)}, bf16[2048,4,128]{2,1,0:T(4,128)(2,1)}, u32[]{:S(2)}) copy-start(bf16[2048,4,128]{2,1,0:T(4,128)(2,1)} %param.11) | copy-start | bytes 6291460
  19.2 9.5 %copy-start.3 = (bf16[2048,4,128]{2,1,0:T(4,128)(2,1)S(1)}, bf16[2048,4,128]{2,1,0:T(4,128)(2,1)}, u32[]{:S(2)}) copy-start(bf16[2048,4,128]{2,1,0:T(4,128)(2,1)} %param.12) | copy-start | bytes 6291460
  140.7 105.5 %all-gather.9.cloned.1.call-start = ((), (), s32[]{:S(2)}) async-start(), calls=%async_computation.2 | async-start | bytes 5242880 | tf_op jit(solution)/shard_map/all_gather | solution.py:706
  141.0 6.2 %copy-start.7 = (f32[2048]{0:T(1024)S(1)}, f32[2048]{0:T(1024)}, u32[]{:S(2)}) copy-start(f32[2048]{0:T(1024)} %param.16) | copy-start | bytes 24580
  149.2 10.9 %copy-start = (bf16[256,2048]{1,0:T(8,128)(2,1)}, bf16[256,2048]{1,0:T(8,128)(2,1)S(1)}, u32[]{:S(2)}) copy-start(bf16[256,2048]{1,0:T(8,128)(2,1)S(1)} %get-tuple-element.55.refs_5_) | copy-start | bytes 3145732
  153.0 362.5 %all-gather.7.cloned.1.call-start = ((), (), s32[]{:S(2)}) async-start(), calls=%async_computation.1 | async-start | bytes 5242880 | tf_op jit(solution)/shard_map/all_gather | solution.py:708
  246.2 70.3 %copy-start.11 = (bf16[2048,4,128]{2,1,0:T(4,128)(2,1)S(1)}, bf16[2048,4,128]{2,1,0:T(4,128)(2,1)}, u32[]{:S(2)}) copy-start(bf16[2048,4,128]{2,1,0:T(4,128)(2,1)} %param.11) | copy-start | bytes 6291460
  316.5 3.8 copy-start.12
  316.5 3.8 copy-start.14
  320.3 2.4 copy-start.9
  322.7 5.9 %copy-start.6 = (bf16[1,1024,2048]{2,1,0:T(8,128)(2,1)S(1)}, bf16[1,1024,2048]{2,1,0:T(8,128)(2,1)}, u32[]{:S(2)}) copy-start(bf16[1,1024,2048]{2,1,0:T(8,128)(2,1)} %param.9) | copy-start | bytes 12582916
  328.6 4.4 copy-start.13
  333.0 4.7 copy-start.4
  509.1 5.2 copy-start.8
  515.5 4.9 copy-start.2
  520.5 3.7 copy-start.1
Sparse Core Ops, SparseCore 0:
  9.6 84.8 all-gather.4
  140.9 57.5 all-gather.10
  200.0 46.1 all-gather.8
  247.6 45.9 all-gather.6

commit v4 on v3

--- a/solution.py
+++ b/solution.py
@@ -13,6 +13,8 @@
 LOG2E = 1.4426950408889634
 LIMIT = 56 << 20
 LANES = 128
+FAR_A, FAR_B, NEAR_L, NEAR_R, SUM_L, SUM_R, OUT_L, OUT_R, RELAY_L, RELAY_R = range(10)
+PARTS = tuple(zip((RELAY_L, RELAY_R), range(2)))
 VMEM = pltpu.VMEM
 MESH = pl.DeviceIdType.MESH
 NT = (((1,), (1,)), ((), ()))
@@ -27,19 +29,20 @@
     return jnp.cos(angles), jnp.where(lane < half_dim, -1.0, 1.0) * jnp.sin(angles)
 
 
-def vmem_call(kernel, out_shape, n_in, scratch, collective_id=None, limit=LIMIT, cost=None):
-    params = dict(vmem_limit_bytes=limit)
-    if collective_id is not None:
-        params.update(collective_id=collective_id, has_side_effects=True)
+def vmem_call(kernel, out_shape, n_in, scratch, collective_id, n_any=0):
+    n_out = len(out_shape) - n_any
     return pl.pallas_call(
         kernel,
         out_shape=out_shape,
         in_specs=[pl.BlockSpec(memory_space=VMEM)] * n_in,
-        out_specs=[pl.BlockSpec(memory_space=VMEM)] * len(out_shape),
+        out_specs=[pl.BlockSpec(memory_space=VMEM)] * n_out + [pl.BlockSpec(memory_space=pl.ANY)] * n_any,
         scratch_shapes=scratch,
-        compiler_params=pltpu.CompilerParams(**params),
-        cost_estimate=cost,
+        compiler_params=pltpu.CompilerParams(vmem_limit_bytes=LIMIT, collective_id=collective_id, has_side_effects=True),
     )
+
+
+def block_of(ref, index, size):
+    return ref.at[pl.ds(pl.multiple_of(index * size, size), size), :]
 
 
 def remote(src, dst, send_sem, recv_sem, device_id):
@@ -92,7 +95,7 @@
     pl.semaphore_wait(barrier, tp_size * cp_size - 1)
 
 
-def scatter_qkv(heads, tp_size, cp_size, width, q_lin, k_lin, v_in, vec, q_gain, k_gain, cos_t, sin_t, q_out, k_out, v_out, inv_out, q16, k16, got, loc, qs, qr, ks, kr, vs, vr, fks, fkr, fvs, fvr, ts, tr):
+def scatter_qkv(heads, tp_size, cp_size, width, q_lin, k_lin, v_in, vec, q_gain, k_gain, cos_t, sin_t, wo_in, q_out, k_out, v_out, inv_out, wo_out, q16, k16, got, loc, qs, qr, ks, kr, vs, vr, fks, fkr, fvs, fvr, ts, tr, ws, wr, wfs, wfr):
     me_tp = lax.axis_index("tp")
     me = lax.axis_index("cp")
     core = lax.rem(me, 2)
@@ -111,6 +114,13 @@
             sends.append(copy)
 
     spread(v_in, v_out, vs, vr)
+    shard = wo_in.shape[0]
+    keep = pltpu.make_async_copy(wo_in, block_of(wo_out, me_tp, shard), loc.at[4])
+    keep.start()
+    for r in range(1, tp_size):
+        copy = remote(block_of(wo_in, core, shard // 2), block_of(wo_out, me_tp * 2 + core, shard // 2), ws.at[r], wr.at[r], {"tp": lax.rem(me_tp + r, tp_size)})
+        copy.start()
+        sends.append(copy)
     inv_out[...] = lax.rsqrt(finish() / width + NORM_EPS)
     n_chunk = inv_out.shape[0] // 2
     inv_cols = inv_out[...].T
@@ -152,8 +162,14 @@
             copy = remote(buf.at[src], buf.at[src], fs.at[r], fr.at[r], partner)
             copy.start()
             forwards.append(copy)
-    for copy in own[2:]:
+    for copy in own[2:] + [keep]:
         copy.wait()
+    for r in range(1, tp_size):
+        part = block_of(wo_out, lax.rem(me_tp - r + tp_size, tp_size) * 2 + core, shard // 2)
+        remote(part, part, ws.at[r], wr.at[r], partner).wait_recv()
+        copy = remote(part, part, wfs.at[r], wfr.at[r], partner)
+        copy.start()
+        forwards.append(copy)
     for copy in sends:
         copy.wait_send()
     for r in range(1, cp_size):
@@ -231,53 +247,6 @@
     step(s_b, mx_b, blk, 1, None)
     o_ref[0] = (acc_scr[...] / l_scr[...]).T.astype(o_ref.dtype)
     lse_ref[0] = m_scr[...] * coef + jnp.log2(l_scr[...])
-
-
-def attend_back(sub, scale, q_ref, k_ref, v_ref, o_ref, do_ref, lse_ref, dq_ref, dk_ref, dv_ref, kt_scr, dqt_scr, dl_scr):
-    blk = pl.program_id(0)
-    core = lax.rem(lax.axis_index("cp"), 2)
-    coef = scale * LOG2E
-    rows = q_ref.shape[1]
-    block_len = k_ref.shape[1]
-    kt_scr[blk] = k_ref[blk].T
-    prod = o_ref[0].astype(jnp.float32) * do_ref[0].astype(jnp.float32)
-    dl_scr[...] = jnp.sum(prod.T, axis=0, keepdims=True)
-    dqt_scr[...] = jnp.zeros_like(dqt_scr)
-
-    def step(b, masked):
-        q = q_ref[0]
-        do = do_ref[0]
-        lse = lse_ref[0]
-        delta = dl_scr[...]
-        for part in range(block_len // sub):
-            kv = slice(part * sub, (part + 1) * sub)
-            k_blk = k_ref[b, kv, :]
-            s = lax.dot_general(k_blk, q, NT, preferred_element_type=jnp.float32)
-            p = jnp.exp2(s * coef - lse)
-            if masked:
-                kv_pos = part * sub + lax.broadcasted_iota(jnp.int32, (sub, rows), 0)
-                col = lax.broadcasted_iota(jnp.int32, (sub, rows), 1)
-                q_pos = jnp.where(col < sub, core * sub + col, (2 - core) * sub + col)
-                p = jnp.where(kv_pos <= q_pos, p, 0.0)
-            dp = lax.dot_general(v_ref[b, kv, :], do, NT, preferred_element_type=jnp.float32)
-            ds = (p * (dp - delta)).astype(jnp.bfloat16)
-            new_v = jnp.dot(p.astype(jnp.bfloat16), do, preferred_element_type=jnp.float32)
-            new_k = jnp.dot(ds, q, preferred_element_type=jnp.float32) * scale
-            if masked:
-                dv_ref[b, kv, :] = new_v
-                dk_ref[b, kv, :] = new_k
-            else:
-                dv_ref[b, kv, :] += new_v
-                dk_ref[b, kv, :] += new_k
-            dqt_scr[...] += jnp.dot(kt_scr[b, :, kv], ds, preferred_element_type=jnp.float32)
-
-    def body(b, carry):
-        step(b, False)
-        return carry
-
-    step(blk, True)
-    lax.fori_loop(0, blk, body, 0)
-    dq_ref[0] = dqt_scr[...].T * scale
 
 
 def heads_to_rows(heads, tp_size, cp_size, o_in, o_out, ss, rs):
@@ -338,104 +307,180 @@
                     pl.when(row_core == core)(pltpu.make_async_copy(src, place, rs.at[me_cp, slot]).start)
 
 
-def gather_grads(heads, tp_size, cp_size, width, dq_in, dk_in, dv_in, q_lin, k_lin, inv, q_gain, k_gain, cos_t, sin_t, dq_out, dk_out, dv_out, gain_out, dq, dk, pk, pv, sk, sv, part, got, loc, qs, qr, pks, pkr, pvs, pvr, ks, kr, vs, vr, ts, tr):
+def attend_back(heads, tp_size, cp_size, width, scale, q_ref, k_ref, v_ref, o_ref, do_ref, lse_ref, q_lin, k_lin, inv, q_gain, k_gain, cos_t, sin_t, gp_in, or_in,
+                dq_out, dk_out, dv_out, gain_out, gp_out, oo_out,
+                kt_scr, dqt_scr, dl_scr, dqs, acc_k, acc_v, dq, dk, pk, pv, sk, sv, part, got, loc, qs, qr, pks, pkr, pvs, pvr, ks, kr, vs, vr, ts, tr, gs, gr, os, orr):
     me_tp = lax.axis_index("tp")
     me = lax.axis_index("cp")
     core = lax.rem(me, 2)
     chip = me // 2
-    sub = dq_in.shape[1] // 2
+    rows = q_ref.shape[1]
+    sub = rows // 2
+    block_len = k_ref.shape[1]
+    coef = scale * LOG2E
+    f32 = jnp.float32
+    partner = {"cp": me + 1 - 2 * core}
     cross_barrier(me_tp, me, tp_size, cp_size)
-    partner = {"cp": me + 1 - 2 * core}
-    order = (1, heads - 1, 2, 0)
-    pair, sends, own = [], [], []
-    for i, r in enumerate(order):
-        x = lax.rem(chip + r, heads)
-        for src, dst, ss, rs in ((dk_in, pk, pks, pkr), (dv_in, pv, pvs, pvr)):
-            copy = remote(src.at[2 * x + 1 - core], dst.at[x], ss.at[i], rs.at[i], partner)
+    sends = []
+    loc_width = heads * LANES
+    own = [
+        pltpu.make_async_copy(gp_in, block_of(gp_out, me_tp, sub), loc.at[4]),
+        pltpu.make_async_copy(or_in.at[:, pl.ds(pl.multiple_of(me_tp * loc_width, loc_width), loc_width)], block_of(oo_out, me_tp, sub), loc.at[5]),
+    ]
+    for r in range(1, tp_size):
+        dst = lax.rem(me_tp + r, tp_size)
+        sends.append(remote(gp_in, block_of(gp_out, me_tp, sub), gs.at[r], gr.at[r], {"tp": dst}))
+        sends.append(remote(or_in.at[:, pl.ds(pl.multiple_of(dst * loc_width, loc_width), loc_width)], block_of(oo_out, me_tp, sub), os.at[r], orr.at[r], {"tp": dst}))
+    for copy in own + sends:
+        copy.start()
+
+    def prepare(i, carry):
+        kt_scr[i] = k_ref[i].T
+        prod = o_ref[i].astype(f32) * do_ref[i].astype(f32)
+        dl_scr[i] = jnp.sum(prod.T, axis=0, keepdims=True)
+        dqt_scr[i] = jnp.zeros((LANES, rows), f32)
+        return carry
+
+    lax.fori_loop(0, cp_size, prepare, 0)
+
+    def tile(i, b, s, e, masked):
+        q = q_ref[i]
+        do = do_ref[i]
+        lse = lse_ref[i]
+        delta = dl_scr[i]
+        for j in range(block_len // sub):
+            kv = slice(j * sub, (j + 1) * sub)
+            scores = lax.dot_general(k_ref[b, kv, :], q, NT, preferred_element_type=f32)
+            p = jnp.exp2(scores * coef - lse)
+            if masked:
+                kv_pos = j * sub + lax.broadcasted_iota(jnp.int32, (sub, rows), 0)
+                col = lax.broadcasted_iota(jnp.int32, (sub, rows), 1)
+                q_pos = jnp.where(col < sub, core * sub + col, (2 - core) * sub + col)
+                p = jnp.where(kv_pos <= q_pos, p, 0.0)
+            dp = lax.dot_general(v_ref[b, kv, :], do, NT, preferred_element_type=f32)
+            ds = (p * (dp - delta)).astype(jnp.bfloat16)
+            for acc, left, right in ((acc_v, p.astype(jnp.bfloat16), do), (acc_k, ds, q)):
+                new = jnp.dot(left, right, preferred_element_type=f32)
+                acc[s, e, kv, :] = new if masked else acc[s, e, kv, :] + new
+            dqt_scr[i] += jnp.dot(kt_scr[b, :, kv], ds, preferred_element_type=f32)
+
+    def pair_copies(s):
+        return [remote(acc.at[s, 1 - core], dst.at[s], ss.at[s], rs.at[s], partner) for acc, dst, ss, rs in ((acc_k, pk, pks, pkr), (acc_v, pv, pvs, pvr))]
+
+    def home_copies(s):
+        dst = {"cp": lax.rem(chip + 1 + s, heads) * 2 + core}
+        return [remote(src.at[s], cols(out, chip), ss.at[s], rs.at[s], dst) for src, out, ss, rs in ((sk, dk, ks, kr), (sv, dv_out, vs, vr))]
+
+    def add_pair(s):
+        for copy in pair_copies(s):
+            copy.wait()
+        sk[s] = (acc_k[s, core] + pk[s]) * scale
+        sv[s] = (acc_v[s, core] + pv[s]).astype(sv.dtype)
+
+    def key_pair(s, carry):
+        def key_block(e, inner):
+            b = lax.rem(chip + 1 + s, heads) * 2 + e
+            tile(b, b, s, e, True)
+
+            def full(i, last):
+                tile(i, b, s, e, False)
+                return last
+
+            return lax.fori_loop(b + 1, cp_size, full, inner)
+
+        lax.fori_loop(0, 2, key_block, 0)
+        for copy in pair_copies(s):
             copy.start()
-            pair.append(copy)
+
+        @pl.when(s > 0)
+        def _():
+            add_pair(s - 1)
+            for copy in home_copies(s - 1):
+                copy.start()
+
+        return carry
+
+    lax.fori_loop(0, heads, key_pair, 0)
     for r in range(cp_size):
         dst = lax.rem(me + r, cp_size)
+        dqs[dst] = dqt_scr[dst].T * scale
         for s in range(2):
-            src = dq_in.at[dst, s * sub : (s + 1) * sub, :]
+            src = dqs.at[dst, s * sub : (s + 1) * sub, :]
             place = cols(dq, chip, sub_rows(core, s, sub))
             if r == 0:
-                own.append(pltpu.make_async_copy(src, place, loc.at[s]))
-                own[s].start()
+                copy = pltpu.make_async_copy(src, place, loc.at[s])
+                own.append(copy)
             else:
                 copy = remote(src, place, qs.at[r, s], qr.at[r, s], {"cp": dst})
-                copy.start()
-                sends.append(copy)
-    for i, r in enumerate(order):
-        x = lax.rem(chip + r, heads)
-        pair[2 * i].wait()
-        pair[2 * i + 1].wait()
-        sk[x] = dk_in[2 * x + core] + pk[x]
-        sv[x] = (dv_in[2 * x + core] + pv[x]).astype(sv.dtype)
-        for j, (src, out, ss, rs) in enumerate(((sk, dk, ks, kr), (sv, dv_out, vs, vr))):
-            if r == 0:
-                copy = pltpu.make_async_copy(src.at[x], cols(out, chip), loc.at[2 + j])
-                own.append(copy)
-            else:
-                copy = remote(src.at[x], cols(out, chip), ss.at[r], rs.at[r], {"cp": x * 2 + core})
                 sends.append(copy)
             copy.start()
+    last = heads - 1
+    add_pair(last)
+    for j, (src, out) in enumerate(((sk, dk), (sv, dv_out))):
+        copy = pltpu.make_async_copy(src.at[last], cols(out, chip), loc.at[2 + j])
+        copy.start()
+        own.append(copy)
     for copy in own:
         copy.wait()
+    inv_cols = inv[...].T
+    n_chunk = inv.shape[0] // 2
+    dots = []
+
+    def first_pass(i, grad, lin, gain):
+        gains = [jnp.zeros((1, LANES), f32)] * heads
+        for r in range(n_chunk):
+            part_rows = slice(r * LANES, (r + 1) * LANES)
+            c = i * n_chunk + r
+            norm = inv_cols[:, c : c + 1]
+            total = jnp.zeros((LANES, LANES), f32)
+            for h in range(heads):
+                lanes = slice(h * LANES, (h + 1) * LANES)
+                hat = lin[part_rows, lanes] * norm
+                back = rolled(grad[part_rows, lanes], cos_t[part_rows, :], -sin_t[part_rows, :])
+                both = back * hat
+                gains[h] = gains[h] + jnp.sum(both, axis=0, keepdims=True)
+                total = total + both * gain[:, lanes]
+                grad[part_rows, lanes] = back * gain[:, lanes]
+            dots.append(jnp.sum(total, axis=1, keepdims=True))
+        for h in range(heads):
+            gain_out[i * heads + h : i * heads + h + 1, :] = gains[h]
+
+    for s in range(last):
+        place = cols(dk, lax.rem(chip - 1 - s + heads, heads))
+        remote(place, place, ks.at[s], kr.at[s], partner).wait_recv()
+    first_pass(1, dk, k_lin, k_gain)
     for r in range(1, cp_size):
         src = lax.rem(me - r + cp_size, cp_size)
         for s in range(2):
             place = cols(dq, src // 2, sub_rows(lax.rem(src, 2), s, sub))
             remote(place, place, qs.at[r, s], qr.at[r, s], partner).wait_recv()
-    inv_cols = inv[...].T
-    n_chunk = inv.shape[0] // 2
-    dots = []
-
-    def first_pass(i, grad, lin, gain):
-        gains = [jnp.zeros((1, LANES), jnp.float32)] * heads
-        for r in range(n_chunk):
-            rows = slice(r * LANES, (r + 1) * LANES)
-            scale = inv_cols[:, i * n_chunk + r : i * n_chunk + r + 1]
-            total = jnp.zeros((LANES, LANES), jnp.float32)
-            for h in range(heads):
-                lanes = slice(h * LANES, (h + 1) * LANES)
-                hat = lin[rows, lanes] * scale
-                back = rolled(grad[rows, lanes], cos_t[rows, :], -sin_t[rows, :])
-                both = back * hat
-                gains[h] = gains[h] + jnp.sum(both, axis=0, keepdims=True)
-                total = total + both * gain[:, lanes]
-                grad[rows, lanes] = back * gain[:, lanes]
-            dots.append(jnp.sum(total, axis=1, keepdims=True))
-        for h in range(heads):
-            gain_out[i * heads + h : i * heads + h + 1, :] = gains[h]
-
     first_pass(0, dq, q_lin, q_gain)
-    for r in order[:-1]:
-        place = cols(dk, lax.rem(chip - r + heads, heads))
-        remote(place, place, ks.at[r], kr.at[r], partner).wait_recv()
-    first_pass(1, dk, k_lin, k_gain)
-    part[...] = jnp.concatenate(dots, axis=1).T
-    total_dots = share_over_tp(tp_size, me_tp, part, got, ts, tr)() / width
-    dot_cols = total_dots.T
+    part[...] = jnp.concatenate(dots[n_chunk:] + dots[:n_chunk], axis=1).T
+    dot_cols = (share_over_tp(tp_size, me_tp, part, got, ts, tr)() / width).T
     for i, (grad, lin, out) in enumerate(((dq, q_lin, dq_out), (dk, k_lin, dk_out))):
         for r in range(n_chunk):
-            rows = slice(r * LANES, (r + 1) * LANES)
+            part_rows = slice(r * LANES, (r + 1) * LANES)
             c = i * n_chunk + r
-            scale = inv_cols[:, c : c + 1]
-            out[rows, :] = (scale * (grad[rows, :] - lin[rows, :] * scale * dot_cols[:, c : c + 1])).astype(out.dtype)
+            norm = inv_cols[:, c : c + 1]
+            out[part_rows, :] = (norm * (grad[part_rows, :] - lin[part_rows, :] * norm * dot_cols[:, c : c + 1])).astype(out.dtype)
+    for s in range(last):
+        sends.extend(home_copies(s))
+        place = cols(dv_out, lax.rem(chip - 1 - s + heads, heads))
+        remote(place, place, vs.at[s], vr.at[s], partner).wait_recv()
+    for r in range(1, tp_size):
+        for out, ss, rs in ((gp_out, gs, gr), (oo_out, os, orr)):
+            place = block_of(out, lax.rem(me_tp - r + tp_size, tp_size), sub)
+            remote(place, place, ss.at[r], rs.at[r], partner).wait_recv()
     for copy in sends:
         copy.wait_send()
-    for r in order[:-1]:
-        place = cols(dv_out, lax.rem(chip - r + heads, heads))
-        remote(place, place, vs.at[r], vr.at[r], partner).wait_recv()
-
-
-def reduce_tail(tp_size, cp_size, n_heads, *refs):
+
+
+def reduce_tail(tp_size, cp_size, *refs):
     n_w = 4
-    w_in, (dx_in, dy_in, small) = refs[:n_w], refs[n_w : n_w + 3]
+    w_in, (dx_in, dy_in, small, y_in) = refs[:n_w], refs[n_w : 2 * n_w]
+    refs = refs[2 * n_w :]
+    w_out, (dx_out, y_out, small_out) = refs[:n_w], refs[n_w : n_w + 3]
     refs = refs[n_w + 3 :]
-    w_out, (dx_out, small_out) = refs[:n_w], refs[n_w : n_w + 2]
-    refs = refs[n_w + 2 :]
     acc, pair, far_a, far_b, fin_l, fin_r = (refs[i * n_w : (i + 1) * n_w] for i in range(6))
     refs = refs[6 * n_w :]
     dxa, dxb, dx_own, dx_fa, dx_fb, dx_fl, dx_fr, dx16, got_small, got_post, ss, rs, ps, pr, fs, fr, loc, sms, smr, gps, gpr = refs
@@ -449,7 +494,8 @@
     partner = {"cp": me_cp + 1 - 2 * core}
     to_l, to_r = {"cp": left * 2 + core}, {"cp": right * 2 + core}
     tp_l, tp_r = {"tp": t_left}, {"tp": t_right}
-    dx_i = n_w
+    dx_i, y_i = n_w, n_w + 1
+    outs = []
 
     def ring_sems(t, kind):
         return ss.at[t, kind], rs.at[t, kind]
@@ -487,10 +533,18 @@
 
     for r in range(1, cp_size):
         go(small, got_small.at[me_cp], sms.at[r], smr.at[r], {"cp": lax.rem(me_cp + r, cp_size)})
-    go(rows_of(dx_in, t_far, 0), dx_fa, *ring_sems(dx_i, 0), tp_l)
-    go(rows_of(dx_in, t_far, 1), dx_fb, *ring_sems(dx_i, 1), tp_r)
-    go(rows_of(dx_in, t_left, 1), half_of(dx_fr, 1), *ring_sems(dx_i, 2), tp_l)
-    go(rows_of(dx_in, t_right, 0), half_of(dx_fl, 0), *ring_sems(dx_i, 3), tp_r)
+    go(rows_of(dx_in, t_far, 0), dx_fa, *ring_sems(dx_i, FAR_A), tp_l)
+    go(rows_of(dx_in, t_far, 1), dx_fb, *ring_sems(dx_i, FAR_B), tp_r)
+    go(rows_of(dx_in, t_left, 1), half_of(dx_fr, 1), *ring_sems(dx_i, NEAR_L), tp_l)
+    go(rows_of(dx_in, t_right, 0), half_of(dx_fl, 0), *ring_sems(dx_i, NEAR_R), tp_r)
+    def give(src, stream, out, dev_l, dev_r):
+        copy = pltpu.make_async_copy(src, out, loc.at[stream, n_w])
+        copy.start()
+        outs.append(copy)
+        go(src, out, *ring_sems(stream, OUT_L), dev_l)
+        go(src, out, *ring_sems(stream, OUT_R), dev_r)
+
+    give(y_in, y_i, rows_of(y_out, me_tp), tp_l, tp_r)
     order = (far, left, right, chip)
     loads = []
     for t in range(n_w):
@@ -512,10 +566,10 @@
             loads[t * 4 + i].wait()
             landed(pair[t].at[x], ps.at[t, i], pr.at[t, i])
             acc[t][x] += pair[t][x]
-        go(half_of(acc[t].at[far], 0), far_a[t], *ring_sems(t, 0), to_l)
-        go(half_of(acc[t].at[far], 1), far_b[t], *ring_sems(t, 1), to_r)
-        go(half_of(acc[t].at[left], 1), half_of(fin_r[t], 1), *ring_sems(t, 2), to_l)
-        go(half_of(acc[t].at[right], 0), half_of(fin_l[t], 0), *ring_sems(t, 3), to_r)
+        go(half_of(acc[t].at[far], 0), far_a[t], *ring_sems(t, FAR_A), to_l)
+        go(half_of(acc[t].at[far], 1), far_b[t], *ring_sems(t, FAR_B), to_r)
+        go(half_of(acc[t].at[left], 1), half_of(fin_r[t], 1), *ring_sems(t, NEAR_L), to_l)
+        go(half_of(acc[t].at[right], 0), half_of(fin_l[t], 0), *ring_sems(t, NEAR_R), to_r)
 
     got_small[me_cp] = small[...]
     for r in range(1, cp_size):
@@ -528,18 +582,18 @@
 
     def second_half(t, acc_l, acc_r, fa, fb, fl, fr, dev_l, dev_r):
         half = fa.shape[0]
-        landed(fa, *ring_sems(t, 0))
+        landed(fa, *ring_sems(t, FAR_A))
         acc_l[...] += fa[...]
-        landed(fb, *ring_sems(t, 1))
+        landed(fb, *ring_sems(t, FAR_B))
         acc_r[...] += fb[...]
-        go(acc_l, half_of(fr, 0), *ring_sems(t, 4), dev_l)
-        go(acc_r, half_of(fl, 1), *ring_sems(t, 5), dev_r)
+        go(acc_l, half_of(fr, 0), *ring_sems(t, SUM_L), dev_l)
+        go(acc_r, half_of(fl, 1), *ring_sems(t, SUM_R), dev_r)
 
     def all_landed(t, fl, fr):
-        landed(half_of(fr, 1), *ring_sems(t, 2))
-        landed(half_of(fl, 0), *ring_sems(t, 3))
-        landed(half_of(fr, 0), *ring_sems(t, 4))
-        landed(half_of(fl, 1), *ring_sems(t, 5))
+        landed(half_of(fr, 1), *ring_sems(t, NEAR_L))
+        landed(half_of(fl, 0), *ring_sems(t, NEAR_R))
+        landed(half_of(fr, 0), *ring_sems(t, SUM_L))
+        landed(half_of(fl, 1), *ring_sems(t, SUM_R))
 
     for t in range(n_w):
         second_half(t, half_of(acc[t].at[left], 0), half_of(acc[t].at[right], 1), far_a[t], far_b[t], fin_l[t], fin_r[t], to_l, to_r)
@@ -550,43 +604,30 @@
     for r in range(1, tp_size):
         go(post, got_post.at[r], gps.at[r], gpr.at[r], {"tp": lax.rem(me_tp + r, tp_size)})
 
-    outs = []
     for t in range(n_w):
         all_landed(t, fin_l[t], fin_r[t])
         acc[t][chip] = acc[t][chip] + (fin_l[t][...] + fin_r[t][...])
         src = acc[t].at[chip]
         dst = piece(w_out[t], t, chip, core)
-        copy = pltpu.make_async_copy(src, dst, loc.at[t, 4])
-        copy.start()
-        outs.append(copy)
-        go(src, dst, *ring_sems(t, 6), to_l)
-        go(src, dst, *ring_sems(t, 7), to_r)
+        give(src, t, dst, to_l, to_r)
         go(src, dst, *pair_sems(t, 0), partner)
     all_landed(dx_i, dx_fl, dx_fr)
     dx16[...] = (dx_own[...] + (dx_fl[...] + dx_fr[...]) + dy_in[...].astype(jnp.float32)).astype(dx16.dtype)
-    copy = pltpu.make_async_copy(dx16, rows_of(dx_out, me_tp), loc.at[n_w, 4])
-    copy.start()
-    outs.append(copy)
-    go(dx16, rows_of(dx_out, me_tp), *ring_sems(dx_i, 6), tp_l)
-    go(dx16, rows_of(dx_out, me_tp), *ring_sems(dx_i, 7), tp_r)
+    give(dx16, dx_i, rows_of(dx_out, me_tp), tp_l, tp_r)
+
+    def relay(stream, part_of, x_l, x_r, dev_l, dev_r, pass_on):
+        for arrived, x, kind, part, dev in ((OUT_L, x_r, RELAY_L, 0, dev_l), (OUT_R, x_l, RELAY_R, 1, dev_r)):
+            whole = part_of(x)
+            landed(whole, *ring_sems(stream, arrived))
+            half = part_of(x, part)
+            go(half, half, *ring_sems(stream, kind), dev)
+            if pass_on:
+                go(whole, whole, *pair_sems(stream, 1 + part), partner)
 
     for t in range(n_w):
-        landed(piece(w_out[t], t, right, core), *ring_sems(t, 6))
-        half = piece(w_out[t], t, right, core, 0)
-        go(half, half, *ring_sems(t, 8), to_l)
-        whole = piece(w_out[t], t, right, core)
-        go(whole, whole, *pair_sems(t, 1), partner)
-        landed(piece(w_out[t], t, left, core), *ring_sems(t, 7))
-        half = piece(w_out[t], t, left, core, 1)
-        go(half, half, *ring_sems(t, 9), to_r)
-        whole = piece(w_out[t], t, left, core)
-        go(whole, whole, *pair_sems(t, 2), partner)
-    landed(rows_of(dx_out, t_right), *ring_sems(dx_i, 6))
-    half = rows_of(dx_out, t_right, 0)
-    go(half, half, *ring_sems(dx_i, 8), tp_l)
-    landed(rows_of(dx_out, t_left), *ring_sems(dx_i, 7))
-    half = rows_of(dx_out, t_left, 1)
-    go(half, half, *ring_sems(dx_i, 9), tp_r)
+        relay(t, functools.partial(lambda ref, t, x, part=None: piece(ref, t, x, core, part), w_out[t], t), left, right, to_l, to_r, True)
+    for stream, out in ((y_i, y_out), (dx_i, dx_out)):
+        relay(stream, functools.partial(rows_of, out), t_left, t_right, tp_l, tp_r, False)
 
     sums = small_out[n_gain:, :]
     for r in range(1, tp_size):
@@ -594,12 +635,13 @@
     sums = (sums + got_post[2]) + (got_post[1] + got_post[3])
 
     for t in range(n_w):
-        for kind, part in ((8, 0), (9, 1)):
+        for kind, part in PARTS:
             half = piece(w_out[t], t, far, core, part)
             landed(half, *ring_sems(t, kind))
             go(half, half, *pair_sems(t, 3 + part), partner)
-    for kind, part in ((8, 0), (9, 1)):
-        landed(rows_of(dx_out, t_far, part), *ring_sems(dx_i, kind))
+    for stream, out in ((y_i, y_out), (dx_i, dx_out)):
+        for kind, part in PARTS:
+            landed(rows_of(out, t_far, part), *ring_sems(stream, kind))
     for t in range(n_w):
         for i, x in enumerate((chip, right, left)):
             landed(piece(w_out[t], t, x, 1 - core), *pair_sems(t, i))
@@ -637,7 +679,6 @@
         cos_tab, sin_tab = rope_tables(cp_index * block_len, block_len, head_dim)
         x_loc = x_in[0]
         dy_loc = grad_y[0]
-        w_o_full = lax.all_gather(w_o.reshape(-1, d_model), "tp", axis=0, tiled=True)
         w_q2, w_k2, w_v2 = (w.reshape(d_model, -1) for w in (w_q, w_k, w_v))
         gains = [g.reshape(1, -1) for g in (q_norm_w, k_norm_w)]
         loc_width = heads * head_dim
@@ -650,13 +691,14 @@
         kv_shape = jax.ShapeDtypeStruct((cp_size, block_len, head_dim), b16)
         lin16 = VMEM((block_len, loc_width), b16)
         tp_scratch = VMEM((tp_size,) + vec.shape, f32)
-        q_all, k_all, v_all, inv = vmem_call(
+        q_all, k_all, v_all, inv, w_o_full = vmem_call(
             functools.partial(scatter_qkv, heads, tp_size, cp_size, width),
-            [jax.ShapeDtypeStruct((cp_size, rows, head_dim), b16), kv_shape, kv_shape, vec_shape],
-            8,
-            [lin16, lin16, tp_scratch, dma((4,))] + [dma((cp_size, 2))] * 2 + [dma((heads,))] * 8 + [dma((tp_size,))] * 2,
-            collective_id=0,
-        )(q_lin, k_lin, v_val, vec, *gains, cos_tab, sin_tab)
+            [jax.ShapeDtypeStruct((cp_size, rows, head_dim), b16), kv_shape, kv_shape, vec_shape, jax.ShapeDtypeStruct((width, d_model), b16)],
+            9,
+            [lin16, lin16, tp_scratch, dma((5,))] + [dma((cp_size, 2))] * 2 + [dma((heads,))] * 8 + [dma((tp_size,))] * 6,
+            0,
+            1,
+        )(q_lin, k_lin, v_val, vec, *gains, cos_tab, sin_tab, w_o.reshape(-1, d_model))
 
         qspec = pl.BlockSpec((1, rows, head_dim), lambda i: (i, 0, 0))
         lspec = pl.BlockSpec((1, 1, rows), lambda i: (i, 0, 0))
@@ -680,7 +722,7 @@
             [jax.ShapeDtypeStruct((sub, width), b16)],
             1,
             [dma((2, cp_size)), dma((n_heads,))],
-            collective_id=1,
+            1,
         )(o_all)[0]
 
         x_rows = lax.dynamic_slice_in_dim(x_loc, tp_index * sub, sub, 0)
@@ -700,36 +742,22 @@
             [jax.ShapeDtypeStruct((cp_size, rows, head_dim), b16)],
             1,
             [dma((tp_size, heads)), dma((cp_size, 2))],
-            collective_id=2,
+            2,
         )(do_rows)[0]
 
-        grad_proj = lax.all_gather(gp_rows, "tp", axis=0, tiled=True)
-        o_gath = lax.all_gather(o_rows, "tp", axis=0, tiled=True)
-        y_out = lax.all_gather(y_rows, "tp", axis=0, tiled=True)
-
-        dq_all, dk_all, dv_all = pl.pallas_call(
-            functools.partial(attend_back, sub, scale),
-            grid=(cp_size,),
-            in_specs=[qspec, whole, whole, qspec, qspec, lspec],
-            out_specs=[qspec, whole, whole],
-            out_shape=[jax.ShapeDtypeStruct((cp_size, rows, head_dim), f32)] + [jax.ShapeDtypeStruct((cp_size, block_len, head_dim), f32)] * 2,
-            scratch_shapes=[VMEM((cp_size, head_dim, block_len), b16), VMEM((head_dim, rows), f32), VMEM((1, rows), f32)],
-            compiler_params=pltpu.CompilerParams(vmem_limit_bytes=LIMIT),
-            cost_estimate=pl.CostEstimate(flops=5 * pair_flops, bytes_accessed=16 << 20, transcendentals=0),
-        )(q_all, k_all, v_all, o_all, do_all, lse)
-
-        dq_all, grad_proj, o_gath = lax.optimization_barrier((dq_all, grad_proj, o_gath))
-        lin_f, lin_h = VMEM((block_len, loc_width), f32), jax.ShapeDtypeStruct((block_len, loc_width), b16)
+        lin_h, f_lin = jax.ShapeDtypeStruct((block_len, loc_width), b16), VMEM((block_len, loc_width), f32)
         head_f = VMEM((heads, block_len, head_dim), f32)
-        dq16, dk16, dv16, gain_grads = vmem_call(
-            functools.partial(gather_grads, heads, tp_size, cp_size, width),
-            [lin_h, lin_h, lin_h, jax.ShapeDtypeStruct((2 * heads, head_dim), f32)],
-            10,
-            [lin_f, lin_f, head_f, head_f, head_f, VMEM((heads, block_len, head_dim), b16), VMEM(vec.shape, f32), tp_scratch, dma((4,))]
-            + [dma((cp_size, 2))] * 2 + [dma((heads,))] * 8 + [dma((tp_size,))] * 2,
-            collective_id=3,
-        )(dq_all, dk_all, dv_all, q_lin, k_lin, inv, *gains, cos_tab, sin_tab)
-        o_own = lax.dynamic_slice_in_dim(o_gath, tp_index * loc_width, loc_width, 1)
+        pair_f = VMEM((heads, 2, block_len, head_dim), f32)
+        dq16, dk16, dv16, gain_grads, grad_proj, o_own = vmem_call(
+            functools.partial(attend_back, heads, tp_size, cp_size, width, scale),
+            [lin_h, lin_h, lin_h, jax.ShapeDtypeStruct((2 * heads, head_dim), f32), jax.ShapeDtypeStruct((block_len, d_model), b16), lin_h],
+            15,
+            [VMEM((cp_size, head_dim, block_len), b16), VMEM((cp_size, head_dim, rows), f32), VMEM((cp_size, 1, rows), f32), VMEM((cp_size, rows, head_dim), f32)]
+            + [pair_f, pair_f, f_lin, f_lin, head_f, head_f, head_f, VMEM((heads, block_len, head_dim), b16), VMEM(vec.shape, f32), tp_scratch, dma((6,))]
+            + [dma((cp_size, 2))] * 2 + [dma((heads,))] * 8 + [dma((tp_size,))] * 6,
+            3,
+            2,
+        )(q_all, k_all, v_all, o_all, do_all, lse, q_lin, k_lin, inv, *gains, cos_tab, sin_tab, gp_rows, o_rows)
 
         def wgrad(left, right):
             return lax.dot_general(left, right, (((0,), (0,)), ((), ())), preferred_element_type=f32)
@@ -747,18 +775,18 @@
         ring = cp_size // 2
         rows_dx, half_dx = VMEM((sub, d_model), f32), VMEM((sub // 2, d_model), f32)
         res = pl.pallas_call(
-            functools.partial(reduce_tail, tp_size, cp_size, heads),
-            out_shape=[jax.ShapeDtypeStruct(w.shape, f32) for w in w_parts] + [jax.ShapeDtypeStruct((block_len, d_model), b16), jax.ShapeDtypeStruct(small.shape, f32)],
-            in_specs=[any_spec] * 5 + [vmem_spec] * 2,
-            out_specs=[any_spec] * 5 + [vmem_spec],
+            functools.partial(reduce_tail, tp_size, cp_size),
+            out_shape=[jax.ShapeDtypeStruct(w.shape, f32) for w in w_parts] + [jax.ShapeDtypeStruct((block_len, d_model), b16)] * 2 + [jax.ShapeDtypeStruct(small.shape, f32)],
+            in_specs=[any_spec] * 5 + [vmem_spec] * 3,
+            out_specs=[any_spec] * 6 + [vmem_spec],
             scratch_shapes=bufs((ring,), cp_size) * 2 + bufs((), 2 * cp_size) * 2 + bufs((), cp_size) * 2
             + [half_dx, half_dx, rows_dx, half_dx, half_dx, rows_dx, rows_dx, VMEM((sub, d_model), b16)]
             + [VMEM((cp_size,) + small.shape, f32), VMEM((tp_size, d_model // head_dim, head_dim), f32)]
-            + [dma((5, 10))] * 2 + [dma((4, 4))] * 2 + [dma((4, 5))] * 2 + [dma((5, 5))] + [dma((cp_size,))] * 2 + [dma((tp_size,))] * 2,
+            + [dma((6, 10))] * 2 + [dma((4, 4))] * 2 + [dma((4, 5))] * 2 + [dma((6, 5))] + [dma((cp_size,))] * 2 + [dma((tp_size,))] * 2,
             compiler_params=pltpu.CompilerParams(vmem_limit_bytes=LIMIT, collective_id=6, has_side_effects=True),
-        )(*w_parts, dx_part, dy_rows, small)
+        )(*w_parts, dx_part, dy_rows, small, y_rows)
         grad_w_v, grad_w_q, grad_w_k = (g.reshape(w_q.shape) for g in res[1:4])
-        grad_x, small_sum = res[4:]
+        grad_x, y_out, small_sum = res[4:]
         return (y_out[None], grad_x[None], grad_w_q, grad_w_k, grad_w_v, res[0].reshape(w_o.shape), small_sum[:heads], small_sum[heads : 2 * heads], small_sum[2 * heads :].reshape(-1))
 
     return jax.shard_map(local_run, mesh=mesh, in_specs=in_specs, out_specs=out_specs, check_vma=False)

time: 538 us -> 541 us (level)
  Pallas kernels: 410 us -> 432 us
  between operations: 14.4 us -> 1.03 us
    pallas_call x1, Pallas kernels: 49 us -> 67.4 us  [local_run(): vmem_call(functools.partial(scatter_qkv, heads, tp_size, cp_size, width),...]
    pallas_call x1, Pallas kernels: 36.2 us -> 46.3 us  [local_run(): pl.pallas_call(functools.partial(attend, sub, scale), grid=(cp_size,), in...]
    pallas_call x3 -> x2, Pallas kernels: 279 us -> 272 us  [the longest x1 159 us: local_run(): pl.pallas_call(functools.partial(reduce_tail, tp_size, cp_size), out_shap...]
  transfers between devices with their start and end apart: 4 -> 0, of which waited for: 1 -> 0; matrix products, arithmetic and copies ran while one was open for 18% -> 0% of each run, Pallas kernels for 77% -> 0%
where the time goes in v4:
time: 541 us; the launch traced here: 532 us
  Pallas kernels  432 us (80%)
  matrix products  58.2 us (11%)
  local copies, waits for them, and re-layouts  33.7 us (6%)
  other arithmetic  7.37 us (1%)
    pallas_call x1, Pallas kernels, local_run(): pl.pallas_call(functools.partial(reduce_tail, tp_size, cp_size), out_shap...  159 us
    pallas_call x1, Pallas kernels, local_run(): vmem_call(functools.partial(attend_back, heads, tp_size, cp_size, width,...  113 us
    pallas_call x1, Pallas kernels, local_run(): vmem_call(functools.partial(scatter_qkv, heads, tp_size, cp_size, width),...  67.4 us
    pallas_call x1, Pallas kernels, local_run(): pl.pallas_call(functools.partial(attend, sub, scale), grid=(cp_size,), in...  46.3 us
    pallas_call x1, Pallas kernels, local_run(): vmem_call(functools.partial(rows_to_heads, heads, tp_size, cp_size), [jax...  25.5 us
    pallas_call x1, Pallas kernels, local_run(): vmem_call(functools.partial(heads_to_rows, heads, tp_size, cp_size), [jax...  20.7 us
    dot_general x4, matrix products, wgrad(): lax.dot_general(left, right, (((0,), (0,)), ((), ())), preferred_element_...  20.6 us
    reshape x3, local copies, waits for them, and re-layouts, local_run(): grad_w_v, grad_w_q, grad_w_k = (g.reshape(w_q.shape) for g in res[1:4])  15.7 us

profile of v4, /device:TPU:97, one launch (start us, length us, event | category | flops | bytes accessed | tf_op | source)
XLA Modules:
  0.0 532.3 jit_solution(16346560508189241410)
XLA Ops:
  0.7 3.1 fusion.47
  3.8 6.3 %fusion.42.v_in = bf16[1024,512]{1,0:T(8,128)(2,1)} fusion(bf16[256,8,4,128]{3,2,1,0:T(4,128)(2,1)} %bitcast.88, bf16[1,1024,2048]{2,1,0:T(8,128)(2,1)} %param.9), kind=kOutput, calls=%fused_computation.44 | convolution fusion | flops 2148007936 | bytes 7340032 | tf_op jit(solution)/shard_map/dot_general | solution.py:688
  10.1 2.4 multiply_reduce_fusion.2
  14.3 5.2 multiply_reduce_fusion.1
  22.0 67.4 %shard_map.160 = (bf16[8,512,128]{2,1,0:T(8,128)(2,1)}, bf16[8,1024,128]{2,1,0:T(8,128)(2,1)}, bf16[8,1024,128]{2,1,0:T(8,128)(2,1)}, f32[16,128]{1,0:T(8,128)}, bf16[2048,2048]{1,0:T(8,128)(2,1)}) custom-call(f32[1024,512]{1,0:T(8,128)} %copy.18.q_lin, f32[1024,512]{1,0:T(8,128)} %copy.19.k_lin, bf16[1024,512]{1,0:T(8,128)(2,1)} %fusion.42.v_in, ...), custom_call_target="tpu_custom_call" | custom-call | tf_op jit(solution)/shard_map/pallas_call | solution.py:694
  89.4 46.3 %shard_map.161 = (bf16[8,512,128]{2,1,0:T(8,128)(2,1)}, f32[8,1,512]{2,1,0:T(1,128)}) custom-call(bf16[8,512,128]{2,1,0:T(8,128)(2,1)} %get-tuple-element.29.q_ref, bf16[8,1024,128]{2,1,0:T(8,128)(2,1)} %get-tuple-element.30.k_ref, bf16[8,1024,128]{2,1,0:T(8,128)(2,1)} %get-tuple-element.31.v_ref), custom_call_target="tpu_custom_call" | custom-call | flops 9663676416 | bytes 6291456 | tf_op jit(solution)/shard_map/pallas_call | solution.py:707
  135.6 20.7 %shard_map.162.or_in = bf16[256,2048]{1,0:T(8,128)(2,1)} custom-call(bf16[8,512,128]{2,1,0:T(8,128)(2,1)} %get-tuple-element.32.o_in.o_ref), custom_call_target="tpu_custom_call" | custom-call | tf_op jit(solution)/shard_map/pallas_call | solution.py:720
  156.4 6.3 %multiply_reduce_fusion = (f32[256]{0:T(256)S(1)}, f32[256,2048]{1,0:T(8,128)S(1)}) fusion(bf16[256,2048]{1,0:T(8,128)(2,1)} %shard_map.162.or_in, bf16[2048,2048]{1,0:T(8,128)(2,1)} %get-tuple-element.33), kind=kOutput, calls=%fused_computation.35 | convolution fusion | flops 2148531968 | bytes 11535360 | tf_op jit(solution)/shard_map/dot_general | solution.py:731
  162.7 3.1 fusion.26
  166.8 7.1 %convolution_convert_fusion.g_in = bf16[256,2048]{1,0:T(8,128)(2,1)} fusion(bf16[256,2048]{1,0:T(8,128)(2,1)S(1)} %fusion.25.gp_in, bf16[2048,2048]{1,0:T(8,128)(2,1)} %get-tuple-element.33), kind=kOutput, calls=%fused_computation.18 | convolution fusion | flops 2148007936 | bytes 10485760 | tf_op jit(solution)/shard_map/dot_general | solution.py:738
  173.9 25.5 %shard_map.163.do_ref = bf16[8,512,128]{2,1,0:T(8,128)(2,1)} custom-call(bf16[256,2048]{1,0:T(8,128)(2,1)} %convolution_convert_fusion.g_in), custom_call_target="tpu_custom_call" | custom-call | tf_op jit(solution)/shard_map/pallas_call | solution.py:740
  199.4 112.8 %shard_map.164 = (bf16[1024,512]{1,0:T(8,128)(2,1)}, bf16[1024,512]{1,0:T(8,128)(2,1)}, bf16[1024,512]{1,0:T(8,128)(2,1)}, f32[8,128]{1,0:T(8,128)}, bf16[1024,2...) custom-call(bf16[8,512,128]{2,1,0:T(8,128)(2,1)} %get-tuple-element.29.q_ref, bf16[8,1024,128]{2,1,0:T(8,128)(2,1)} %get-tuple-element.30.k_ref, ...), custom_call_target="tpu_custom_call" | custom-call | tf_op jit(solution)/shard_map/pallas_call | solution.py:751
  312.3 7.0 %fusion.52.refs_0_ = f32[512,2048]{1,0:T(8,128)} fusion(bf16[1024,512]{1,0:T(8,128)(2,1)} %get-tuple-element.36, bf16[1024,2048]{1,0:T(8,128)(2,1)} %get-tuple-element.37), kind=kOutput, calls=%fused_computation.61 | convolution fusion | flops 2147483648 | bytes 9437184 | tf_op jit(solution)/shard_map/dot_general | solution.py:763
  319.9 4.5 fusion.12.refs_1_
  324.3 4.5 fusion.15.refs_2_
  328.8 4.7 fusion.18.refs_3_
  333.4 2.4 fusion.29
  335.8 2.4 fusion.32
  338.2 5.6 %add_add_fusion.refs_4_ = f32[1024,2048]{1,0:T(8,128)} fusion(f32[1024,2048]{1,0:T(8,128)S(1)} %fusion.32, f32[1024,2048]{1,0:T(8,128)S(1)} %fusion.29, bf16[1024,512]{1,0:T(8,128)(2,1)S(1)} %copy-done.5, bf16[256,8,4,128]{3,2,1,0:T(4,128)(2,1)S(1)} %bitcast.89), kind=kOutput, calls=%fused_computation | convolution fusion | flops 2151677952 | bytes 28311552 | tf_op jit(solution)/shard_map/dot_general | solution.py:766
  343.8 159.4 %shard_map.165 = (f32[512,2048]{1,0:T(8,128)}, f32[2048,512]{1,0:T(8,128)}, f32[2048,512]{1,0:T(8,128)}, f32[2048,512]{1,0:T(8,128)}, bf16[1024,2048]{1,0:T(8,12...) custom-call(f32[512,2048]{1,0:T(8,128)} %fusion.52.refs_0_, f32[2048,512]{1,0:T(8,128)} %fusion.12.refs_1_, ...), custom_call_target="tpu_custom_call" | custom-call | tf_op jit(solution)/shard_map/pallas_call | solution.py:777
  505.8 5.2 reshape.104
  511.1 5.2 reshape.105
  516.3 5.2 reshape.106
  521.5 4.9 copy.64
  (44 shorter events, 14.3 us)
Async XLA Ops:
  3.7 6.3 %copy-start.6 = (bf16[1,1024,2048]{2,1,0:T(8,128)(2,1)S(1)}, bf16[1,1024,2048]{2,1,0:T(8,128)(2,1)}, u32[]{:S(2)}) copy-start(bf16[1,1024,2048]{2,1,0:T(8,128)(2,1)} %param.9) | copy-start | bytes 12582916
  3.8 6.3 %copy-start.11 = (bf16[2048,4,128]{2,1,0:T(4,128)(2,1)S(1)}, bf16[2048,4,128]{2,1,0:T(4,128)(2,1)}, u32[]{:S(2)}) copy-start(bf16[2048,4,128]{2,1,0:T(4,128)(2,1)} %param.10) | copy-start | bytes 6291460
  156.3 6.3 %copy-start.7 = (bf16[1,1024,2048]{2,1,0:T(8,128)(2,1)S(1)}, bf16[1,1024,2048]{2,1,0:T(8,128)(2,1)}, u32[]{:S(2)}) copy-start(bf16[1,1024,2048]{2,1,0:T(8,128)(2,1)} %param.9) | copy-start | bytes 12582916
  156.3 6.3 %copy-start.8 = (f32[2048]{0:T(1024)S(1)}, f32[2048]{0:T(1024)}, u32[]{:S(2)}) copy-start(f32[2048]{0:T(1024)} %param.16) | copy-start | bytes 24580
  165.8 1.0 copy-start
  166.8 7.1 %copy-start.3 = (bf16[256,2048]{1,0:T(8,128)(2,1)}, bf16[256,2048]{1,0:T(8,128)(2,1)S(1)}, u32[]{:S(2)}) copy-start(bf16[256,2048]{1,0:T(8,128)(2,1)S(1)} %fusion.25.gp_in) | copy-start | bytes 3145732
  312.2 7.0 %copy-start.9 = (f32[8,128]{1,0:T(8,128)S(1)}, f32[8,128]{1,0:T(8,128)}, u32[]{:S(2)}) copy-start(f32[8,128]{1,0:T(8,128)} %get-tuple-element.41) | copy-start | bytes 12292
  312.2 7.6 %copy-start.5 = (bf16[1024,512]{1,0:T(8,128)(2,1)S(1)}, bf16[1024,512]{1,0:T(8,128)(2,1)}, u32[]{:S(2)}) copy-start(bf16[1024,512]{1,0:T(8,128)(2,1)} %get-tuple-element.38) | copy-start | bytes 3145732
  319.8 4.5 copy-start.13
  324.3 4.5 copy-start.14
  328.8 4.7 copy-start.10
  333.4 2.4 copy-start.12
  335.8 2.4 copy-start.4
  521.5 4.9 copy-start.2
  526.4 3.7 copy-start.1

commit v5 on v4

--- a/solution.py
+++ b/solution.py
@@ -29,12 +29,12 @@
     return jnp.cos(angles), jnp.where(lane < half_dim, -1.0, 1.0) * jnp.sin(angles)
 
 
-def vmem_call(kernel, out_shape, n_in, scratch, collective_id, n_any=0):
+def vmem_call(kernel, out_shape, n_in, scratch, collective_id, n_any=0, n_any_in=0):
     n_out = len(out_shape) - n_any
     return pl.pallas_call(
         kernel,
         out_shape=out_shape,
-        in_specs=[pl.BlockSpec(memory_space=VMEM)] * n_in,
+        in_specs=[pl.BlockSpec(memory_space=VMEM)] * (n_in - n_any_in) + [pl.BlockSpec(memory_space=pl.ANY)] * n_any_in,
         out_specs=[pl.BlockSpec(memory_space=VMEM)] * n_out + [pl.BlockSpec(memory_space=pl.ANY)] * n_any,
         scratch_shapes=scratch,
         compiler_params=pltpu.CompilerParams(vmem_limit_bytes=LIMIT, collective_id=collective_id, has_side_effects=True),
@@ -95,7 +95,7 @@
     pl.semaphore_wait(barrier, tp_size * cp_size - 1)
 
 
-def scatter_qkv(heads, tp_size, cp_size, width, q_lin, k_lin, v_in, vec, q_gain, k_gain, cos_t, sin_t, wo_in, q_out, k_out, v_out, inv_out, wo_out, q16, k16, got, loc, qs, qr, ks, kr, vs, vr, fks, fkr, fvs, fvr, ts, tr, ws, wr, wfs, wfr):
+def scatter_qkv(heads, tp_size, cp_size, width, q_lin, k_lin, vec, q_gain, k_gain, cos_t, sin_t, wo_in, v_in, q_out, k_out, v_out, inv_out, wo_out, q16, k16, got, loc, qs, qr, ks, kr, vs, vr, fks, fkr, fvs, fvr, ts, tr, ws, wr, wfs, wfr):
     me_tp = lax.axis_index("tp")
     me = lax.axis_index("cp")
     core = lax.rem(me, 2)
@@ -117,8 +117,10 @@
     shard = wo_in.shape[0]
     keep = pltpu.make_async_copy(wo_in, block_of(wo_out, me_tp, shard), loc.at[4])
     keep.start()
-    for r in range(1, tp_size):
-        copy = remote(block_of(wo_in, core, shard // 2), block_of(wo_out, me_tp * 2 + core, shard // 2), ws.at[r], wr.at[r], {"tp": lax.rem(me_tp + r, tp_size)})
+    t_left, t_right, t_far = (lax.rem(me_tp + d, tp_size) for d in (tp_size - 1, 1, 2))
+    ways = tuple(enumerate(((t_right, t_left), (t_left, t_right))))
+    for k, (_, dst) in ways:
+        copy = remote(block_of(wo_in, core, shard // 2), block_of(wo_out, me_tp * 2 + core, shard // 2), ws.at[k], wr.at[k], {"tp": dst})
         copy.start()
         sends.append(copy)
     inv_out[...] = lax.rsqrt(finish() / width + NORM_EPS)
@@ -152,24 +154,37 @@
         copy.start()
     partner = {"cp": me + 1 - 2 * core}
     forwards = []
-    for r in (0,) + far_chips:
-        src = lax.rem(chip - r + heads, heads) * 2 + core
-        for i, (buf, ss, rs, fs, fr) in enumerate(((v_out, vs, vr, fvs, fvr), (k_out, ks, kr, fks, fkr))):
+
+    def pass_on(part, ss, rs):
+        copy = remote(part, part, ss, rs, partner)
+        copy.start()
+        forwards.append(copy)
+
+    def forward(local, buf, ss, rs, fs, fr):
+        for r in (0,) + far_chips:
+            src = lax.rem(chip - r + heads, heads) * 2 + core
             if r == 0:
-                own[1 - i].wait()
+                local.wait()
             else:
                 remote(buf.at[src], buf.at[src], ss.at[r], rs.at[r], partner).wait_recv()
-            copy = remote(buf.at[src], buf.at[src], fs.at[r], fr.at[r], partner)
-            copy.start()
-            forwards.append(copy)
+            pass_on(buf.at[src], fs.at[r], fr.at[r])
+
+    forward(own[1], v_out, vs, vr, fvs, fvr)
+    for k, (src, dst) in ways:
+        whole = block_of(wo_out, src * 2 + core, shard // 2)
+        remote(whole, whole, ws.at[k], wr.at[k], partner).wait_recv()
+        half = block_of(wo_out, (src * 2 + core) * 2 + k, shard // 4)
+        copy = remote(half, half, ws.at[2 + k], wr.at[2 + k], {"tp": dst})
+        copy.start()
+        sends.append(copy)
+        pass_on(whole, wfs.at[k], wfr.at[k])
+    forward(own[0], k_out, ks, kr, fks, fkr)
     for copy in own[2:] + [keep]:
         copy.wait()
-    for r in range(1, tp_size):
-        part = block_of(wo_out, lax.rem(me_tp - r + tp_size, tp_size) * 2 + core, shard // 2)
-        remote(part, part, ws.at[r], wr.at[r], partner).wait_recv()
-        copy = remote(part, part, wfs.at[r], wfr.at[r], partner)
-        copy.start()
-        forwards.append(copy)
+    for k, _ in ways:
+        half = block_of(wo_out, (t_far * 2 + core) * 2 + k, shard // 4)
+        remote(half, half, ws.at[2 + k], wr.at[2 + k], partner).wait_recv()
+        pass_on(half, wfs.at[2 + k], wfr.at[2 + k])
     for copy in sends:
         copy.wait_send()
     for r in range(1, cp_size):
@@ -180,14 +195,15 @@
         copy.wait()
 
 
-def attend(sub, scale, q_ref, k_ref, v_ref, o_ref, lse_ref, vt_scr, m_scr, l_scr, acc_scr, s_a, s_b, mx_a):
+def attend(sub, scale, q_ref, k_ref, v_ref, o_ref, lse_ref, k_scr, vt_scr, m_scr, l_scr, acc_scr, s_a, s_b, mx_a):
     blk = pl.program_id(0)
     core = lax.rem(lax.axis_index("cp"), 2)
     coef = scale * LOG2E
     half = k_ref.shape[1] // 2
     cols = q_ref.shape[1]
     chunk = half // 2
-    vt_scr[blk] = v_ref[blk].T
+    k_scr[blk] = k_ref[0]
+    vt_scr[blk] = v_ref[0].T
     m_scr[...] = jnp.full_like(m_scr, -jnp.inf)
     l_scr[...] = jnp.zeros_like(l_scr)
     acc_scr[...] = jnp.zeros_like(acc_scr)
@@ -197,7 +213,7 @@
 
     def scores(b, h, c):
         kv = slice(h * half + c * chunk, h * half + (c + 1) * chunk)
-        return lax.dot_general(k_ref[b, kv, :], q_ref[0], NT, preferred_element_type=jnp.float32)
+        return lax.dot_general(k_scr[b, kv, :], q_ref[0], NT, preferred_element_type=jnp.float32)
 
     def mask(s, h, c):
         kv_pos = h * half + c * chunk + lax.broadcasted_iota(jnp.int32, s.shape, 0)
@@ -307,9 +323,9 @@
                     pl.when(row_core == core)(pltpu.make_async_copy(src, place, rs.at[me_cp, slot]).start)
 
 
-def attend_back(heads, tp_size, cp_size, width, scale, q_ref, k_ref, v_ref, o_ref, do_ref, lse_ref, q_lin, k_lin, inv, q_gain, k_gain, cos_t, sin_t, gp_in, or_in,
+def attend_back(heads, tp_size, cp_size, width, scale, q_ref, k_ref, v_ref, o_ref, do_ref, lse_ref, inv, q_gain, k_gain, cos_t, sin_t, gp_in, or_in, q_hbm, k_hbm,
                 dq_out, dk_out, dv_out, gain_out, gp_out, oo_out,
-                kt_scr, dqt_scr, dl_scr, dqs, acc_k, acc_v, dq, dk, pk, pv, sk, sv, part, got, loc, qs, qr, pks, pkr, pvs, pvr, ks, kr, vs, vr, ts, tr, gs, gr, os, orr):
+                q_lin, k_lin, kt_scr, dqt_scr, dl_scr, dqs, acc_k, acc_v, dq, dk, pk, pv, sk, sv, part, got, loc, qs, qr, pks, pkr, pvs, pvr, ks, kr, vs, vr, ts, tr, gs, gr, os, orr):
     me_tp = lax.axis_index("tp")
     me = lax.axis_index("cp")
     core = lax.rem(me, 2)
@@ -326,13 +342,22 @@
     own = [
         pltpu.make_async_copy(gp_in, block_of(gp_out, me_tp, sub), loc.at[4]),
         pltpu.make_async_copy(or_in.at[:, pl.ds(pl.multiple_of(me_tp * loc_width, loc_width), loc_width)], block_of(oo_out, me_tp, sub), loc.at[5]),
+        pltpu.make_async_copy(q_hbm, q_lin, loc.at[6]),
+        pltpu.make_async_copy(k_hbm, k_lin, loc.at[7]),
     ]
     for r in range(1, tp_size):
         dst = lax.rem(me_tp + r, tp_size)
-        sends.append(remote(gp_in, block_of(gp_out, me_tp, sub), gs.at[r], gr.at[r], {"tp": dst}))
         sends.append(remote(or_in.at[:, pl.ds(pl.multiple_of(dst * loc_width, loc_width), loc_width)], block_of(oo_out, me_tp, sub), os.at[r], orr.at[r], {"tp": dst}))
+    t_left, t_right, t_far = (lax.rem(me_tp + d, tp_size) for d in (tp_size - 1, 1, 2))
+    ways = tuple(enumerate(((t_right, t_left), (t_left, t_right))))
+    for k, (_, dst) in ways:
+        sends.append(remote(gp_in, block_of(gp_out, me_tp, sub), gs.at[k], gr.at[k], {"tp": dst}))
     for copy in own + sends:
         copy.start()
+
+    def relay(k, src, dst):
+        half = block_of(gp_out, src * 2 + k, sub // 2)
+        return remote(half, half, gs.at[2 + k], gr.at[2 + k], {"tp": dst})
 
     def prepare(i, carry):
         kt_scr[i] = k_ref[i].T
@@ -391,6 +416,13 @@
         lax.fori_loop(0, 2, key_block, 0)
         for copy in pair_copies(s):
             copy.start()
+
+        @pl.when(s == 1)
+        def _():
+            for k, (src, dst) in ways:
+                whole = block_of(gp_out, src, sub)
+                remote(whole, whole, gs.at[k], gr.at[k], partner).wait_recv()
+                relay(k, src, dst).start()
 
         @pl.when(s > 0)
         def _():
@@ -468,9 +500,12 @@
         place = cols(dv_out, lax.rem(chip - 1 - s + heads, heads))
         remote(place, place, vs.at[s], vr.at[s], partner).wait_recv()
     for r in range(1, tp_size):
-        for out, ss, rs in ((gp_out, gs, gr), (oo_out, os, orr)):
-            place = block_of(out, lax.rem(me_tp - r + tp_size, tp_size), sub)
-            remote(place, place, ss.at[r], rs.at[r], partner).wait_recv()
+        place = block_of(oo_out, lax.rem(me_tp - r + tp_size, tp_size), sub)
+        remote(place, place, os.at[r], orr.at[r], partner).wait_recv()
+    for k, (src, dst) in ways:
+        sends.append(relay(k, src, dst))
+        half = block_of(gp_out, t_far * 2 + k, sub // 2)
+        remote(half, half, gs.at[2 + k], gr.at[2 + k], partner).wait_recv()
     for copy in sends:
         copy.wait_send()
 
@@ -698,19 +733,20 @@
             [lin16, lin16, tp_scratch, dma((5,))] + [dma((cp_size, 2))] * 2 + [dma((heads,))] * 8 + [dma((tp_size,))] * 6,
             0,
             1,
-        )(q_lin, k_lin, v_val, vec, *gains, cos_tab, sin_tab, w_o.reshape(-1, d_model))
+            1,
+        )(q_lin, k_lin, vec, *gains, cos_tab, sin_tab, w_o.reshape(-1, d_model), v_val)
 
         qspec = pl.BlockSpec((1, rows, head_dim), lambda i: (i, 0, 0))
         lspec = pl.BlockSpec((1, 1, rows), lambda i: (i, 0, 0))
-        whole = pl.BlockSpec(memory_space=VMEM)
+        kvspec = pl.BlockSpec((1, block_len, head_dim), lambda i: (i, 0, 0))
         pair_flops = cp_size * (cp_size + 1) // 2 * rows * block_len * head_dim * 2
         o_all, lse = pl.pallas_call(
             functools.partial(attend, sub, scale),
             grid=(cp_size,),
-            in_specs=[qspec, whole, whole],
+            in_specs=[qspec, kvspec, kvspec],
             out_specs=[qspec, lspec],
             out_shape=[jax.ShapeDtypeStruct((cp_size, rows, head_dim), b16), jax.ShapeDtypeStruct((cp_size, 1, rows), f32)],
-            scratch_shapes=[VMEM((cp_size, head_dim, block_len), b16), VMEM((1, rows), f32), VMEM((1, rows), f32), VMEM((head_dim, rows), f32)]
+            scratch_shapes=[VMEM((cp_size, block_len, head_dim), b16), VMEM((cp_size, head_dim, block_len), b16), VMEM((1, rows), f32), VMEM((1, rows), f32), VMEM((head_dim, rows), f32)]
             + [VMEM((block_len // 2, rows), f32)] * 2 + [VMEM((1, rows), f32)],
             compiler_params=pltpu.CompilerParams(vmem_limit_bytes=LIMIT),
             cost_estimate=pl.CostEstimate(flops=2 * pair_flops, bytes_accessed=6 << 20, transcendentals=0),
@@ -752,12 +788,13 @@
             functools.partial(attend_back, heads, tp_size, cp_size, width, scale),
             [lin_h, lin_h, lin_h, jax.ShapeDtypeStruct((2 * heads, head_dim), f32), jax.ShapeDtypeStruct((block_len, d_model), b16), lin_h],
             15,
-            [VMEM((cp_size, head_dim, block_len), b16), VMEM((cp_size, head_dim, rows), f32), VMEM((cp_size, 1, rows), f32), VMEM((cp_size, rows, head_dim), f32)]
-            + [pair_f, pair_f, f_lin, f_lin, head_f, head_f, head_f, VMEM((heads, block_len, head_dim), b16), VMEM(vec.shape, f32), tp_scratch, dma((6,))]
+            [f_lin, f_lin, VMEM((cp_size, head_dim, block_len), b16), VMEM((cp_size, head_dim, rows), f32), VMEM((cp_size, 1, rows), f32), VMEM((cp_size, rows, head_dim), f32)]
+            + [pair_f, pair_f, f_lin, f_lin, head_f, head_f, head_f, VMEM((heads, block_len, head_dim), b16), VMEM(vec.shape, f32), tp_scratch, dma((8,))]
             + [dma((cp_size, 2))] * 2 + [dma((heads,))] * 8 + [dma((tp_size,))] * 6,
             3,
             2,
-        )(q_all, k_all, v_all, o_all, do_all, lse, q_lin, k_lin, inv, *gains, cos_tab, sin_tab, gp_rows, o_rows)
+            2,
+        )(q_all, k_all, v_all, o_all, do_all, lse, inv, *gains, cos_tab, sin_tab, gp_rows, o_rows, q_lin, k_lin)
 
         def wgrad(left, right):
             return lax.dot_general(left, right, (((0,), (0,)), ((), ())), preferred_element_type=f32)

time: 541 us -> 531 us (0.982)
  Pallas kernels: 432 us -> 422 us
    pallas_call x1, Pallas kernels: 113 us -> 129 us  [local_run(): vmem_call(functools.partial(attend_back, heads, tp_size, cp_size, width,...]
    pallas_call x1, Pallas kernels: 67.4 us -> 53 us  [local_run(): vmem_call(functools.partial(scatter_qkv, heads, tp_size, cp_size, width),...]
    pallas_call x1, Pallas kernels: 159 us -> 149 us  [local_run(): pl.pallas_call(functools.partial(reduce_tail, tp_size, cp_size), out_shap...]
where the time goes in v5:
time: 531 us; the launch traced here: 523 us
  Pallas kernels  422 us (79%)
  matrix products  58.3 us (11%)
  local copies, waits for them, and re-layouts  33.7 us (6%)
  other arithmetic  7.37 us (1%)
    pallas_call x1, Pallas kernels, local_run(): pl.pallas_call(functools.partial(reduce_tail, tp_size, cp_size), out_shap...  149 us
    pallas_call x1, Pallas kernels, local_run(): vmem_call(functools.partial(attend_back, heads, tp_size, cp_size, width,...  129 us
    pallas_call x1, Pallas kernels, local_run(): vmem_call(functools.partial(scatter_qkv, heads, tp_size, cp_size, width),...  53 us
    pallas_call x1, Pallas kernels, local_run(): pl.pallas_call(functools.partial(attend, sub, scale), grid=(cp_size,), in...  44.6 us
    pallas_call x1, Pallas kernels, local_run(): vmem_call(functools.partial(rows_to_heads, heads, tp_size, cp_size), [jax...  25.2 us
    pallas_call x1, Pallas kernels, local_run(): vmem_call(functools.partial(heads_to_rows, heads, tp_size, cp_size), [jax...  21.5 us
    dot_general x4, matrix products, wgrad(): lax.dot_general(left, right, (((0,), (0,)), ((), ())), preferred_element_...  20.6 us
    reshape x3, local copies, waits for them, and re-layouts, local_run(): grad_w_v, grad_w_q, grad_w_k = (g.reshape(w_q.shape) for g in res[1:4])  15.7 us

profile of v5, /device:TPU:97, one launch (start us, length us, event | category | flops | bytes accessed | tf_op | source)
XLA Modules:
  0.0 522.6 jit_solution(7013998707865415384)
XLA Ops:
  0.7 3.1 fusion.47
  3.8 6.3 %fusion.42.v_in = bf16[1024,512]{1,0:T(8,128)(2,1)} fusion(bf16[256,8,4,128]{3,2,1,0:T(4,128)(2,1)} %bitcast.88, bf16[1,1024,2048]{2,1,0:T(8,128)(2,1)} %param.9), kind=kOutput, calls=%fused_computation.44 | convolution fusion | flops 2148007936 | bytes 7340032 | tf_op jit(solution)/shard_map/dot_general | solution.py:723
  10.1 2.4 multiply_reduce_fusion.2
  14.3 5.2 %multiply_reduce_fusion.1 = (f32[1024]{0:T(1024)S(1)}, f32[1024,512]{0,1:T(8,128)S(1)}) fusion(bf16[256,8,4,128]{3,2,1,0:T(4,128)(2,1)} %bitcast.97, bf16[1,1024,2048]{2,1,0:T(8,128)(2,1)} %param.9), kind=kOutput, calls=%fused_computation.36 | convolution fusion | flops 2148531200 | bytes 8392704 | tf_op jit(solution)/shard_map/dot_general | solution.py:722
  22.0 53.0 %shard_map.160 = (bf16[8,512,128]{2,1,0:T(8,128)(2,1)}, bf16[8,1024,128]{2,1,0:T(8,128)(2,1)}, bf16[8,1024,128]{2,1,0:T(8,128)(2,1)}, f32[16,128]{1,0:T(8,128)}, bf16[2048,2048]{1,0:T(8,128)(2,1)}) custom-call(f32[1024,512]{1,0:T(8,128)} %copy.18.q_lin.q_hbm, f32[1024,512]{1,0:T(8,128)} %copy.19.k_lin.k_hbm, f32[16,128]{1,0:T(8,128)} %reshape.98.vec, ...), custom_call_target="tpu_custom_call" | custom-call | tf_op jit(solution)/shard_map/pallas_call | solution.py:729
  75.0 44.6 %shard_map.161 = (bf16[8,512,128]{2,1,0:T(8,128)(2,1)}, f32[8,1,512]{2,1,0:T(1,128)}) custom-call(bf16[8,512,128]{2,1,0:T(8,128)(2,1)} %get-tuple-element.29.q_ref, bf16[8,1024,128]{2,1,0:T(8,128)(2,1)} %get-tuple-element.30.k_ref, bf16[8,1024,128]{2,1,0:T(8,128)(2,1)} %get-tuple-element.31.v_ref), custom_call_target="tpu_custom_call" | custom-call | flops 9663676416 | bytes 6291456 | tf_op jit(solution)/shard_map/pallas_call | solution.py:743
  119.6 21.5 %shard_map.162.or_in = bf16[256,2048]{1,0:T(8,128)(2,1)} custom-call(bf16[8,512,128]{2,1,0:T(8,128)(2,1)} %get-tuple-element.32.o_in.o_ref), custom_call_target="tpu_custom_call" | custom-call | tf_op jit(solution)/shard_map/pallas_call | solution.py:756
  141.1 6.3 %multiply_reduce_fusion = (f32[256]{0:T(256)S(1)}, f32[256,2048]{1,0:T(8,128)S(1)}) fusion(bf16[256,2048]{1,0:T(8,128)(2,1)} %shard_map.162.or_in, bf16[2048,2048]{1,0:T(8,128)(2,1)} %get-tuple-element.33), kind=kOutput, calls=%fused_computation.35 | convolution fusion | flops 2148531968 | bytes 11535360 | tf_op jit(solution)/shard_map/dot_general | solution.py:767
  147.4 3.1 fusion.26
  151.6 7.1 %convolution_convert_fusion.g_in = bf16[256,2048]{1,0:T(8,128)(2,1)} fusion(bf16[256,2048]{1,0:T(8,128)(2,1)S(1)} %fusion.25.gp_in, bf16[2048,2048]{1,0:T(8,128)(2,1)} %get-tuple-element.33), kind=kOutput, calls=%fused_computation.18 | convolution fusion | flops 2148007936 | bytes 10485760 | tf_op jit(solution)/shard_map/dot_general | solution.py:774
  158.7 25.2 %shard_map.163.do_ref = bf16[8,512,128]{2,1,0:T(8,128)(2,1)} custom-call(bf16[256,2048]{1,0:T(8,128)(2,1)} %convolution_convert_fusion.g_in), custom_call_target="tpu_custom_call" | custom-call | tf_op jit(solution)/shard_map/pallas_call | solution.py:776
  183.9 128.7 %shard_map.164 = (bf16[1024,512]{1,0:T(8,128)(2,1)}, bf16[1024,512]{1,0:T(8,128)(2,1)}, bf16[1024,512]{1,0:T(8,128)(2,1)}, f32[8,128]{1,0:T(8,128)}, bf16[1024,2...) custom-call(bf16[8,512,128]{2,1,0:T(8,128)(2,1)} %get-tuple-element.29.q_ref, bf16[8,1024,128]{2,1,0:T(8,128)(2,1)} %get-tuple-element.30.k_ref, ...), custom_call_target="tpu_custom_call" | custom-call | tf_op jit(solution)/shard_map/pallas_call | solution.py:787
  312.6 7.0 %fusion.52.refs_0_ = f32[512,2048]{1,0:T(8,128)} fusion(bf16[1024,512]{1,0:T(8,128)(2,1)} %get-tuple-element.36, bf16[1024,2048]{1,0:T(8,128)(2,1)} %get-tuple-element.37), kind=kOutput, calls=%fused_computation.61 | convolution fusion | flops 2147483648 | bytes 9437184 | tf_op jit(solution)/shard_map/dot_general | solution.py:800
  320.2 4.5 fusion.12.refs_1_
  324.7 4.5 fusion.15.refs_2_
  329.2 4.7 fusion.18.refs_3_
  333.8 2.4 fusion.29
  336.2 2.4 fusion.32
  338.6 5.6 %add_add_fusion.refs_4_ = f32[1024,2048]{1,0:T(8,128)} fusion(f32[1024,2048]{1,0:T(8,128)S(1)} %fusion.32, f32[1024,2048]{1,0:T(8,128)S(1)} %fusion.29, bf16[1024,512]{1,0:T(8,128)(2,1)S(1)} %copy-done.5, bf16[256,8,4,128]{3,2,1,0:T(4,128)(2,1)S(1)} %bitcast.89), kind=kOutput, calls=%fused_computation | convolution fusion | flops 2151677952 | bytes 28311552 | tf_op jit(solution)/shard_map/dot_general | solution.py:803
  344.2 149.3 %shard_map.165 = (f32[512,2048]{1,0:T(8,128)}, f32[2048,512]{1,0:T(8,128)}, f32[2048,512]{1,0:T(8,128)}, f32[2048,512]{1,0:T(8,128)}, bf16[1024,2048]{1,0:T(8,12...) custom-call(f32[512,2048]{1,0:T(8,128)} %fusion.52.refs_0_, f32[2048,512]{1,0:T(8,128)} %fusion.12.refs_1_, ...), custom_call_target="tpu_custom_call" | custom-call | tf_op jit(solution)/shard_map/pallas_call | solution.py:814
  496.1 5.2 reshape.104
  501.3 5.2 reshape.105
  506.6 5.2 reshape.106
  511.8 4.9 copy.64
  (44 shorter events, 14.3 us)
Async XLA Ops:
  3.7 6.3 %copy-start.6 = (bf16[1,1024,2048]{2,1,0:T(8,128)(2,1)S(1)}, bf16[1,1024,2048]{2,1,0:T(8,128)(2,1)}, u32[]{:S(2)}) copy-start(bf16[1,1024,2048]{2,1,0:T(8,128)(2,1)} %param.9) | copy-start | bytes 12582916
  3.8 6.3 %copy-start.11 = (bf16[2048,4,128]{2,1,0:T(4,128)(2,1)S(1)}, bf16[2048,4,128]{2,1,0:T(4,128)(2,1)}, u32[]{:S(2)}) copy-start(bf16[2048,4,128]{2,1,0:T(4,128)(2,1)} %param.10) | copy-start | bytes 6291460
  141.1 6.3 %copy-start.7 = (bf16[1,1024,2048]{2,1,0:T(8,128)(2,1)S(1)}, bf16[1,1024,2048]{2,1,0:T(8,128)(2,1)}, u32[]{:S(2)}) copy-start(bf16[1,1024,2048]{2,1,0:T(8,128)(2,1)} %param.9) | copy-start | bytes 12582916
  141.1 6.3 %copy-start.8 = (f32[2048]{0:T(1024)S(1)}, f32[2048]{0:T(1024)}, u32[]{:S(2)}) copy-start(f32[2048]{0:T(1024)} %param.16) | copy-start | bytes 24580
  150.6 1.0 copy-start
  151.6 7.1 %copy-start.3 = (bf16[256,2048]{1,0:T(8,128)(2,1)}, bf16[256,2048]{1,0:T(8,128)(2,1)S(1)}, u32[]{:S(2)}) copy-start(bf16[256,2048]{1,0:T(8,128)(2,1)S(1)} %fusion.25.gp_in) | copy-start | bytes 3145732
  312.6 7.0 %copy-start.9 = (f32[8,128]{1,0:T(8,128)S(1)}, f32[8,128]{1,0:T(8,128)}, u32[]{:S(2)}) copy-start(f32[8,128]{1,0:T(8,128)} %get-tuple-element.41) | copy-start | bytes 12292
  312.6 7.6 %copy-start.5 = (bf16[1024,512]{1,0:T(8,128)(2,1)S(1)}, bf16[1024,512]{1,0:T(8,128)(2,1)}, u32[]{:S(2)}) copy-start(bf16[1024,512]{1,0:T(8,128)(2,1)} %get-tuple-element.38) | copy-start | bytes 3145732
  320.2 4.5 copy-start.13
  324.7 4.5 copy-start.14
  329.2 4.7 copy-start.10
  333.8 2.4 copy-start.12
  336.2 2.4 copy-start.4
  511.8 4.9 copy-start.2
  516.7 3.7 copy-start.1

commit v6 on v5

--- a/solution.py
+++ b/solution.py
@@ -11,10 +11,11 @@
 ROPE_THETA = 500000.0
 NORM_EPS = 1e-6
 LOG2E = 1.4426950408889634
-LIMIT = 56 << 20
+LIMIT = 61 << 20
 LANES = 128
 FAR_A, FAR_B, NEAR_L, NEAR_R, SUM_L, SUM_R, OUT_L, OUT_R, RELAY_L, RELAY_R = range(10)
-PARTS = tuple(zip((RELAY_L, RELAY_R), range(2)))
+BOTH = range(2)
+PARTS = tuple(zip((RELAY_L, RELAY_R), BOTH))
 VMEM = pltpu.VMEM
 MESH = pl.DeviceIdType.MESH
 NT = (((1,), (1,)), ((), ()))
@@ -141,7 +142,7 @@
     own = [pltpu.make_async_copy(cols(k16, chip), k_out.at[me], loc.at[0]), pltpu.make_async_copy(cols(v_in, chip), v_out.at[me], loc.at[1])]
     for r in range(cp_size):
         dst = lax.rem(me + r, cp_size)
-        for s in range(2):
+        for s in BOTH:
             src = cols(q16, dst // 2, sub_rows(lax.rem(dst, 2), s, sub))
             place = q_out.at[me, s * sub : (s + 1) * sub, :]
             if r == 0:
@@ -188,7 +189,7 @@
     for copy in sends:
         copy.wait_send()
     for r in range(1, cp_size):
-        for s in range(2):
+        for s in BOTH:
             place = q_out.at[lax.rem(me - r + cp_size, cp_size), s * sub : (s + 1) * sub, :]
             remote(place, place, qs.at[r, s], qr.at[r, s], partner).wait_recv()
     for copy in forwards:
@@ -228,7 +229,7 @@
         alpha = jnp.exp2((m_old - m_new) * coef)
         lsum = jnp.zeros((8, cols), jnp.float32)
         new_mx = None
-        for c in range(2):
+        for c in BOTH:
             rows = slice(c * chunk, (c + 1) * chunk)
             if nxt is not None:
                 nbuf, nb, nh, masked = nxt
@@ -246,7 +247,7 @@
         m_scr[...] = m_new
         return None if nxt is None else jnp.max(new_mx, axis=0, keepdims=True)
 
-    for c in range(2):
+    for c in BOTH:
         s_a[c * chunk : (c + 1) * chunk, :] = scores(0, 0, c)
     mx_a[...] = jnp.max(s_a[...], axis=0, keepdims=True)
 
@@ -256,7 +257,7 @@
         return carry
 
     lax.fori_loop(0, blk, body, 0)
-    for c in range(2):
+    for c in BOTH:
         rows = slice(c * chunk, (c + 1) * chunk)
         s_a[rows, :] = mask(s_a[rows, :], 0, c)
     mx_b = step(s_a, jnp.max(s_a[...], axis=0, keepdims=True), blk, 0, (s_b, blk, 1, True))
@@ -273,12 +274,12 @@
     sub = o_out.shape[0]
     place = cols(o_out, head)
     group_barrier(me_tp, me_cp, tp_size, cp_size)
-    for finish in range(2):
+    for finish in BOTH:
         if finish:
             for h in range(heads * tp_size):
                 part = o_out.at[:, h * LANES : (h + 1) * LANES]
                 pltpu.make_async_copy(part, part, rs.at[h]).wait()
-        for s in range(2):
+        for s in BOTH:
             dst_tp = core if s == 0 else 3 - core
             for r in range(cp_size):
                 dst_cp = lax.rem(me_cp + r, cp_size)
@@ -302,10 +303,10 @@
     slot = me_tp // 2
     place = g_out.at[me_cp, pl.ds(pl.multiple_of(slot * sub, sub), sub), :]
     group_barrier(me_tp, me_cp, tp_size, cp_size)
-    for finish in range(2):
+    for finish in BOTH:
         if finish:
             for i in range(cp_size):
-                for s in range(2):
+                for s in BOTH:
                     part = g_out.at[i, s * sub : (s + 1) * sub, :]
                     pltpu.make_async_copy(part, part, rs.at[i, s]).wait()
         for rt in range(tp_size):
@@ -402,6 +403,28 @@
         sk[s] = (acc_k[s, core] + pk[s]) * scale
         sv[s] = (acc_v[s, core] + pv[s]).astype(sv.dtype)
 
+    last = heads - 1
+
+    def dq_copies(r):
+        dst = lax.rem(me + r, cp_size)
+        copies = []
+        for s in BOTH:
+            src = dqs.at[dst, s * sub : (s + 1) * sub, :]
+            place = cols(dq, chip, sub_rows(core, s, sub))
+            copies.append(remote(src, place, qs.at[r, s], qr.at[r, s], {"cp": dst}) if r else pltpu.make_async_copy(src, place, loc.at[s]))
+        return copies
+
+    def send_dq(early):
+        for r in range(cp_size):
+            dst = lax.rem(me + r, cp_size)
+            ready = dst // 2 < chip
+
+            @pl.when(ready if early else jnp.logical_not(ready))
+            def _():
+                dqs[dst] = dqt_scr[dst].T * scale
+                for copy in dq_copies(r):
+                    copy.start()
+
     def key_pair(s, carry):
         def key_block(e, inner):
             b = lax.rem(chip + 1 + s, heads) * 2 + e
@@ -411,7 +434,19 @@
                 tile(i, b, s, e, False)
                 return last
 
-            return lax.fori_loop(b + 1, cp_size, full, inner)
+            lax.fori_loop(b + 1, cp_size, full, inner)
+
+            @pl.when(jnp.logical_and(e < 1, s > 0))
+            def _():
+                add_pair(s - 1)
+                for copy in home_copies(s - 1):
+                    copy.start()
+
+            return inner
+
+        @pl.when(s == last)
+        def _():
+            send_dq(True)
 
         lax.fori_loop(0, 2, key_block, 0)
         for copy in pair_copies(s):
@@ -424,29 +459,13 @@
                 remote(whole, whole, gs.at[k], gr.at[k], partner).wait_recv()
                 relay(k, src, dst).start()
 
-        @pl.when(s > 0)
-        def _():
-            add_pair(s - 1)
-            for copy in home_copies(s - 1):
-                copy.start()
-
         return carry
 
     lax.fori_loop(0, heads, key_pair, 0)
-    for r in range(cp_size):
-        dst = lax.rem(me + r, cp_size)
-        dqs[dst] = dqt_scr[dst].T * scale
-        for s in range(2):
-            src = dqs.at[dst, s * sub : (s + 1) * sub, :]
-            place = cols(dq, chip, sub_rows(core, s, sub))
-            if r == 0:
-                copy = pltpu.make_async_copy(src, place, loc.at[s])
-                own.append(copy)
-            else:
-                copy = remote(src, place, qs.at[r, s], qr.at[r, s], {"cp": dst})
-                sends.append(copy)
-            copy.start()
-    last = heads - 1
+    send_dq(False)
+    own.extend(dq_copies(0))
+    for r in range(1, cp_size):
+        sends.extend(dq_copies(r))
     add_pair(last)
     for j, (src, out) in enumerate(((sk, dk), (sv, dv_out))):
         copy = pltpu.make_async_copy(src.at[last], cols(out, chip), loc.at[2 + j])
@@ -483,7 +502,7 @@
     first_pass(1, dk, k_lin, k_gain)
     for r in range(1, cp_size):
         src = lax.rem(me - r + cp_size, cp_size)
-        for s in range(2):
+        for s in BOTH:
             place = cols(dq, src // 2, sub_rows(lax.rem(src, 2), s, sub))
             remote(place, place, qs.at[r, s], qr.at[r, s], partner).wait_recv()
     first_pass(0, dq, q_lin, q_gain)
@@ -512,13 +531,14 @@
 
 def reduce_tail(tp_size, cp_size, *refs):
     n_w = 4
-    w_in, (dx_in, dy_in, small, y_in) = refs[:n_w], refs[n_w : 2 * n_w]
-    refs = refs[2 * n_w :]
+    (w_o_in, w_v_in), (dx_in, dy_in, small, y_in, x_in, dq_in, dk_in) = refs[:2], refs[2:9]
+    refs = refs[9:]
     w_out, (dx_out, y_out, small_out) = refs[:n_w], refs[n_w : n_w + 3]
     refs = refs[n_w + 3 :]
     acc, pair, far_a, far_b, fin_l, fin_r = (refs[i * n_w : (i + 1) * n_w] for i in range(6))
     refs = refs[6 * n_w :]
-    dxa, dxb, dx_own, dx_fa, dx_fb, dx_fl, dx_fr, dx16, got_small, got_post, ss, rs, ps, pr, fs, fr, loc, sms, smr, gps, gpr = refs
+    w_q_in, w_k_in, dxa, dxb, dx_own, dx_fa, dx_fb, dx_fl, dx_fr, dx16, got_small, got_post, ss, rs, ps, pr, fs, fr, loc, sms, smr, gps, gpr = refs
+    w_in = (w_o_in, w_v_in, w_q_in, w_k_in)
     me_tp = lax.axis_index("tp")
     me_cp = lax.axis_index("cp")
     core = lax.rem(me_cp, 2)
@@ -581,13 +601,17 @@
 
     give(y_in, y_i, rows_of(y_out, me_tp), tp_l, tp_r)
     order = (far, left, right, chip)
-    loads = []
-    for t in range(n_w):
+    loads = {}
+
+    def start_pair(t):
         for i, x in enumerate(order):
             go(piece(w_in[t], t, x, 1 - core), pair[t].at[x], ps.at[t, i], pr.at[t, i], partner)
             copy = pltpu.make_async_copy(piece(w_in[t], t, x, core), acc[t].at[x], loc.at[t, i])
             copy.start()
-            loads.append(copy)
+            loads[t, i] = copy
+
+    start_pair(0)
+    start_pair(1)
     dx_loads = [
         pltpu.make_async_copy(rows_of(dx_in, t_left, 0), dxa, loc.at[n_w, 0]),
         pltpu.make_async_copy(rows_of(dx_in, t_right, 1), dxb, loc.at[n_w, 1]),
@@ -598,13 +622,20 @@
 
     for t in range(n_w):
         for i, x in enumerate(order):
-            loads[t * 4 + i].wait()
+            loads[t, i].wait()
             landed(pair[t].at[x], ps.at[t, i], pr.at[t, i])
             acc[t][x] += pair[t][x]
         go(half_of(acc[t].at[far], 0), far_a[t], *ring_sems(t, FAR_A), to_l)
         go(half_of(acc[t].at[far], 1), far_b[t], *ring_sems(t, FAR_B), to_r)
         go(half_of(acc[t].at[left], 1), half_of(fin_r[t], 1), *ring_sems(t, NEAR_L), to_l)
         go(half_of(acc[t].at[right], 0), half_of(fin_l[t], 0), *ring_sems(t, NEAR_R), to_r)
+        if t < 2:
+            out, grad = ((w_q_in, dq_in), (w_k_in, dk_in))[t]
+            size = out.shape[0] // cp_size
+            for p in range(cp_size):
+                rows = slice(p * size, (p + 1) * size)
+                out[rows, :] = jnp.dot(x_in[:, rows].T, grad[...], preferred_element_type=jnp.float32)
+            start_pair(2 + t)
 
     got_small[me_cp] = small[...]
     for r in range(1, cp_size):
@@ -680,7 +711,7 @@
     for t in range(n_w):
         for i, x in enumerate((chip, right, left)):
             landed(piece(w_out[t], t, x, 1 - core), *pair_sems(t, i))
-        for part in range(2):
+        for part in BOTH:
             landed(piece(w_out[t], t, far, 1 - core, part), *pair_sems(t, 3 + part))
     for copy in outs:
         copy.wait()
@@ -799,9 +830,9 @@
         def wgrad(left, right):
             return lax.dot_general(left, right, (((0,), (0,)), ((), ())), preferred_element_type=f32)
 
-        grad_w_o, grad_w_v, grad_w_q, grad_w_k = wgrad(o_own, grad_proj), wgrad(x_loc, dv16), wgrad(x_loc, dq16), wgrad(x_loc, dk16)
+        grad_w_o, grad_w_v = wgrad(o_own, grad_proj), wgrad(x_loc, dv16)
         dx_part = sum(lax.dot_general(g, w, NT, preferred_element_type=f32) for g, w in ((dq16, w_q2), (dk16, w_k2), (dv16, w_v2)))
-        w_parts = [grad_w_o, grad_w_v, grad_w_q, grad_w_k]
+        w_parts = [grad_w_o, grad_w_v, grad_w_v, grad_w_v]
         small = jnp.concatenate([gain_grads, grad_post.reshape(-1, head_dim)], axis=0)
         any_spec = pl.BlockSpec(memory_space=pl.ANY)
         vmem_spec = pl.BlockSpec(memory_space=VMEM)
@@ -814,14 +845,14 @@
         res = pl.pallas_call(
             functools.partial(reduce_tail, tp_size, cp_size),
             out_shape=[jax.ShapeDtypeStruct(w.shape, f32) for w in w_parts] + [jax.ShapeDtypeStruct((block_len, d_model), b16)] * 2 + [jax.ShapeDtypeStruct(small.shape, f32)],
-            in_specs=[any_spec] * 5 + [vmem_spec] * 3,
+            in_specs=[any_spec] * 3 + [vmem_spec] * 6,
             out_specs=[any_spec] * 6 + [vmem_spec],
             scratch_shapes=bufs((ring,), cp_size) * 2 + bufs((), 2 * cp_size) * 2 + bufs((), cp_size) * 2
-            + [half_dx, half_dx, rows_dx, half_dx, half_dx, rows_dx, rows_dx, VMEM((sub, d_model), b16)]
+            + [VMEM(grad_w_v.shape, f32)] * 2 + [half_dx, half_dx, rows_dx, half_dx, half_dx, rows_dx, rows_dx, VMEM((sub, d_model), b16)]
             + [VMEM((cp_size,) + small.shape, f32), VMEM((tp_size, d_model // head_dim, head_dim), f32)]
             + [dma((6, 10))] * 2 + [dma((4, 4))] * 2 + [dma((4, 5))] * 2 + [dma((6, 5))] + [dma((cp_size,))] * 2 + [dma((tp_size,))] * 2,
             compiler_params=pltpu.CompilerParams(vmem_limit_bytes=LIMIT, collective_id=6, has_side_effects=True),
-        )(*w_parts, dx_part, dy_rows, small, y_rows)
+        )(grad_w_o, grad_w_v, dx_part, dy_rows, small, y_rows, x_loc, dq16, dk16)
         grad_w_v, grad_w_q, grad_w_k = (g.reshape(w_q.shape) for g in res[1:4])
         grad_x, y_out, small_sum = res[4:]
         return (y_out[None], grad_x[None], grad_w_q, grad_w_k, grad_w_v, res[0].reshape(w_o.shape), small_sum[:heads], small_sum[heads : 2 * heads], small_sum[2 * heads :].reshape(-1))

time: 531 us -> 516 us (0.972)
  matrix products: 58.3 us -> 49.2 us
  Pallas kernels: 422 us -> 416 us
    pallas_call x1, Pallas kernels: 129 us -> 105 us  [local_run(): vmem_call(functools.partial(attend_back, heads, tp_size, cp_size, width,...]
    pallas_call x1, Pallas kernels: 149 us -> 166 us  [local_run(): pl.pallas_call(functools.partial(reduce_tail, tp_size, cp_size), out_shap...]
    dot_general x4 -> x2, matrix products: 20.6 us -> 11.5 us  [wgrad(): lax.dot_general(left, right, (((0,), (0,)), ((), ())), preferred_element_...]
where the time goes in v6:
time: 516 us; the launch traced here: 508 us
  Pallas kernels  416 us (81%)
  matrix products  49.2 us (10%)
  local copies, waits for them, and re-layouts  33.7 us (7%)
  other arithmetic  7.69 us (1%)
    pallas_call x1, Pallas kernels, local_run(): pl.pallas_call(functools.partial(reduce_tail, tp_size, cp_size), out_shap...  166 us
    pallas_call x1, Pallas kernels, local_run(): vmem_call(functools.partial(attend_back, heads, tp_size, cp_size, width,...  105 us
    pallas_call x1, Pallas kernels, local_run(): vmem_call(functools.partial(scatter_qkv, heads, tp_size, cp_size, width),...  53 us
    pallas_call x1, Pallas kernels, local_run(): pl.pallas_call(functools.partial(attend, sub, scale), grid=(cp_size,), in...  45.3 us
    pallas_call x1, Pallas kernels, local_run(): vmem_call(functools.partial(rows_to_heads, heads, tp_size, cp_size), [jax...  25.3 us
    pallas_call x1, Pallas kernels, local_run(): vmem_call(functools.partial(heads_to_rows, heads, tp_size, cp_size), [jax...  21.4 us
    reshape x3, local copies, waits for them, and re-layouts, local_run(): grad_w_v, grad_w_q, grad_w_k = (g.reshape(w_q.shape) for g in res[1:4])  15.7 us
    dot_general x2, matrix products, wgrad(): lax.dot_general(left, right, (((0,), (0,)), ((), ())), preferred_element_...  11.5 us

profile of v6, /device:TPU:97, one launch (start us, length us, event | category | flops | bytes accessed | tf_op | source)
XLA Modules:
  0.0 507.6 jit_solution(3278076851404781160)
XLA Ops:
  0.7 3.1 fusion.27
  3.8 6.3 %fusion.24.v_in = bf16[1024,512]{1,0:T(8,128)(2,1)} fusion(bf16[256,8,4,128]{3,2,1,0:T(4,128)(2,1)} %bitcast.71, bf16[1,1024,2048]{2,1,0:T(8,128)(2,1)} %param.9), kind=kOutput, calls=%fused_computation.33 | convolution fusion | flops 2148007936 | bytes 7340032 | tf_op jit(solution)/shard_map/dot_general | solution.py:754
  10.1 2.4 multiply_reduce_fusion.2
  14.3 5.2 %multiply_reduce_fusion.1 = (f32[1024]{0:T(1024)S(1)}, f32[1024,512]{0,1:T(8,128)S(1)}) fusion(bf16[256,8,4,128]{3,2,1,0:T(4,128)(2,1)} %bitcast.82, bf16[1,1024,2048]{2,1,0:T(8,128)(2,1)} %param.9), kind=kOutput, calls=%fused_computation.25 | convolution fusion | flops 2148531200 | bytes 8392704 | tf_op jit(solution)/shard_map/dot_general | solution.py:753
  22.0 53.0 %shard_map.160 = (bf16[8,512,128]{2,1,0:T(8,128)(2,1)}, bf16[8,1024,128]{2,1,0:T(8,128)(2,1)}, bf16[8,1024,128]{2,1,0:T(8,128)(2,1)}, f32[16,128]{1,0:T(8,128)}, bf16[2048,2048]{1,0:T(8,128)(2,1)}) custom-call(f32[1024,512]{1,0:T(8,128)} %copy.18.q_lin.q_hbm, f32[1024,512]{1,0:T(8,128)} %copy.19.k_lin.k_hbm, f32[16,128]{1,0:T(8,128)} %reshape.98.vec, ...), custom_call_target="tpu_custom_call" | custom-call | tf_op jit(solution)/shard_map/pallas_call | solution.py:760
  75.0 45.3 %shard_map.161 = (bf16[8,512,128]{2,1,0:T(8,128)(2,1)}, f32[8,1,512]{2,1,0:T(1,128)}) custom-call(bf16[8,512,128]{2,1,0:T(8,128)(2,1)} %get-tuple-element.29.q_ref, bf16[8,1024,128]{2,1,0:T(8,128)(2,1)} %get-tuple-element.30.k_ref, bf16[8,1024,128]{2,1,0:T(8,128)(2,1)} %get-tuple-element.31.v_ref), custom_call_target="tpu_custom_call" | custom-call | flops 9663676416 | bytes 6291456 | tf_op jit(solution)/shard_map/pallas_call | solution.py:774
  120.3 21.4 %shard_map.162.or_in = bf16[256,2048]{1,0:T(8,128)(2,1)} custom-call(bf16[8,512,128]{2,1,0:T(8,128)(2,1)} %get-tuple-element.32.o_in.o_ref), custom_call_target="tpu_custom_call" | custom-call | tf_op jit(solution)/shard_map/pallas_call | solution.py:787
  141.8 6.1 %multiply_reduce_fusion = (f32[256]{0:T(256)S(1)}, f32[256,2048]{1,0:T(8,128)S(1)}) fusion(bf16[256,2048]{1,0:T(8,128)(2,1)} %shard_map.162.or_in, bf16[2048,2048]{1,0:T(8,128)(2,1)} %get-tuple-element.33), kind=kOutput, calls=%fused_computation.24 | convolution fusion | flops 2148531968 | bytes 11535360 | tf_op jit(solution)/shard_map/dot_general | solution.py:798
  147.9 3.4 fusion.5
  152.4 7.1 %convolution_convert_fusion.g_in = bf16[256,2048]{1,0:T(8,128)(2,1)} fusion(bf16[256,2048]{1,0:T(8,128)(2,1)S(1)} %fusion.4.gp_in, bf16[2048,2048]{1,0:T(8,128)(2,1)} %get-tuple-element.33), kind=kOutput, calls=%fused_computation.4 | convolution fusion | flops 2148007936 | bytes 10485760 | tf_op jit(solution)/shard_map/dot_general | solution.py:805
  159.5 25.3 %shard_map.163.do_ref = bf16[8,512,128]{2,1,0:T(8,128)(2,1)} custom-call(bf16[256,2048]{1,0:T(8,128)(2,1)} %convolution_convert_fusion.g_in), custom_call_target="tpu_custom_call" | custom-call | tf_op jit(solution)/shard_map/pallas_call | solution.py:807
  184.8 105.0 %shard_map.164 = (bf16[1024,512]{1,0:T(8,128)(2,1)}, bf16[1024,512]{1,0:T(8,128)(2,1)}, bf16[1024,512]{1,0:T(8,128)(2,1)}, f32[8,128]{1,0:T(8,128)}, bf16[1024,2...) custom-call(bf16[8,512,128]{2,1,0:T(8,128)(2,1)} %get-tuple-element.29.q_ref, bf16[8,1024,128]{2,1,0:T(8,128)(2,1)} %get-tuple-element.30.k_ref, ...), custom_call_target="tpu_custom_call" | custom-call | tf_op jit(solution)/shard_map/pallas_call | solution.py:818
  289.8 7.0 %fusion.36.refs_0_ = f32[512,2048]{1,0:T(8,128)} fusion(bf16[1024,512]{1,0:T(8,128)(2,1)} %get-tuple-element.36, bf16[1024,2048]{1,0:T(8,128)(2,1)} %get-tuple-element.37), kind=kOutput, calls=%fused_computation.54 | convolution fusion | flops 2147483648 | bytes 9437184 | tf_op jit(solution)/shard_map/dot_general | solution.py:831
  297.5 4.4 convolution_bitcast_fusion.refs_1_
  301.9 2.4 fusion.13
  304.4 2.4 fusion.9
  306.7 5.8 %add_add_fusion.refs_2_ = f32[1024,2048]{1,0:T(8,128)} fusion(f32[1024,2048]{1,0:T(8,128)S(1)} %fusion.13, f32[1024,2048]{1,0:T(8,128)S(1)} %fusion.9, bf16[1024,512]{1,0:T(8,128)(2,1)S(1)} %copy-done.7, bf16[256,8,4,128]{3,2,1,0:T(4,128)(2,1)S(1)} %bitcast.72), kind=kOutput, calls=%fused_computation | convolution fusion | flops 2151677952 | bytes 28311552 | tf_op jit(solution)/shard_map/dot_general | solution.py:834
  312.5 165.9 %shard_map.165 = (f32[512,2048]{1,0:T(8,128)}, f32[2048,512]{1,0:T(8,128)}, f32[2048,512]{1,0:T(8,128)}, f32[2048,512]{1,0:T(8,128)}, bf16[1024,2048]{1,0:T(8,12...) custom-call(f32[512,2048]{1,0:T(8,128)} %fusion.36.refs_0_, f32[2048,512]{1,0:T(8,128)} %convolution_bitcast_fusion.refs_1_, ...), custom_call_target="tpu_custom_call" | custom-call | tf_op jit(solution)/shard_map/pallas_call | solution.py:845
  481.1 5.2 %reshape.104 = f32[2048,4,128]{2,1,0:T(4,128)} reshape(f32[2048,512]{1,0:T(8,128)} %get-tuple-element.44) | data formatting | bytes 8388608 | tf_op jit(solution)/shard_map/reshape | solution.py:856
  486.3 5.2 %reshape.105 = f32[2048,4,128]{2,1,0:T(4,128)} reshape(f32[2048,512]{1,0:T(8,128)} %get-tuple-element.45) | data formatting | bytes 8388608 | tf_op jit(solution)/shard_map/reshape | solution.py:856
  491.5 5.2 %reshape.106 = f32[2048,4,128]{2,1,0:T(4,128)} reshape(f32[2048,512]{1,0:T(8,128)} %get-tuple-element.46) | data formatting | bytes 8388608 | tf_op jit(solution)/shard_map/reshape | solution.py:856
  496.7 4.9 copy.60
  501.7 2.1 copy.61
  505.4 2.0 copy.62
  (42 shorter events, 10.1 us)
Async XLA Ops:
  3.8 6.3 %copy-start.1 = (bf16[1,1024,2048]{2,1,0:T(8,128)(2,1)S(1)}, bf16[1,1024,2048]{2,1,0:T(8,128)(2,1)}, u32[]{:S(2)}) copy-start(bf16[1,1024,2048]{2,1,0:T(8,128)(2,1)} %param.9) | copy-start | bytes 12582916
  3.8 6.3 %copy-start.12 = (bf16[2048,4,128]{2,1,0:T(4,128)(2,1)S(1)}, bf16[2048,4,128]{2,1,0:T(4,128)(2,1)}, u32[]{:S(2)}) copy-start(bf16[2048,4,128]{2,1,0:T(4,128)(2,1)} %param.10) | copy-start | bytes 6291460
  141.7 6.2 %copy-start.10 = (f32[2048]{0:T(1024)S(1)}, f32[2048]{0:T(1024)}, u32[]{:S(2)}) copy-start(f32[2048]{0:T(1024)} %param.16) | copy-start | bytes 24580
  151.4 1.0 copy-start
  152.4 7.1 %copy-start.5 = (bf16[256,2048]{1,0:T(8,128)(2,1)}, bf16[256,2048]{1,0:T(8,128)(2,1)S(1)}, u32[]{:S(2)}) copy-start(bf16[256,2048]{1,0:T(8,128)(2,1)S(1)} %fusion.4.gp_in) | copy-start | bytes 3145732
  289.8 7.1 %copy-start.11 = (f32[8,128]{1,0:T(8,128)S(1)}, f32[8,128]{1,0:T(8,128)}, u32[]{:S(2)}) copy-start(f32[8,128]{1,0:T(8,128)} %get-tuple-element.41) | copy-start | bytes 12292
  289.8 7.7 %copy-start.2 = (bf16[1,1024,2048]{2,1,0:T(8,128)(2,1)S(1)}, bf16[1,1024,2048]{2,1,0:T(8,128)(2,1)}, u32[]{:S(2)}) copy-start(bf16[1,1024,2048]{2,1,0:T(8,128)(2,1)} %param.9) | copy-start | bytes 12582916
  289.8 7.7 %copy-start.7 = (bf16[1024,512]{1,0:T(8,128)(2,1)S(1)}, bf16[1024,512]{1,0:T(8,128)(2,1)}, u32[]{:S(2)}) copy-start(bf16[1024,512]{1,0:T(8,128)(2,1)} %get-tuple-element.38) | copy-start | bytes 3145732
  297.5 4.4 copy-start.8
  297.5 4.4 copy-start.13
  301.9 2.4 copy-start.9
  301.9 2.4 copy-start.14
  304.3 2.4 copy-start.6
  496.7 4.9 copy-start.4
  501.7 3.7 copy-start.3

commit v7 on v6

--- a/solution.py
+++ b/solution.py
@@ -12,6 +12,7 @@
 NORM_EPS = 1e-6
 LOG2E = 1.4426950408889634
 LIMIT = 61 << 20
+SMALL = 28 << 20
 LANES = 128
 FAR_A, FAR_B, NEAR_L, NEAR_R, SUM_L, SUM_R, OUT_L, OUT_R, RELAY_L, RELAY_R = range(10)
 BOTH = range(2)
@@ -38,7 +39,7 @@
         in_specs=[pl.BlockSpec(memory_space=VMEM)] * (n_in - n_any_in) + [pl.BlockSpec(memory_space=pl.ANY)] * n_any_in,
         out_specs=[pl.BlockSpec(memory_space=VMEM)] * n_out + [pl.BlockSpec(memory_space=pl.ANY)] * n_any,
         scratch_shapes=scratch,
-        compiler_params=pltpu.CompilerParams(vmem_limit_bytes=LIMIT, collective_id=collective_id, has_side_effects=True),
+        compiler_params=pltpu.CompilerParams(vmem_limit_bytes=LIMIT if collective_id == 3 else SMALL, collective_id=collective_id, has_side_effects=True),
     )
 
 
@@ -779,7 +780,7 @@
             out_shape=[jax.ShapeDtypeStruct((cp_size, rows, head_dim), b16), jax.ShapeDtypeStruct((cp_size, 1, rows), f32)],
             scratch_shapes=[VMEM((cp_size, block_len, head_dim), b16), VMEM((cp_size, head_dim, block_len), b16), VMEM((1, rows), f32), VMEM((1, rows), f32), VMEM((head_dim, rows), f32)]
             + [VMEM((block_len // 2, rows), f32)] * 2 + [VMEM((1, rows), f32)],
-            compiler_params=pltpu.CompilerParams(vmem_limit_bytes=LIMIT),
+            compiler_params=pltpu.CompilerParams(vmem_limit_bytes=SMALL),
             cost_estimate=pl.CostEstimate(flops=2 * pair_flops, bytes_accessed=6 << 20, transcendentals=0),
         )(q_all, k_all, v_all)
 

time: 516 us -> 506 us (0.981)
  Pallas kernels: 416 us -> 404 us
  local copies, waits for them, and re-layouts: 33.7 us -> 40.7 us
    unnamed x33 -> x65, local copies, waits for them, and re-layouts: 11.2 us -> 17.6 us
    pallas_call x1, Pallas kernels: 53 us -> 47.5 us  [local_run(): vmem_call(functools.partial(scatter_qkv, heads, tp_size, cp_size, width),...]
where the time goes in v7:
time: 506 us; the launch traced here: 498 us
  Pallas kernels  404 us (80%)
  matrix products  44.3 us (9%)
  local copies, waits for them, and re-layouts  40.7 us (8%)
  other arithmetic  7.6 us (2%)
    pallas_call x1, Pallas kernels, local_run(): pl.pallas_call(functools.partial(reduce_tail, tp_size, cp_size), out_shap...  166 us
    pallas_call x1, Pallas kernels, local_run(): vmem_call(functools.partial(attend_back, heads, tp_size, cp_size, width,...  105 us
    pallas_call x1, Pallas kernels, local_run(): vmem_call(functools.partial(scatter_qkv, heads, tp_size, cp_size, width),...  47.5 us
    pallas_call x1, Pallas kernels, local_run(): pl.pallas_call(functools.partial(attend, sub, scale), grid=(cp_size,), in...  43.5 us
    pallas_call x1, Pallas kernels, local_run(): vmem_call(functools.partial(rows_to_heads, heads, tp_size, cp_size), [jax...  22.8 us
    pallas_call x1, Pallas kernels, local_run(): vmem_call(functools.partial(heads_to_rows, heads, tp_size, cp_size), [jax...  19.4 us
    unnamed x65, local copies, waits for them, and re-layouts  17.6 us
    reshape x3, local copies, waits for them, and re-layouts, local_run(): grad_w_v, grad_w_q, grad_w_k = (g.reshape(w_q.shape) for g in res[1:4])  15.7 us

profile of v7, /device:TPU:97, one launch (start us, length us, event | category | flops | bytes accessed | tf_op | source)
XLA Modules:
  0.0 497.8 jit_solution(11193596903289476159)
XLA Ops:
  0.7 3.0 fusion.27
  3.7 6.4 %fusion.24.v_in = bf16[1024,512]{1,0:T(8,128)(2,1)} fusion(bf16[256,8,4,128]{3,2,1,0:T(4,128)(2,1)} %bitcast.75, bf16[1,1024,2048]{2,1,0:T(8,128)(2,1)} %param.9), kind=kOutput, calls=%fused_computation.33 | convolution fusion | flops 2148007936 | bytes 7340032 | tf_op jit(solution)/shard_map/dot_general | solution.py:755
  10.1 3.8 multiply_reduce_fusion.2
  15.8 7.3 %multiply_reduce_fusion.1 = (f32[1024]{0:T(1024)S(1)}, f32[1024,512]{0,1:T(8,128)}) fusion(bf16[256,8,4,128]{3,2,1,0:T(4,128)(2,1)} %bitcast.82, bf16[1,1024,2048]{2,1,0:T(8,128)(2,1)} %param.9), kind=kOutput, calls=%fused_computation.25 | convolution fusion | flops 2148531200 | bytes 8392704 | tf_op jit(solution)/shard_map/dot_general | solution.py:754
  23.1 2.9 copy.19.k_lin.k_hbm
  31.5 47.5 %shard_map.160 = (bf16[8,512,128]{2,1,0:T(8,128)(2,1)S(1)}, bf16[8,1024,128]{2,1,0:T(8,128)(2,1)S(1)}, bf16[8,1024,128]{2,1,0:T(8,128)(2,1)S(1)}, f32[16,128]{1,0:T(8,128)S(1)}, bf16[2048,2048]{1,0:T(8,128)(2,1)S(1)}) custom-call(f32[1024,512]{1,0:T(8,128)S(1)} %copy.18.q_lin.q_hbm, f32[1024,512]{1,0:T(8,128)S(1)} %copy-done.1, f32[16,128]{1,0:T(8,128)S(1)} %reshape.98.vec, ...), custom_call_target="tpu_custom_call" | custom-call | tf_op jit(solution)/shard_map/pallas_call | solution.py:761
  79.0 43.5 %shard_map.161 = (bf16[8,512,128]{2,1,0:T(8,128)(2,1)S(1)}, f32[8,1,512]{2,1,0:T(1,128)S(1)}) custom-call(bf16[8,512,128]{2,1,0:T(8,128)(2,1)S(1)} %get-tuple-element.29.q_ref, bf16[8,1024,128]{2,1,0:T(8,128)(2,1)S(1)} %get-tuple-element.30.k_ref, bf16[8,1024,128]{2,1,0:T(8,128)(2,1)S(1)} %get-tuple-element.31.v_ref), custom_call_target="tpu_custom_call" | custom-call | flops 9663676416 | bytes 6291456 | tf_op jit(solution)/shard_map/pallas_call | solution.py:775
  122.6 19.4 %shard_map.162.or_in = bf16[256,2048]{1,0:T(8,128)(2,1)S(1)} custom-call(bf16[8,512,128]{2,1,0:T(8,128)(2,1)S(1)} %get-tuple-element.32.o_in.o_ref), custom_call_target="tpu_custom_call" | custom-call | tf_op jit(solution)/shard_map/pallas_call | solution.py:788
  142.0 2.4 multiply_reduce_fusion
  144.5 3.5 fusion.5
  148.9 2.4 convolution_convert_fusion.g_in
  151.3 22.8 %shard_map.163.do_ref = bf16[8,512,128]{2,1,0:T(8,128)(2,1)S(1)} custom-call(bf16[256,2048]{1,0:T(8,128)(2,1)S(1)} %convolution_convert_fusion.g_in), custom_call_target="tpu_custom_call" | custom-call | tf_op jit(solution)/shard_map/pallas_call | solution.py:808
  175.1 104.8 %shard_map.164 = (bf16[1024,512]{1,0:T(8,128)(2,1)}, bf16[1024,512]{1,0:T(8,128)(2,1)}, bf16[1024,512]{1,0:T(8,128)(2,1)}, f32[8,128]{1,0:T(8,128)}, bf16[1024,2...) custom-call(bf16[8,512,128]{2,1,0:T(8,128)(2,1)} %copy-done.10, bf16[8,1024,128]{2,1,0:T(8,128)(2,1)} %copy-done.8, ...), custom_call_target="tpu_custom_call" | custom-call | tf_op jit(solution)/shard_map/pallas_call | solution.py:819
  279.9 7.0 %fusion.36.refs_0_ = f32[512,2048]{1,0:T(8,128)} fusion(bf16[1024,512]{1,0:T(8,128)(2,1)} %get-tuple-element.36, bf16[1024,2048]{1,0:T(8,128)(2,1)} %get-tuple-element.37), kind=kOutput, calls=%fused_computation.54 | convolution fusion | flops 2147483648 | bytes 9437184 | tf_op jit(solution)/shard_map/dot_general | solution.py:832
  287.6 4.4 convolution_bitcast_fusion.refs_1_
  292.0 2.4 fusion.13
  294.4 2.4 fusion.9
  296.8 5.8 %add_add_fusion.refs_2_ = f32[1024,2048]{1,0:T(8,128)} fusion(f32[1024,2048]{1,0:T(8,128)S(1)} %fusion.13, f32[1024,2048]{1,0:T(8,128)S(1)} %fusion.9, bf16[1024,512]{1,0:T(8,128)(2,1)S(1)} %copy-done.23, bf16[256,8,4,128]{3,2,1,0:T(4,128)(2,1)S(1)} %bitcast.76), kind=kOutput, calls=%fused_computation | convolution fusion | flops 2151677952 | bytes 28311552 | tf_op jit(solution)/shard_map/dot_general | solution.py:835
  302.7 166.0 %shard_map.165 = (f32[512,2048]{1,0:T(8,128)}, f32[2048,512]{1,0:T(8,128)}, f32[2048,512]{1,0:T(8,128)}, f32[2048,512]{1,0:T(8,128)}, bf16[1024,2048]{1,0:T(8,12...) custom-call(f32[512,2048]{1,0:T(8,128)} %fusion.36.refs_0_, f32[2048,512]{1,0:T(8,128)} %convolution_bitcast_fusion.refs_1_, ...), custom_call_target="tpu_custom_call" | custom-call | tf_op jit(solution)/shard_map/pallas_call | solution.py:846
  471.3 5.2 %reshape.104 = f32[2048,4,128]{2,1,0:T(4,128)} reshape(f32[2048,512]{1,0:T(8,128)} %get-tuple-element.44) | data formatting | bytes 8388608 | tf_op jit(solution)/shard_map/reshape | solution.py:857
  476.5 5.2 %reshape.105 = f32[2048,4,128]{2,1,0:T(4,128)} reshape(f32[2048,512]{1,0:T(8,128)} %get-tuple-element.45) | data formatting | bytes 8388608 | tf_op jit(solution)/shard_map/reshape | solution.py:857
  481.7 5.2 %reshape.106 = f32[2048,4,128]{2,1,0:T(4,128)} reshape(f32[2048,512]{1,0:T(8,128)} %get-tuple-element.46) | data formatting | bytes 8388608 | tf_op jit(solution)/shard_map/reshape | solution.py:857
  486.9 4.9 copy.60
  491.9 2.1 copy.61
  (74 shorter events, 16.3 us)
Async XLA Ops:
  3.6 22.4 %copy-start.2 = (f32[1024,128]{1,0:T(8,128)}, f32[1024,128]{1,0:T(8,128)S(1)}, u32[]{:S(2)}) copy-start(f32[1024,128]{1,0:T(8,128)S(1)} %get-tuple-element.55.sin_t) | copy-start | bytes 1572868
  3.6 6.4 %copy-start.17 = (bf16[1,1024,2048]{2,1,0:T(8,128)(2,1)S(1)}, bf16[1,1024,2048]{2,1,0:T(8,128)(2,1)}, u32[]{:S(2)}) copy-start(bf16[1,1024,2048]{2,1,0:T(8,128)(2,1)} %param.9) | copy-start | bytes 12582916
  3.6 6.4 %copy-start.28 = (bf16[2048,4,128]{2,1,0:T(4,128)(2,1)S(1)}, bf16[2048,4,128]{2,1,0:T(4,128)(2,1)}, u32[]{:S(2)}) copy-start(bf16[2048,4,128]{2,1,0:T(4,128)(2,1)} %param.10) | copy-start | bytes 6291460
  15.7 10.3 %copy-start = (f32[1024,512]{1,0:T(8,128)}, f32[1024,512]{1,0:T(8,128)S(1)}, u32[]{:S(2)}) copy-start(f32[1024,512]{1,0:T(8,128)S(1)} %copy.18.q_lin.q_hbm) | copy-start | bytes 6291460
  23.1 2.9 copy-start.14
  23.1 2.9 copy-start.15
  79.0 43.5 %copy-start.8 = (bf16[8,1024,128]{2,1,0:T(8,128)(2,1)}, bf16[8,1024,128]{2,1,0:T(8,128)(2,1)S(1)}, u32[]{:S(2)}) copy-start(bf16[8,1024,128]{2,1,0:T(8,128)(2,1)S(1)} %get-tuple-element.30.k_ref) | copy-start | bytes 6291460
  79.0 43.5 %copy-start.9 = (bf16[8,1024,128]{2,1,0:T(8,128)(2,1)}, bf16[8,1024,128]{2,1,0:T(8,128)(2,1)S(1)}, u32[]{:S(2)}) copy-start(bf16[8,1024,128]{2,1,0:T(8,128)(2,1)S(1)} %get-tuple-element.31.v_ref) | copy-start | bytes 6291460
  79.0 43.5 %copy-start.10 = (bf16[8,512,128]{2,1,0:T(8,128)(2,1)}, bf16[8,512,128]{2,1,0:T(8,128)(2,1)S(1)}, u32[]{:S(2)}) copy-start(bf16[8,512,128]{2,1,0:T(8,128)(2,1)S(1)} %get-tuple-element.29.q_ref) | copy-start | bytes 3145732
  79.0 43.5 %copy-start.13 = (f32[16,128]{1,0:T(8,128)}, f32[16,128]{1,0:T(8,128)S(1)}, u32[]{:S(2)}) copy-start(f32[16,128]{1,0:T(8,128)S(1)} %get-tuple-element.35.inv) | copy-start | bytes 24580
  122.5 21.9 %copy-start.4 = (bf16[8,512,128]{2,1,0:T(8,128)(2,1)}, bf16[8,512,128]{2,1,0:T(8,128)(2,1)S(1)}, u32[]{:S(2)}) copy-start(bf16[8,512,128]{2,1,0:T(8,128)(2,1)S(1)} %get-tuple-element.32.o_in.o_ref) | copy-start | bytes 3145732
  122.6 21.9 %copy-start.12 = (f32[8,1,512]{2,1,0:T(1,128)}, f32[8,1,512]{2,1,0:T(1,128)S(1)}, u32[]{:S(2)}) copy-start(f32[8,1,512]{2,1,0:T(1,128)S(1)} %get-tuple-element.34.lse_ref) | copy-start | bytes 49156
  142.0 2.5 copy-start.5
  142.0 2.5 copy-start.26
  279.9 7.1 %copy-start.27 = (f32[8,128]{1,0:T(8,128)S(1)}, f32[8,128]{1,0:T(8,128)}, u32[]{:S(2)}) copy-start(f32[8,128]{1,0:T(8,128)} %get-tuple-element.41) | copy-start | bytes 12292
  279.9 7.7 %copy-start.18 = (bf16[1,1024,2048]{2,1,0:T(8,128)(2,1)S(1)}, bf16[1,1024,2048]{2,1,0:T(8,128)(2,1)}, u32[]{:S(2)}) copy-start(bf16[1,1024,2048]{2,1,0:T(8,128)(2,1)} %param.9) | copy-start | bytes 12582916
  279.9 7.7 %copy-start.23 = (bf16[1024,512]{1,0:T(8,128)(2,1)S(1)}, bf16[1024,512]{1,0:T(8,128)(2,1)}, u32[]{:S(2)}) copy-start(bf16[1024,512]{1,0:T(8,128)(2,1)} %get-tuple-element.38) | copy-start | bytes 3145732
  287.6 4.4 copy-start.24
  287.6 4.4 copy-start.29
  292.0 2.4 copy-start.25
  292.0 2.4 copy-start.30
  294.4 2.4 copy-start.22
  486.9 4.9 copy-start.20
  491.9 3.7 copy-start.19
  (7 other events, 9.8 us)
